TPU v7x, 128 devices: a whole 4x4x4 slice. The times are simulated.
128 devices in a mesh: rows: 4 (over y_hi, core), cols: 32 (over y_lo, x, z).
Axes of the slice: x: 4, y: 4 (y_hi: 2, y_lo: 2; y = y_hi * 2 + y_lo), z: 4, core: 2. Of those that a mesh axis runs over, the one named last changes fastest.
Arguments:
- features: bfloat16 [131072, 2048], P(('rows', 'cols')), may hold values from -6 to 6
- w_in: bfloat16 [2048, 1024], replicated, may hold values from -0.125 to 0.125
- w_out: bfloat16 [1024, 256], replicated, may hold values from -0.1875 to 0.1875
- item_ids: int32 [131072], P(('rows', 'cols')), may hold values from 0 to 131071, as said below
- item_counts: int32 [131072], P(('rows', 'cols')), may hold values from 0 to 65535
- owners: int32 [131072, 1], P(('rows', 'cols')), may hold values from 0 to 127; in each aligned block of 1024 rows (0 to 1023, 1024 to 2047, ...) at most 16 rows name the same one
- queries: bfloat16 [8192, 256], P('rows'), may hold values from -60 to 60
- positives: int32 [8192], replicated, may hold values from 0 to 131071, as said below
Outputs:
- cache_emb: bfloat16 [262144, 256], P(('rows', 'cols'))
- cache_ids: int32 [262144], P(('rows', 'cols'))
- query_loss: float32 [8192], P('rows')
Inputs may be any that keep to these rules, and one draw needn't show every extreme that they name: `item_ids`: all ids are different. `owners`: the items of one device name each owner at most 16 times; some owner is named exactly 16 times by one device's items. `positives`: each is the id of some item.
All inputs are finite; a program needn't handle non-finite values.
Results may differ from a plain program's by a relative error of at most 0.0049.
Values may be sent and summed in bfloat16 or wider, within the bound.
No kernel may reach another device: no remote copies, remote signals or barrier semaphores. Data moves between devices by JAX's collectives and lax.ppermute only.
A program may use at most 128 MiB of HBM per device.

v0:
```python
import math

import jax
import jax.numpy as jnp
from jax import lax
from jax.sharding import Mesh
from jax.sharding import PartitionSpec as P

ROWS = ("rows_0", "rows_1")
COLS = ("cols_0", "cols_1", "cols_2")
ROWS_COLS = ("rows_0", "rows_1", "cols_0", "cols_1", "cols_2")


FLOOR = -1e30


def collected_together(value, axis):
    leaves = jax.tree.leaves(value)
    order = sorted(range(len(leaves)), key=lambda k: -leaves[k].size)
    width = (1, *leaves[order[0]].shape)[-1]
    lines = [
        jnp.pad(leaves[k].reshape(-1), (0, -leaves[k].size % width)).reshape(-1, width)
        for k in order
    ]
    both, at, found = (lax.all_gather(jnp.concatenate(lines), axis), 0, {})
    for k, line in zip(order, lines):
        slab = both[:, at : at + len(line)].reshape(len(both), -1)
        found[k] = slab[:, : leaves[k].size].reshape(-1, *leaves[k].shape)
        at += len(line)
    numbers = iter(range(len(leaves)))
    return jax.tree.map(lambda _: found[next(numbers)], value)


def combined_by_axis(value, axes, combine):
    for axis in axes:
        pieces = collected_together(value, axis)
        value = jax.tree.map(lambda part: part[0], pieces)
        for k in range(1, lax.axis_size(axis)):
            value = combine(value, jax.tree.map(lambda part: part[k], pieces))
    return value


def combine(left_part, right_part):
    highest = jnp.maximum(left_part[0], right_part[0])
    summed = left_part[1] * jnp.exp(left_part[0] - highest) + right_part[1] * jnp.exp(
        right_part[0] - highest
    )
    return (highest, summed, left_part[2] + right_part[2])


def block_stats(q_rows, pos_rows, key_rows, key_ids, key_counts):
    score_scale = 4.0 / math.sqrt(key_rows.shape[1])
    log_q = jnp.log1p(key_counts.astype(jnp.float32))
    live_slot = key_ids >= 0
    raw_scores = (
        jnp.einsum("qe,ke->qk", q_rows, key_rows, preferred_element_type=jnp.float32) * score_scale
        - log_q[None, :]
    )
    masked = jnp.where(live_slot[None, :], raw_scores, FLOOR)
    highest = jnp.max(masked, axis=1)
    summed = jnp.sum(jnp.where(live_slot[None, :], jnp.exp(masked - highest[:, None]), 0.0), axis=1)
    positive_hit = jnp.sum(
        jnp.where(key_ids[None, :] == pos_rows[:, None], raw_scores, 0.0), axis=1
    )
    return (highest, summed, positive_hit)


def query_stats(q_all, pos_all, key_rows, key_ids, key_counts):
    query_count = q_all.shape[0]
    block_rows = min(query_count, 512)

    def score_block(inputs):
        return block_stats(inputs[0], inputs[1], key_rows, key_ids, key_counts)

    highest, summed, positive_hit = lax.map(
        score_block,
        (
            q_all.reshape(query_count // block_rows, block_rows, q_all.shape[1]),
            pos_all.reshape(query_count // block_rows, block_rows),
        ),
    )
    return (
        highest.reshape(query_count),
        summed.reshape(query_count),
        positive_hit.reshape(query_count),
    )


def local(features, w_in, w_out, item_ids, item_counts, owners, queries, positives):
    hidden = jnp.maximum(jnp.dot(features, w_in, preferred_element_type=jnp.float32), 0.0).astype(
        jnp.bfloat16
    )
    embedded = jnp.dot(hidden, w_out, preferred_element_type=jnp.float32).astype(jnp.bfloat16)
    n_rows = lax.axis_size(ROWS)
    n_cols = lax.axis_size(COLS)
    devices = n_rows * n_cols
    items_dev = features.shape[0]
    capacity = 2 * items_dev // devices
    slot_count = devices * capacity
    owner_index = owners[:, 0]
    onehot = (owner_index[:, None] == jnp.arange(devices, dtype=jnp.int32)[None, :]).astype(
        jnp.int32
    )
    rank_within = jnp.sum((jnp.cumsum(onehot, axis=0) - onehot) * onehot, axis=1)
    slot_index = owner_index * capacity + rank_within
    send_emb = jnp.zeros((slot_count, embedded.shape[1]), jnp.bfloat16).at[slot_index].set(embedded)
    send_ids = jnp.full((slot_count,), -1, jnp.int32).at[slot_index].set(item_ids)
    send_counts = jnp.zeros((slot_count,), jnp.int32).at[slot_index].set(item_counts)
    pool_emb, pool_ids, pool_counts = (
        lax.all_to_all(send_emb, ROWS_COLS, split_axis=0, concat_axis=0, tiled=True),
        lax.all_to_all(send_ids, ROWS_COLS, split_axis=0, concat_axis=0, tiled=True),
        lax.all_to_all(send_counts, ROWS_COLS, split_axis=0, concat_axis=0, tiled=True),
    )
    q_dev = queries.shape[0]
    row_index = lax.axis_index(ROWS)
    offset = row_index * q_dev
    q_every = lax.all_gather(queries, ROWS, axis=0, tiled=True)
    own_partials = query_stats(q_every, positives, embedded, item_ids, item_counts)
    merged = combined_by_axis(own_partials, ROWS_COLS, combine)
    highest = lax.dynamic_slice_in_dim(merged[0], offset, q_dev)
    summed = lax.dynamic_slice_in_dim(merged[1], offset, q_dev)
    positive_hit = lax.dynamic_slice_in_dim(merged[2], offset, q_dev)
    query_loss = highest + jnp.log(summed) - positive_hit
    return (pool_emb, pool_ids, query_loss)


def solution(mesh):
    torus = Mesh(
        mesh.devices.reshape(2, 2, 2, 4, 4), ("rows_0", "rows_1", "cols_0", "cols_1", "cols_2")
    )
    placed = (
        P(ROWS_COLS, None),
        P(),
        P(),
        P(ROWS_COLS),
        P(ROWS_COLS),
        P(ROWS_COLS, None),
        P(ROWS, None),
        P(),
    )
    return jax.shard_map(
        local,
        mesh=torus,
        in_specs=placed,
        out_specs=(P(ROWS_COLS, None), P(ROWS_COLS), P(ROWS)),
        check_vma=False,
    )
```

profile of v0, /device:TPU:0, one launch (start us, length us, event | category | flops | bytes accessed | tf_op | source)
XLA Modules:
  0.0 163.1 jit_solution(8168572875715860221)
XLA Ops:
  9.5 4.3 %scatter_custom_fusion.1 = s32[2048]{0:T(1024)S(1)} fusion(s32[1024]{0:T(1024)S(1)} %bitcast.261, s32[1024]{0:T(1024)S(1)} %copy-done.1, s32[]{:T(128)} %constant.65.clone.1), kind=kCustom, calls=%fused_computation.109 | custom fusion | bytes 8196 | tf_op jit(solution)/shard_map/scatter | solution.py:107
  14.6 11.2 %all-to-all-start.1 = ((s32[128,16,1]{1,2,0:T(1,128)}), s32[128,16,1]{1,2,0:T(1,128)S(1)}, u32[]{:S(2)}, u32[]{:S(2)}) async-start(s32[128,16,1]{1,2,0:T(1,128)} %bitcast.15), calls=%async_computation.1 | async-start | bytes 131072 | tf_op jit(solution)/shard_map/all_to_all | solution.py:111
  25.8 8.6 %convolution_convert_fusion = bf16[1024,256]{1,0:T(8,128)(2,1)S(1)} fusion(bf16[1024,256]{1,0:T(8,128)(2,1)S(1)} %copy-done, bf16[1024,2048]{1,0:T(8,128)(2,1)} %param.10, bf16[2048,1024]{1,0:T(8,128)(2,1)} %param.11), kind=kOutput, calls=%fused_computation.12 | convolution fusion | flops 4834197504 | bytes 9437184 | tf_op jit(solution)/shard_map/dot_general | solution.py:93
  34.4 6.0 %scatter_custom_fusion = bf16[2048,256]{1,0:T(8,128)(2,1)} fusion(s32[1024]{0:T(1024)S(1)} %bitcast.262, bf16[1024,256]{1,0:T(8,128)(2,1)S(1)} %convolution_convert_fusion, bf16[]{:T(256)} %constant.60.clone.1), kind=kCustom, calls=%fused_computation.20 | custom fusion | bytes 1048578 | tf_op jit(solution)/shard_map/scatter | solution.py:106
  40.4 9.8 %all-to-all-start = ((bf16[128,16,256]{2,1,0:T(8,128)(2,1)}), bf16[128,16,256]{2,1,0:T(8,128)(2,1)S(1)}, u32[]{:S(2)}, u32[]{:S(2)}) async-start(bf16[128,16,256]{2,1,0:T(8,128)(2,1)} %bitcast.13), calls=%async_computation | async-start | bytes 2097152 | tf_op jit(solution)/shard_map/all_to_all | solution.py:110
  52.3 16.9 %all-to-all-done = bf16[128,16,256]{2,1,0:T(8,128)(2,1)S(1)} async-done(((bf16[128,16,256]{2,1,0:T(8,128)(2,1)}), bf16[128,16,256]{2,1,0:T(8,128)(2,1)S(1)}, u32[]{:S(2)}, u32[]{:S(2)}) %all-to-all-start) | async-done | bytes 1048608 | tf_op jit(solution)/shard_map/all_to_all | solution.py:110
  69.2 41.3 %while.16 = (s32[]{:T(128)}, f32[16,512]{1,0:T(8,128)S(1)}, f32[16,512]{1,0:T(8,128)S(1)}, f32[16,512]{1,0:T(8,128)S(1)}, s32[1024]{0:T(1024)S(1)}, /*index=5*/b...) while((s32[]{:T(128)}, f32[16,512]{1,0:T(8,128)S(1)}, ...), condition=%wide.region_9.10_spmd, body=%wide.region_5.9_spmd.sunk | while | flops 274202112 | bytes 5023357 | solution.py:75
  69.2 1.5 select_reduce_fusion.5
  70.8 0.8 select_reduce_fusion.6
  71.8 1.5 select_reduce_fusion.5
  74.4 1.5 select_reduce_fusion.5
  77.0 1.5 select_reduce_fusion.5
  79.6 1.5 select_reduce_fusion.5
  81.1 0.8 select_reduce_fusion.6
  82.1 1.5 select_reduce_fusion.5
  84.7 1.5 select_reduce_fusion.5
  87.3 1.5 select_reduce_fusion.5
  89.9 1.5 select_reduce_fusion.5
  92.5 1.5 select_reduce_fusion.5
  95.0 1.5 select_reduce_fusion.5
  97.6 1.5 select_reduce_fusion.5
  100.2 1.5 select_reduce_fusion.5
  102.8 1.5 select_reduce_fusion.5
  104.3 0.8 select_reduce_fusion.6
  105.4 1.5 select_reduce_fusion.5
  108.0 1.5 select_reduce_fusion.5
  110.7 7.1 %all-gather.5 = f32[2,3,8192]{2,1,0:T(4,128)S(1)} all-gather(f32[1,3,8192]{2,1,0:T(4,128)S(1)} %maximum_bitcast_fusion), channel_id=2, replica_groups=mesh['rows_0'=2,'rows_1'=2,'cols_0'=2,'cols_1'=4,'cols_2'=4] {'rows_0'}, dimensions={0}, use_global_device_ids=true | all-gather | bytes 294912 | tf_op jit(solution)/shard_map/all_gather | solution.py:25
  118.2 2.0 %all-gather.6 = f32[2,3,8192]{2,1,0:T(4,128)S(1)} all-gather(f32[1,3,8192]{2,1,0:T(4,128)S(1)} %maximum_bitcast_fusion.1), channel_id=3, replica_groups=mesh['rows_0'=2,'rows_1'=2,'cols_0'=2,'cols_1'=4,'cols_2'=4] {'rows_1'}, dimensions={0}, use_global_device_ids=true | all-gather | bytes 294912 | tf_op jit(solution)/shard_map/all_gather | solution.py:25
  120.5 6.2 %all-gather.7 = f32[2,3,8192]{2,1,0:T(4,128)S(1)} all-gather(f32[1,3,8192]{2,1,0:T(4,128)S(1)} %maximum_bitcast_fusion.2), channel_id=4, replica_groups=mesh['rows_0'=2,'rows_1'=2,'cols_0'=2,'cols_1'=4,'cols_2'=4] {'cols_0'}, dimensions={0}, use_global_device_ids=true | all-gather | bytes 294912 | tf_op jit(solution)/shard_map/all_gather | solution.py:25
  127.0 13.4 %all-gather.8 = f32[4,3,8192]{2,1,0:T(4,128)S(1)} all-gather(f32[1,3,8192]{2,1,0:T(4,128)S(1)} %maximum_bitcast_fusion.3), channel_id=5, replica_groups=mesh['rows_0'=2,'rows_1'=2,'cols_0'=2,'cols_1'=4,'cols_2'=4] {'cols_1'}, dimensions={0}, use_global_device_ids=true | all-gather | bytes 491520 | tf_op jit(solution)/shard_map/all_gather | solution.py:25
  140.9 13.3 %all-gather.9 = f32[4,3,8192]{2,1,0:T(4,128)S(1)} all-gather(f32[1,3,8192]{2,1,0:T(4,128)S(1)} %maximum_bitcast_fusion.4), channel_id=6, replica_groups=mesh['rows_0'=2,'rows_1'=2,'cols_0'=2,'cols_1'=4,'cols_2'=4] {'cols_2'}, dimensions={0}, use_global_device_ids=true | all-gather | bytes 491520 | tf_op jit(solution)/shard_map/all_gather | solution.py:25
  155.3 1.0 copy.36
  (146 shorter events, 21.3 us)
Async XLA Ops:
  7.2 18.6 %copy-start = (bf16[1024,256]{1,0:T(8,128)(2,1)S(1)}, bf16[1024,256]{1,0:T(8,128)(2,1)}, u32[]{:S(2)}) copy-start(bf16[1024,256]{1,0:T(8,128)(2,1)} %param.12) | copy-start | bytes 1572868
  7.2 2.0 %copy-start.2 = (s32[1024,1]{0,1:T(1,128)S(1)}, s32[1024,1]{0,1:T(1,128)}, u32[]{:S(2)}) copy-start(s32[1024,1]{0,1:T(1,128)} %param.15) | copy-start | bytes 12292
  7.2 2.3 %copy-start.1 = (s32[1024]{0:T(1024)S(1)}, s32[1024]{0:T(1024)}, u32[]{:S(2)}) copy-start(s32[1024]{0:T(1024)} %param.13) | copy-start | bytes 12292
  7.2 62.0 %all-gather.12.cloned.1.call-start = ((), (), s32[]{:S(2)}) async-start(), calls=%async_computation.2 | async-start | bytes 5242880 | tf_op jit(solution)/shard_map/all_gather | solution.py:117
  14.6 25.9 %all-to-all-start.1 = ((s32[128,16,1]{1,2,0:T(1,128)}), s32[128,16,1]{1,2,0:T(1,128)S(1)}, u32[]{:S(2)}, u32[]{:S(2)}) async-start(s32[128,16,1]{1,2,0:T(1,128)} %bitcast.15), calls=%async_computation.1 | async-start | bytes 131072 | tf_op jit(solution)/shard_map/all_to_all | solution.py:111
  34.4 15.8 %copy-start.3 = (s32[8192]{0:T(1024)S(1)}, s32[8192]{0:T(1024)}, u32[]{:S(2)}) copy-start(s32[8192]{0:T(1024)} %param.17) | copy-start | bytes 98308
  34.4 15.9 %copy-start.4 = (s32[1024]{0:T(1024)S(1)}, s32[1024]{0:T(1024)}, u32[]{:S(2)}) copy-start(s32[1024]{0:T(1024)} %param.14) | copy-start | bytes 12292
  40.4 28.8 %all-to-all-start = ((bf16[128,16,256]{2,1,0:T(8,128)(2,1)}), bf16[128,16,256]{2,1,0:T(8,128)(2,1)S(1)}, u32[]{:S(2)}, u32[]{:S(2)}) async-start(bf16[128,16,256]{2,1,0:T(8,128)(2,1)} %bitcast.13), calls=%async_computation | async-start | bytes 2097152 | tf_op jit(solution)/shard_map/all_to_all | solution.py:110
Sparse Core Ops, SparseCore 0:
  9.7 41.6 all-gather.11
where the time goes:
time: 164 us; the launch traced here: 163 us
  blocking collectives  42.1 us (26%)
  matrix products  32.9 us (20%)
  starting transfers between devices  21 us (13%)
  local copies, waits for them, and re-layouts  17.7 us (11%)
  waiting for transfers between devices  17.6 us (11%)
  other arithmetic  16.6 us (10%)
  between operations  14.4 us (9%)
    all_gather x5, blocking collectives, collected_together(): both, at, found = (lax.all_gather(jnp.concatenate(lines), axis), 0, {})  42.1 us
    dot_general x16, matrix products, block_stats(): jnp.einsum('qe,ke->qk', q_rows, key_rows, preferred_element_type=jnp.floa...  24.3 us
    all_to_all x1, waiting for transfers between devices, local(): lax.all_to_all(send_emb, ROWS_COLS, split_axis=0, concat_axis=0, tiled=True)  16.9 us
    reduce_sum x16, other arithmetic, block_stats(): jnp.sum(jnp.where(key_ids[None, :] == pos_rows[:, None], raw_scores, 0.0)...  12.9 us
    all_to_all x1, starting transfers between devices, local(): lax.all_to_all(send_ids, ROWS_COLS, split_axis=0, concat_axis=0, tiled=True)  11.2 us
    all_to_all x1, starting transfers between devices, local(): lax.all_to_all(send_emb, ROWS_COLS, split_axis=0, concat_axis=0, tiled=True)  9.75 us
    dot_general x1, matrix products, local(): jnp.dot(hidden, w_out, preferred_element_type=jnp.float32)  8.63 us
    scatter x1, local copies, waits for them, and re-layouts, local(): jnp.zeros((slot_count, embedded.shape[1]), jnp.bfloat16).at[slot_index]  6.01 us
  transfers between devices with their start and end apart: 3, of which 1 were waited for; matrix products, arithmetic and copies ran while one was open for 13% of the time, Pallas kernels for 0%

commit v1 on v0

v1 whole, which is shorter than its diff:
```python
import math

import jax
import jax.numpy as jnp
from jax import lax
from jax.experimental import pallas as pl
from jax.experimental.pallas import tpu as pltpu
from jax.sharding import Mesh
from jax.sharding import PartitionSpec as P

ROWS = ("rows_0", "rows_1")
COLS = ("cols_0", "cols_1", "cols_2")
ROWS_COLS = ("rows_0", "rows_1", "cols_0", "cols_1", "cols_2")

F32 = jnp.float32
BF16 = jnp.bfloat16
I32 = jnp.int32

N_DEV = 128
N_ROWS = 4
N_COLS = 32
ITEMS = 1024
CAP = 16
EMB = 256
HID = 1024
F_IN = 2048
QDEV = 2048
LANES = 128
BLOCKS = ITEMS // LANES

LOG2E = math.log2(math.e)
LN2 = math.log(2.0)
SCALE2 = 4.0 / math.sqrt(EMB) * LOG2E
FLOOR = -1e30

PACK_IDS = N_DEV
PACK_LOGQ = N_DEV + BLOCKS
PACK_ROWS = N_DEV + 2 * BLOCKS

PART_POS = QDEV // LANES
PART_IDS = 2 * PART_POS
PART_ROWS = PART_IDS + 8

NT = (((1,), (1,)), ((), ()))

ROW_BLOCK = 256


def tower_kernel(
    feat_hbm, w_in_hbm, w_out_hbm, owners_ref, ids_ref, counts_ref,
    emb_ref, send_ref, pack_ref,
    feat, w_in, w_out, slots, feat_sem, w_in_sem, w_out_sem,
):
    n_blocks = ITEMS // ROW_BLOCK
    copies = [
        pltpu.make_async_copy(
            feat_hbm.at[pl.ds(k * ROW_BLOCK, ROW_BLOCK)],
            feat.at[pl.ds(k * ROW_BLOCK, ROW_BLOCK)],
            feat_sem.at[k],
        )
        for k in range(n_blocks)
    ]
    w_in_copy = pltpu.make_async_copy(w_in_hbm, w_in, w_in_sem)
    w_out_copy = pltpu.make_async_copy(w_out_hbm, w_out, w_out_sem)
    copies[0].start()
    w_in_copy.start()
    w_out_copy.start()
    for k in range(1, n_blocks):
        copies[k].start()

    owner_iota = lax.broadcasted_iota(I32, (N_DEV, LANES), 0)
    upper = (
        lax.broadcasted_iota(I32, (LANES, LANES), 0) < lax.broadcasted_iota(I32, (LANES, LANES), 1)
    ).astype(F32).astype(BF16)
    slot_of_lane = lax.broadcasted_iota(I32, (LANES, LANES), 0) % CAP
    seen = jnp.zeros((N_DEV, 1), F32)
    parts = [jnp.zeros((N_DEV, LANES), F32) for _ in range(3)]
    for j in range(BLOCKS):
        owner = owners_ref[j : j + 1, :]
        onehot = (owner_iota == owner).astype(F32)
        onehot_b = onehot.astype(BF16)
        before = jnp.dot(onehot_b, upper, preferred_element_type=F32) + seen
        rank = jnp.sum(onehot * before, axis=0, keepdims=True).astype(I32)
        seen = seen + jnp.sum(onehot, axis=1, keepdims=True)
        slots[j : j + 1, :] = owner * CAP + rank
        value = ids_ref[j : j + 1, :] + 1
        here = slot_of_lane == rank
        for p, piece in enumerate((value >> 12, (value >> 6) & 63, value & 63)):
            chosen = jnp.where(here, piece.astype(F32), 0.0).astype(BF16)
            parts[p] = parts[p] + lax.dot_general(onehot_b, chosen, NT, preferred_element_type=F32)
    pack_ref[0:N_DEV, :] = parts[0] * 4096.0 + parts[1] * 64.0 + parts[2] - 1.0
    pack_ref[PACK_IDS : PACK_IDS + BLOCKS, :] = ids_ref[...].astype(F32)
    pack_ref[PACK_LOGQ : PACK_LOGQ + BLOCKS, :] = jnp.log(1.0 + counts_ref[...].astype(F32)) * LOG2E

    for k in range(n_blocks):
        copies[k].wait()
        if k == 0:
            w_in_copy.wait()
        rows = pl.ds(k * ROW_BLOCK, ROW_BLOCK)
        hidden = jnp.maximum(
            jnp.dot(feat[rows, :], w_in[...], preferred_element_type=F32), 0.0
        ).astype(BF16)
        if k == 0:
            w_out_copy.wait()
        emb_ref[rows, :] = jnp.dot(hidden, w_out[...], preferred_element_type=F32).astype(BF16)

    chunk = 512
    slot_row = jnp.concatenate([slots[j : j + 1, :] for j in range(BLOCKS)], axis=1)
    for c in range(N_DEV * CAP // chunk):
        place = lax.broadcasted_iota(I32, (chunk, ITEMS), 0) + c * chunk
        chosen = (place == slot_row).astype(F32).astype(BF16)
        send_ref[pl.ds(c * chunk, chunk), :] = jnp.dot(
            chosen, emb_ref[...], preferred_element_type=F32
        ).astype(BF16)


def tower(features, w_in, w_out, owners, ids, counts):
    any_spec = pl.BlockSpec(memory_space=pl.ANY)
    vmem_spec = pl.BlockSpec(memory_space=pltpu.VMEM)
    n_blocks = ITEMS // ROW_BLOCK
    return pl.pallas_call(
        tower_kernel,
        in_specs=[any_spec, any_spec, any_spec, vmem_spec, vmem_spec, vmem_spec],
        out_specs=[vmem_spec, vmem_spec, vmem_spec],
        out_shape=[
            jax.ShapeDtypeStruct((ITEMS, EMB), BF16),
            jax.ShapeDtypeStruct((N_DEV * CAP, EMB), BF16),
            jax.ShapeDtypeStruct((PACK_ROWS, LANES), F32),
        ],
        scratch_shapes=[
            pltpu.VMEM((ITEMS, F_IN), BF16),
            pltpu.VMEM((F_IN, HID), BF16),
            pltpu.VMEM((HID, EMB), BF16),
            pltpu.VMEM((BLOCKS, LANES), I32),
            pltpu.SemaphoreType.DMA((n_blocks,)),
            pltpu.SemaphoreType.DMA,
            pltpu.SemaphoreType.DMA,
        ],
        cost_estimate=pl.CostEstimate(
            flops=2 * ITEMS * F_IN * HID + 2 * ITEMS * HID * EMB,
            bytes_accessed=2 * (ITEMS * F_IN + F_IN * HID),
            transcendentals=0,
        ),
        name="tower",
    )(features, w_in, w_out, owners, ids, counts)


Q_TILE = 256
I_TILE = 512


def score_blocks(q_ref, pos_ref, embs, packs, col_ids, col_logq, state_in, state_out):
    for n, pack in enumerate(packs):
        for rows, col in ((PACK_IDS, col_ids), (PACK_LOGQ, col_logq)):
            turned = jnp.concatenate(
                [pack[pl.ds(rows, BLOCKS), :], jnp.zeros((LANES - BLOCKS, LANES), F32)], axis=0
            ).T
            for j in range(BLOCKS):
                col[pl.ds(n * ITEMS + j * LANES, LANES), :] = jnp.broadcast_to(
                    turned[:, j : j + 1], (LANES, LANES)
                )

    def query_tile(t, _):
        q_rows = q_ref[pl.ds(pl.multiple_of(t * Q_TILE, Q_TILE), Q_TILE), :]
        pos_rows = [
            pos_ref[pl.ds(t * (Q_TILE // LANES) + u, 1), :].astype(F32) for u in range(Q_TILE // LANES)
        ]
        pos_row = jnp.concatenate(pos_rows, axis=1)
        top, total, hit = [state_in(k, t) for k in range(3)]
        for n, emb in enumerate(embs):
            for c in range(ITEMS // I_TILE):
                raw = lax.dot_general(
                    emb[pl.ds(c * I_TILE, I_TILE), :], q_rows, NT, preferred_element_type=F32
                )
                at = pl.ds(n * ITEMS + c * I_TILE, I_TILE)
                logq = jnp.concatenate([col_logq[at, :]] * (Q_TILE // LANES), axis=1)
                ids = jnp.concatenate([col_ids[at, :]] * (Q_TILE // LANES), axis=1)
                logit = raw * SCALE2 - logq
                match = jnp.where(ids == pos_row, logit, 0.0)
                grouped = logit.reshape(I_TILE // 8, 8, Q_TILE)
                new_top = jnp.maximum(top, jnp.max(grouped, axis=0))
                total = total * jnp.exp2(top - new_top) + jnp.sum(
                    jnp.exp2(grouped - new_top[None]), axis=0
                )
                hit = hit + jnp.sum(match.reshape(I_TILE // 8, 8, Q_TILE), axis=0)
                top = new_top
        state_out(t, top, total, hit)
        return 0

    lax.fori_loop(0, QDEV // Q_TILE, query_tile, 0)


def near_kernel(
    where_ref, q_ref, pos_all, emb0, emb1, pack0, pack1, state_ref, col_ids, col_logq
):
    pos_ref = pos_all.at[pl.ds(where_ref[0] * (QDEV // LANES), QDEV // LANES)]

    def state_in(k, t):
        return jnp.full((8, Q_TILE), FLOOR if k == 0 else 0.0, F32)

    def state_out(t, *state):
        for k in range(3):
            state_ref[k, t] = state[k]

    score_blocks(q_ref, pos_ref, (emb0, emb1), (pack0, pack1), col_ids, col_logq, state_in, state_out)


def far_kernel(
    where_ref, q_ref, pos_all, emb0, emb1, pack0, pack1, near0, near1, before_ref,
    out_ref, parts, col_ids, col_logq,
):
    row = where_ref[0]
    col = where_ref[1]
    pos_ref = pos_all.at[pl.ds(row * (QDEV // LANES), QDEV // LANES)]

    def state_in(k, t):
        return before_ref[k, t]

    def state_out(t, top, total, hit):
        highest = jnp.max(top, axis=0, keepdims=True)
        summed = jnp.sum(total * jnp.exp2(top - highest), axis=0, keepdims=True)
        both = (highest + jnp.log(summed) * LOG2E, jnp.sum(hit, axis=0, keepdims=True))
        for k in range(2):
            for u in range(Q_TILE // LANES):
                parts[pl.ds(k * PART_POS + t * (Q_TILE // LANES) + u, 1), :] = both[k][
                    :, u * LANES : (u + 1) * LANES
                ]

    score_blocks(q_ref, pos_ref, (emb0, emb1), (pack0, pack1), col_ids, col_logq, state_in, state_out)

    out_ref[:, 0:PART_IDS, :] = jnp.broadcast_to(
        parts[...][None], (N_COLS, PART_IDS, LANES)
    )
    mine = lax.broadcasted_iota(I32, (N_COLS, 8, LANES), 2) // CAP == col % 8
    place = lax.broadcasted_iota(I32, (N_COLS, 8, LANES), 1)
    rows = pl.ds(row * N_COLS, N_COLS)
    found = jnp.zeros((N_COLS, 8, LANES), F32)
    for source, pack in (
        (row, near0), (row ^ 1, near1), (row ^ 2, pack0), (row ^ 3, pack1)
    ):
        found = jnp.where(
            mine & (place == source),
            jnp.broadcast_to(pack[rows, :][:, None, :], (N_COLS, 8, LANES)),
            found,
        )
    out_ref[:, PART_IDS:PART_ROWS, :] = found


SCORE_COST = pl.CostEstimate(
    flops=2 * QDEV * 2 * ITEMS * EMB,
    bytes_accessed=2 * (QDEV * EMB + 2 * ITEMS * EMB),
    transcendentals=QDEV * 2 * ITEMS,
)


def score_near(where, queries, pos, embs, packs):
    vmem_spec = pl.BlockSpec(memory_space=pltpu.VMEM)
    return pl.pallas_call(
        near_kernel,
        in_specs=[pl.BlockSpec(memory_space=pltpu.SMEM)] + [vmem_spec] * 6,
        out_specs=vmem_spec,
        out_shape=jax.ShapeDtypeStruct((3, QDEV // Q_TILE, 8, Q_TILE), F32),
        scratch_shapes=[pltpu.VMEM((2 * ITEMS, LANES), F32)] * 2,
        cost_estimate=SCORE_COST,
        name="score_near",
    )(where, queries, pos, *embs, *packs)


def score_far(where, queries, pos, embs, packs, near_packs, state):
    vmem_spec = pl.BlockSpec(memory_space=pltpu.VMEM)
    return pl.pallas_call(
        far_kernel,
        in_specs=[pl.BlockSpec(memory_space=pltpu.SMEM)] + [vmem_spec] * 9,
        out_specs=vmem_spec,
        out_shape=jax.ShapeDtypeStruct((N_COLS, PART_ROWS, LANES), F32),
        scratch_shapes=[pltpu.VMEM((PART_IDS, LANES), F32)]
        + [pltpu.VMEM((2 * ITEMS, LANES), F32)] * 2,
        cost_estimate=SCORE_COST,
        name="score_far",
    )(where, queries, pos, *embs, *packs, *near_packs, state)


def merge_kernel(parts_ref, loss_ref, ids_ref):
    part = parts_ref[:, 0:PART_POS, :]
    highest = jnp.max(part, axis=0)
    summed = jnp.sum(jnp.exp2(part - highest[None]), axis=0)
    hit = jnp.sum(parts_ref[:, PART_POS:PART_IDS, :], axis=0)
    loss_ref[...] = jnp.log(summed) + (highest - hit) * LN2
    for a in range(N_COLS // 8):
        found = jnp.sum(parts_ref[a * 8 : (a + 1) * 8, PART_IDS:PART_ROWS, :], axis=0).astype(I32)
        for r in range(N_ROWS):
            ids_ref[r * (N_COLS // 8) + a : r * (N_COLS // 8) + a + 1, :] = found[r : r + 1, :]


def merge(parts):
    vmem_spec = pl.BlockSpec(memory_space=pltpu.VMEM)
    return pl.pallas_call(
        merge_kernel,
        in_specs=[vmem_spec],
        out_specs=[vmem_spec, vmem_spec],
        out_shape=[
            jax.ShapeDtypeStruct((QDEV // LANES, LANES), F32),
            jax.ShapeDtypeStruct((N_DEV * CAP // LANES, LANES), I32),
        ],
        name="merge",
    )(parts)


SWAP = [(0, 1), (1, 0)]


def local(features, w_in, w_out, item_ids, item_counts, owners, queries, positives):
    where = jnp.stack([lax.axis_index(ROWS), lax.axis_index(COLS)]).astype(I32)
    emb, send, pack = tower(
        features,
        w_in,
        w_out,
        owners.reshape(BLOCKS, LANES),
        item_ids.reshape(BLOCKS, LANES),
        item_counts.reshape(BLOCKS, LANES),
    )
    emb_y = lax.ppermute(emb, "rows_0", SWAP)
    pack_y = lax.ppermute(pack, "rows_0", SWAP)
    emb_c = lax.ppermute(emb, "rows_1", SWAP)
    pack_c = lax.ppermute(pack, "rows_1", SWAP)
    pool_emb = lax.all_to_all(send, ROWS_COLS, split_axis=0, concat_axis=0, tiled=True)
    emb_yc = lax.ppermute(emb_y, "rows_1", SWAP)
    pack_yc = lax.ppermute(pack_y, "rows_1", SWAP)
    pos = positives.reshape(-1, LANES)
    state = score_near(where, queries, pos, (emb, emb_c), (pack, pack_c))
    parts = score_far(
        where, queries, pos, (emb_y, emb_yc), (pack_y, pack_yc), (pack, pack_c), state
    )
    parts = lax.all_to_all(parts, COLS, split_axis=0, concat_axis=0, tiled=True)
    loss, ids = merge(parts)
    return (pool_emb, ids.reshape(-1), loss.reshape(-1))


def solution(mesh):
    torus = Mesh(
        mesh.devices.reshape(2, 2, 2, 4, 4), ("rows_0", "rows_1", "cols_0", "cols_1", "cols_2")
    )
    placed = (
        P(ROWS_COLS, None),
        P(),
        P(),
        P(ROWS_COLS),
        P(ROWS_COLS),
        P(ROWS_COLS, None),
        P(ROWS, None),
        P(),
    )
    return jax.shard_map(
        local,
        mesh=torus,
        in_specs=placed,
        out_specs=(P(ROWS_COLS, None), P(ROWS_COLS), P(ROWS)),
        check_vma=False,
    )
```

time: 164 us -> 94.7 us (0.58)
  blocking collectives: 42.1 us -> 0 us
  Pallas kernels: 0 us -> 35.4 us
  matrix products: 32.9 us -> 0 us
  other arithmetic: 16.6 us -> 0.61 us
  between operations: 14.4 us -> 0.72 us
  local copies, waits for them, and re-layouts: 17.7 us -> 4.07 us
  waiting for transfers between devices: 17.6 us -> 25.7 us
  starting transfers between devices: 21 us -> 27.8 us
    all_gather x5 -> x0, blocking collectives: 42.1 us -> none  [collected_together(): both, at, found = (lax.all_gather(jnp.concatenate(lines), axis), 0, {})]
    pallas_call x0 -> x4, Pallas kernels: none -> 35.4 us  [the longest x1 12.1 us: tower(): pl.pallas_call(tower_kernel, in_specs=[any_spec, any_spec, any_spec, vmem...]
    dot_general x17 -> x0, matrix products: 32.9 us -> none  [the longest x16 24.3 us: block_stats(): jnp.einsum('qe,ke->qk', q_rows, key_rows, preferred_element_type=jnp.floa...]
    reduce_sum x17 -> x0, other arithmetic: 13.3 us -> none  [the longest x16 12.9 us: block_stats(): jnp.sum(jnp.where(key_ids[None, :] == pos_rows[:, None], raw_scores, 0.0)...]
    ppermute x0 -> x6, waiting for transfers between devices: none -> 12.3 us  [the longest x1 10.3 us: local(): emb_y = lax.ppermute(emb, 'rows_0', SWAP)]
    scatter x2 -> x0, local copies, waits for them, and re-layouts: 10.3 us -> none  [the longest x1 6.01 us: local(): jnp.zeros((slot_count, embedded.shape[1]), jnp.bfloat16).at[slot_index]]
    ppermute x0 -> x6, starting transfers between devices: none -> 8.97 us  [the longest x1 4.99 us: local(): pack_y = lax.ppermute(pack, 'rows_0', SWAP)]
    all_to_all x2, waiting for transfers between devices: 16.9 us -> 13.4 us  [the longest x1 13.4 us: local(): parts = lax.all_to_all(parts, COLS, split_axis=0, concat_axis=0, tiled=True)]
  transfers between devices with their start and end apart: 3 -> 8, of which waited for: 1 -> 3; matrix products, arithmetic and copies ran while one was open for 13% -> 1% of each run, Pallas kernels for 0% -> 23%
where the time goes in v1:
time: 94.7 us; the launch traced here: 94.3 us
  Pallas kernels  35.4 us (37%)
  starting transfers between devices  27.8 us (29%)
  waiting for transfers between devices  25.7 us (27%)
  local copies, waits for them, and re-layouts  4.07 us (4%)
    all_to_all x1, waiting for transfers between devices, local(): parts = lax.all_to_all(parts, COLS, split_axis=0, concat_axis=0, tiled=True)  13.4 us
    pallas_call x1, Pallas kernels, tower(): pl.pallas_call(tower_kernel, in_specs=[any_spec, any_spec, any_spec, vmem...  12.1 us
    pallas_call x1, Pallas kernels, score_far(): pl.pallas_call(far_kernel, in_specs=[pl.BlockSpec(memory_space=pltpu.SMEM...  11 us
    pallas_call x1, Pallas kernels, score_near(): pl.pallas_call(near_kernel, in_specs=[pl.BlockSpec(memory_space=pltpu.SME...  10.5 us
    ppermute x1, waiting for transfers between devices, local(): emb_y = lax.ppermute(emb, 'rows_0', SWAP)  10.3 us
    all_to_all x1, starting transfers between devices, local(): parts = lax.all_to_all(parts, COLS, split_axis=0, concat_axis=0, tiled=True)  9.9 us
    all_to_all x1, starting transfers between devices, local(): lax.all_to_all(send, ROWS_COLS, split_axis=0, concat_axis=0, tiled=True)  8.92 us
    ppermute x1, starting transfers between devices, local(): pack_y = lax.ppermute(pack, 'rows_0', SWAP)  4.99 us
  transfers between devices with their start and end apart: 8, of which 3 were waited for; matrix products, arithmetic and copies ran while one was open for 1% of the time, Pallas kernels for 23%

profile of v1, /device:TPU:0, one launch (start us, length us, event | category | flops | bytes accessed | tf_op | source)
XLA Modules:
  0.0 94.3 jit_solution(6050589487482707509)
XLA Ops:
  0.6 12.1 %tower.1 = (bf16[1024,256]{1,0:T(8,128)(2,1)}, bf16[2048,256]{1,0:T(8,128)(2,1)}, f32[144,128]{1,0:T(8,128)}) custom-call(bf16[1024,2048]{1,0:T(8,128)(2,1)} %feat_hbm.1, bf16[2048,1024]{1,0:T(8,128)(2,1)} %w_in_hbm.1, bf16[1024,256]{1,0:T(8,128)(2,1)} %w_out_hbm.1, s32[8,128]{1,0:T(8,128)} %bitcast.16, s32[8,128]{1,0:T(8,128)} %bitcast.17, s32[8,128]{1,0:T(8,128)} %bitcast.18), custom_call_target="tpu_custom_call" | custom-call | flops 4831838208 | bytes 8388608 | tf_op jit(solution)/shard_map/tower/pallas_call | solution.py:121
  12.8 3.4 %collective-permute-start = (bf16[1024,256]{1,0:T(8,128)(2,1)}, bf16[1024,256]{1,0:T(8,128)(2,1)S(1)}, u32[]{:S(2)}, u32[]{:S(2)}) collective-permute-start(bf16[1024,256]{1,0:T(8,128)(2,1)} %get-tuple-element.9.emb0), channel_id=1, source_target_pairs={{0,64},{64,0},{1,65},{65,1},{2,66},{66,2},{3,67},{67,3},{4,68},{68... | collective-permute-start | bytes 1572872 | tf_op jit(solution)/shard_map/ppermute | solution.py:322
  16.2 8.9 %all-to-all-start = ((bf16[128,16,256]{2,1,0:T(8,128)(2,1)}), bf16[128,16,256]{2,1,0:T(8,128)(2,1)S(1)}, u32[]{:S(2)}, u32[]{:S(2)}) async-start(bf16[128,16,256]{2,1,0:T(8,128)(2,1)} %bitcast.11), calls=%async_computation | async-start | bytes 2097152 | tf_op jit(solution)/shard_map/all_to_all | solution.py:326
  25.1 0.1 collective-permute-start.5
  25.2 10.3 %collective-permute-done.emb0 = bf16[1024,256]{1,0:T(8,128)(2,1)S(1)} collective-permute-done((bf16[1024,256]{1,0:T(8,128)(2,1)}, bf16[1024,256]{1,0:T(8,128)(2,1)S(1)}, u32[]{:S(2)}, u32[]{:S(2)}) %collective-permute-start) | collective-permute-done | bytes 524320 | tf_op jit(solution)/shard_map/ppermute | solution.py:322
  35.5 0.0 copy-start.1
  35.5 0.0 collective-permute-start.1
  35.5 0.5 collective-permute-start.4
  36.0 5.0 %collective-permute-start.2 = (f32[144,128]{1,0:T(8,128)}, f32[144,128]{1,0:T(8,128)S(1)}, u32[]{:S(2)}, u32[]{:S(2)}) collective-permute-start(f32[144,128]{1,0:T(8,128)} %get-tuple-element.10.pack0.near0), channel_id=1, source_target_pairs={{0,64},{64,0},{1,65},{65,1},{2,66},{66,2},{3,67},{67,3},{4,68},{68... | collective-permute-start | bytes 221192 | tf_op jit(solution)/shard_map/ppermute | solution.py:323
  41.0 0.6 pad_add_fusion.where_ref
  41.6 2.0 %collective-permute-done.2.pack0 = f32[144,128]{1,0:T(8,128)S(1)} collective-permute-done((f32[144,128]{1,0:T(8,128)}, f32[144,128]{1,0:T(8,128)S(1)}, u32[]{:S(2)}, u32[]{:S(2)}) %collective-permute-start.2) | collective-permute-done | bytes 73760 | tf_op jit(solution)/shard_map/ppermute | solution.py:323
  43.6 0.0 collective-permute-start.3
  43.6 0.0 collective-permute-done.4.pack1.near1
  43.6 0.0 copy-start.4
  43.6 0.0 collective-permute-done.5.emb1
  43.6 0.0 copy-start.3
  43.6 0.6 copy-done.4
  44.3 0.2 copy-done.3
  44.5 10.5 %score_near.1.before_ref = f32[3,8,8,256]{3,2,1,0:T(8,128)} custom-call(s32[2]{0:T(128)} %pad_add_fusion.where_ref, bf16[2048,256]{1,0:T(8,128)(2,1)} %q_ref.3, s32[64,128]{1,0:T(8,128)} %bitcast.12, bf16[1024,256]{1,0:T(8,128)(2,1)} %get-tuple-element.9.emb0, bf16[1024,256]{1,0:T(8,128)(2,1)} %copy-done.3, f32[144,128]{1,0:T(8,128)} %get-tuple-element.10.pack0.near0, ...), custom_call_target="tpu_custom_call" | custom-call | flops 2147483648 | bytes 2097152 | tf_op jit(solution)/shard_map/score_near/pallas_call | solution.py:258
  55.0 0.0 collective-permute-done.3.pack1
  55.0 0.0 collective-permute-done.1.emb1
  55.0 0.0 copy-done.1
  55.0 0.0 copy-done.5
  55.0 0.6 copy-done.6
  55.6 0.8 copy-done.2
  56.4 11.0 %score_far.1 = f32[32,40,128]{2,1,0:T(8,128)} custom-call(s32[2]{0:T(128)} %pad_add_fusion.where_ref, bf16[2048,256]{1,0:T(8,128)(2,1)} %q_ref.3, s32[64,128]{1,0:T(8,128)} %bitcast.13, bf16[1024,256]{1,0:T(8,128)(2,1)} %copy-done.1, bf16[1024,256]{1,0:T(8,128)(2,1)} %copy-done.2, f32[144,128]{1,0:T(8,128)} %copy-done.5, f32[144,128]{1,0:T(8,128)} %copy-done.6, ...), custom_call_target="tpu_custom_call" | custom-call | flops 2147483648 | bytes 2097152 | tf_op jit(solution)/shard_map/score_far/pallas_call | solution.py:271
  67.4 0.0 all-to-all-done
  67.4 9.9 %all-to-all-start.1 = ((f32[32,40,128]{2,1,0:T(8,128)}), f32[32,40,128]{2,1,0:T(8,128)S(1)}, u32[]{:S(2)}, u32[]{:S(2)}) async-start(f32[32,40,128]{2,1,0:T(8,128)} %score_far.1), calls=%async_computation.1 | async-start | bytes 1310720 | tf_op jit(solution)/shard_map/all_to_all | solution.py:334
  77.3 13.4 %all-to-all-done.1.parts_ref = f32[32,40,128]{2,1,0:T(8,128)S(1)} async-done(((f32[32,40,128]{2,1,0:T(8,128)}), f32[32,40,128]{2,1,0:T(8,128)S(1)}, u32[]{:S(2)}, u32[]{:S(2)}) %all-to-all-start.1) | async-done | bytes 655392 | tf_op jit(solution)/shard_map/all_to_all | solution.py:334
  90.7 0.8 copy-done
  91.5 1.8 %merge.1 = (f32[16,128]{1,0:T(8,128)}, s32[16,128]{1,0:T(8,128)}) custom-call(f32[32,40,128]{2,1,0:T(8,128)} %copy-done), custom_call_target="tpu_custom_call" | custom-call | tf_op jit(solution)/shard_map/merge/pallas_call | solution.py:297
  93.3 1.0 %copy.12 = bf16[2048,256]{1,0:T(8,128)(2,1)} copy(bf16[2048,256]{1,0:T(8,128)(2,1)S(1)} %bitcast.10) | data formatting | bytes 2097152
  (4 shorter events, 0.0 us)
Async XLA Ops:
  12.8 22.7 %collective-permute-start = (bf16[1024,256]{1,0:T(8,128)(2,1)}, bf16[1024,256]{1,0:T(8,128)(2,1)S(1)}, u32[]{:S(2)}, u32[]{:S(2)}) collective-permute-start(bf16[1024,256]{1,0:T(8,128)(2,1)} %get-tuple-element.9.emb0), channel_id=1, source_target_pairs={{0,64},{64,0},{1,65},{65,1},{2,66},{66,2},{3,67},{67,3},{4,68},{68... | collective-permute-start | bytes 1572872 | tf_op jit(solution)/shard_map/ppermute | solution.py:322
  16.2 51.3 %all-to-all-start = ((bf16[128,16,256]{2,1,0:T(8,128)(2,1)}), bf16[128,16,256]{2,1,0:T(8,128)(2,1)S(1)}, u32[]{:S(2)}, u32[]{:S(2)}) async-start(bf16[128,16,256]{2,1,0:T(8,128)(2,1)} %bitcast.11), calls=%async_computation | async-start | bytes 2097152 | tf_op jit(solution)/shard_map/all_to_all | solution.py:326
  25.1 18.5 %collective-permute-start.5 = (bf16[1024,256]{1,0:T(8,128)(2,1)}, bf16[1024,256]{1,0:T(8,128)(2,1)S(1)}, u32[]{:S(2)}, u32[]{:S(2)}) collective-permute-start(bf16[1024,256]{1,0:T(8,128)(2,1)} %get-tuple-element.9.emb0), channel_id=1, source_target_pairs={{0,32},{32,0},{1,33},{33,1},{2,34},{34,2},{3,35},{35,3},{4,36},{36... | collective-permute-start | bytes 1572872 | tf_op jit(solution)/shard_map/ppermute | solution.py:324
  35.5 19.5 %copy-start.1 = (bf16[1024,256]{1,0:T(8,128)(2,1)}, bf16[1024,256]{1,0:T(8,128)(2,1)S(1)}, u32[]{:S(2)}) copy-start(bf16[1024,256]{1,0:T(8,128)(2,1)S(1)} %collective-permute-done.emb0) | copy-start | bytes 1572868
  35.5 19.5 %collective-permute-start.1 = (bf16[1024,256]{1,0:T(8,128)(2,1)S(1)}, bf16[1024,256]{1,0:T(8,128)(2,1)S(1)}, u32[]{:S(2)}, u32[]{:S(2)}) collective-permute-start(bf16[1024,256]{1,0:T(8,128)(2,1)S(1)} %collective-permute-done.emb0), channel_id=1, source_target_pairs={{0,32},{32,0},{1,33},{33,1},{2,34},{34,2},{3,35},{35,3},{4,36},{36... | collective-permute-start | bytes 1572872 | tf_op jit(solution)/shard_map/ppermute | solution.py:327
  35.5 8.1 %collective-permute-start.4 = (f32[144,128]{1,0:T(8,128)}, f32[144,128]{1,0:T(8,128)S(1)}, u32[]{:S(2)}, u32[]{:S(2)}) collective-permute-start(f32[144,128]{1,0:T(8,128)} %get-tuple-element.10.pack0.near0), channel_id=1, source_target_pairs={{0,32},{32,0},{1,33},{33,1},{2,34},{34,2},{3,35},{35,3},{4,36},{36... | collective-permute-start | bytes 221192 | tf_op jit(solution)/shard_map/ppermute | solution.py:325
  36.0 7.6 %collective-permute-start.2 = (f32[144,128]{1,0:T(8,128)}, f32[144,128]{1,0:T(8,128)S(1)}, u32[]{:S(2)}, u32[]{:S(2)}) collective-permute-start(f32[144,128]{1,0:T(8,128)} %get-tuple-element.10.pack0.near0), channel_id=1, source_target_pairs={{0,64},{64,0},{1,65},{65,1},{2,66},{66,2},{3,67},{67,3},{4,68},{68... | collective-permute-start | bytes 221192 | tf_op jit(solution)/shard_map/ppermute | solution.py:323
  43.6 11.4 %copy-start.5 = (f32[144,128]{1,0:T(8,128)}, f32[144,128]{1,0:T(8,128)S(1)}, u32[]{:S(2)}) copy-start(f32[144,128]{1,0:T(8,128)S(1)} %collective-permute-done.2.pack0) | copy-start | bytes 221188
  43.6 11.4 %collective-permute-start.3 = (f32[144,128]{1,0:T(8,128)S(1)}, f32[144,128]{1,0:T(8,128)S(1)}, u32[]{:S(2)}, u32[]{:S(2)}) collective-permute-start(f32[144,128]{1,0:T(8,128)S(1)} %collective-permute-done.2.pack0), channel_id=1, source_target_pairs={{0,32},{32,0},{1,33},{33,1},{2,34},{34,2},{3,35},{35,3},{4,36},{36... | collective-permute-start | bytes 221192 | tf_op jit(solution)/shard_map/ppermute | solution.py:328
  43.6 0.6 copy-start.4
  43.6 0.8 copy-start.3
  55.0 0.6 copy-start.6
  55.6 0.8 copy-start.2
  67.4 23.3 %all-to-all-start.1 = ((f32[32,40,128]{2,1,0:T(8,128)}), f32[32,40,128]{2,1,0:T(8,128)S(1)}, u32[]{:S(2)}, u32[]{:S(2)}) async-start(f32[32,40,128]{2,1,0:T(8,128)} %score_far.1), calls=%async_computation.1 | async-start | bytes 1310720 | tf_op jit(solution)/shard_map/all_to_all | solution.py:334
  90.7 0.8 copy-start

commit v2 on v1

v2 whole, which is shorter than its diff:
```python
import math

import jax
import jax.numpy as jnp
from jax import lax
from jax.experimental import pallas as pl
from jax.experimental.pallas import tpu as pltpu
from jax.sharding import Mesh
from jax.sharding import PartitionSpec as P

ROWS = ("rows_0", "rows_1")
COLS = ("cols_0", "cols_1", "cols_2")
ROWS_COLS = ("rows_0", "rows_1", "cols_0", "cols_1", "cols_2")

F32 = jnp.float32
BF16 = jnp.bfloat16
I32 = jnp.int32

N_DEV = 128
N_ROWS = 4
N_COLS = 32
ITEMS = 1024
CAP = 16
EMB = 256
HID = 1024
F_IN = 2048
QDEV = 2048
LANES = 128
BLOCKS = ITEMS // LANES

LOG2E = math.log2(math.e)
LN2 = math.log(2.0)
SCALE2 = 4.0 / math.sqrt(EMB) * LOG2E
FLOOR = -1e30

EXT_SLOTS = ITEMS
EXT_A = EXT_SLOTS + N_DEV // 2
EXT_B = EXT_A + 16
EXT_C = EXT_B + 16
EXT_ROWS = EXT_C + 16

PART_POS = QDEV // LANES
PART_IDS = 2 * PART_POS
PART_ROWS = PART_IDS + 8

NT = (((1,), (1,)), ((), ()))

K_CHUNK = 512
K_STEPS = F_IN // K_CHUNK
ROW_BLOCK = 256


def tower_kernel(
    feat_hbm, w_in_hbm, w_out_hbm, owners_hbm, ids_hbm, counts_hbm,
    ext_ref, send_ref,
    feat, w_in, w_out, acc, owners_ref, ids_ref, counts_ref, slots,
    feat_sem, w_in_sem, w_out_sem, small_sem,
):
    small = [
        pltpu.make_async_copy(held, ref, small_sem.at[k])
        for k, (held, ref) in enumerate(
            ((owners_hbm, owners_ref), (ids_hbm, ids_ref), (counts_hbm, counts_ref))
        )
    ]
    for copy in small:
        copy.start()
    copies = []
    for k in range(K_STEPS):
        at = pl.ds(k * K_CHUNK, K_CHUNK)
        copies.append(
            (
                pltpu.make_async_copy(w_in_hbm.at[at], w_in.at[at], w_in_sem.at[k]),
                pltpu.make_async_copy(feat_hbm.at[:, at], feat.at[:, at], feat_sem.at[k]),
            )
        )
    w_out_copy = pltpu.make_async_copy(w_out_hbm, w_out, w_out_sem)
    for k in range(2):
        for copy in copies[k]:
            copy.start()

    for copy in small:
        copy.wait()

    owner_iota = lax.broadcasted_iota(I32, (N_DEV, LANES), 0)
    row_iota = lax.broadcasted_iota(I32, (LANES, LANES), 0)
    upper = (row_iota < lax.broadcasted_iota(I32, (LANES, LANES), 1)).astype(F32).astype(BF16)
    seen = jnp.zeros((N_DEV, 1), F32)
    by_slot = jnp.zeros((N_DEV, LANES), F32)
    for j in range(BLOCKS):
        owner = owners_ref[j : j + 1, :]
        onehot = (owner_iota == owner).astype(F32)
        onehot_b = onehot.astype(BF16)
        before = jnp.dot(onehot_b, upper, preferred_element_type=F32) + seen
        rank = jnp.sum(onehot * before, axis=0, keepdims=True).astype(I32)
        seen = seen + jnp.sum(onehot, axis=1, keepdims=True)
        slots[j : j + 1, :] = owner * CAP + rank
        value = ids_ref[j : j + 1, :] + 1
        piece = jnp.where(
            row_iota < CAP,
            value >> 12,
            jnp.where(row_iota < 2 * CAP, (value >> 6) & 63, value & 63),
        )
        here = (row_iota % CAP == rank) & (row_iota < 3 * CAP)
        chosen = jnp.where(here, piece, 0).astype(F32).astype(BF16)
        by_slot = by_slot + lax.dot_general(onehot_b, chosen, NT, preferred_element_type=F32)
    half = N_DEV // 2
    ext_ref[EXT_SLOTS:EXT_A, 0:LANES] = by_slot[0:half, :].astype(BF16)
    ext_ref[EXT_SLOTS:EXT_A, LANES:EMB] = by_slot[half:N_DEV, :].astype(BF16)
    ids = ids_ref[...]
    counts = counts_ref[...]
    none = jnp.zeros((BLOCKS, LANES), I32)
    for at, left, right in (
        (EXT_A, ids >> 12, (ids >> 6) & 63),
        (EXT_B, ids & 63, counts >> 8),
        (EXT_C, counts & 255, none),
    ):
        for lanes, piece in ((slice(0, LANES), left), (slice(LANES, EMB), right)):
            ext_ref[at : at + 16, lanes] = (
                jnp.concatenate([piece, none], axis=0).astype(F32).astype(BF16)
            )

    for k in range(K_STEPS):
        for copy in copies[k]:
            copy.wait()
        if k + 2 < K_STEPS:
            for copy in copies[k + 2]:
                copy.start()
        if k + 2 == K_STEPS:
            w_out_copy.start()
        last = k == K_STEPS - 1
        if last:
            w_out_copy.wait()
        at = slice(k * K_CHUNK, (k + 1) * K_CHUNK)
        for b in range(ITEMS // ROW_BLOCK):
            rows = slice(b * ROW_BLOCK, (b + 1) * ROW_BLOCK)
            part = jnp.dot(feat[rows, at], w_in[at, :], preferred_element_type=F32)
            if k > 0:
                part = acc[rows, :] + part
            if not last:
                acc[rows, :] = part
            else:
                hidden = jnp.maximum(part, 0.0).astype(BF16)
                ext_ref[rows, :] = jnp.dot(
                    hidden, w_out[...], preferred_element_type=F32
                ).astype(BF16)

    chunk = 512
    slot_row = jnp.concatenate([slots[j : j + 1, :] for j in range(BLOCKS)], axis=1)
    for c in range(N_DEV * CAP // chunk):
        place = lax.broadcasted_iota(I32, (chunk, ITEMS), 0) + c * chunk
        chosen = (place == slot_row).astype(F32).astype(BF16)
        send_ref[c * chunk : (c + 1) * chunk, :] = jnp.dot(
            chosen, ext_ref[0:ITEMS, :], preferred_element_type=F32
        ).astype(BF16)


VMEM_SPEC = pl.BlockSpec(memory_space=pltpu.VMEM)
ANY_SPEC = pl.BlockSpec(memory_space=pl.ANY)
SMEM_SPEC = pl.BlockSpec(memory_space=pltpu.SMEM)


def near_core(value):
    return pltpu.with_memory_space_constraint(value, pltpu.VMEM)


def in_hbm(value):
    return pltpu.with_memory_space_constraint(value, pltpu.HBM)


def tower(features, w_in, w_out, owners, ids, counts):
    return pl.pallas_call(
        tower_kernel,
        in_specs=[ANY_SPEC] * 6,
        out_specs=[VMEM_SPEC, VMEM_SPEC],
        out_shape=[
            pltpu.VMEM((EXT_ROWS, EMB), BF16),
            pltpu.VMEM((N_DEV * CAP, EMB), BF16),
        ],
        scratch_shapes=[
            pltpu.VMEM((ITEMS, F_IN), BF16),
            pltpu.VMEM((F_IN, HID), BF16),
            pltpu.VMEM((HID, EMB), BF16),
            pltpu.VMEM((ITEMS, HID), F32),
            pltpu.VMEM((BLOCKS, LANES), I32),
            pltpu.VMEM((BLOCKS, LANES), I32),
            pltpu.VMEM((BLOCKS, LANES), I32),
            pltpu.VMEM((BLOCKS, LANES), I32),
            pltpu.SemaphoreType.DMA((K_STEPS,)),
            pltpu.SemaphoreType.DMA((K_STEPS,)),
            pltpu.SemaphoreType.DMA,
            pltpu.SemaphoreType.DMA((3,)),
        ],
        cost_estimate=pl.CostEstimate(
            flops=2 * ITEMS * F_IN * HID + 2 * ITEMS * HID * EMB,
            bytes_accessed=2 * (ITEMS * F_IN + F_IN * HID),
            transcendentals=0,
        ),
        compiler_params=pltpu.CompilerParams(vmem_limit_bytes=28 << 20),
        name="tower",
    )(*[in_hbm(a) for a in (features, w_in, w_out, owners, ids, counts)])


Q_TILE = 256
Q_PARTS = Q_TILE // LANES
Q_STEPS = QDEV // Q_TILE
I_TILE = 512
GROUPS = I_TILE // 8


def unpack_columns(exts, col_ids, col_logq):
    fill = jnp.zeros((LANES - BLOCKS, LANES), F32)
    for n, ext in enumerate(exts):
        a, b, c = [ext[at : at + 16, :].astype(F32) for at in (EXT_A, EXT_B, EXT_C)]
        a, b, c = a[0:BLOCKS], b[0:BLOCKS], c[0:BLOCKS]
        ids = a[:, 0:LANES] * 4096.0 + a[:, LANES:EMB] * 64.0 + b[:, 0:LANES]
        logq = jnp.log(b[:, LANES:EMB] * 256.0 + c[:, 0:LANES] + 1.0) * LOG2E
        for value, col in ((ids, col_ids), (logq, col_logq)):
            turned = jnp.concatenate([value, fill], axis=0).T
            for j in range(BLOCKS):
                at = n * ITEMS + j * LANES
                col[at : at + LANES, :] = jnp.broadcast_to(turned[:, j : j + 1], (LANES, LANES))


def score_blocks(q_ref, pos_ref, exts, col_ids, col_logq, before, after):
    unpack_columns(exts, col_ids, col_logq)

    def tile_inputs(t):
        q_rows = q_ref[pl.ds(pl.multiple_of(t * Q_TILE, Q_TILE), Q_TILE), :]
        pos_row = jnp.concatenate(
            [pos_ref[pl.ds(t * Q_PARTS + u, 1), :].astype(F32) for u in range(Q_PARTS)], axis=1
        )
        return q_rows, jnp.broadcast_to(pos_row, (8, Q_TILE))

    def raw_scores(q_rows, n, c):
        return lax.dot_general(
            exts[n][c * I_TILE : (c + 1) * I_TILE, :], q_rows, NT, preferred_element_type=F32
        )

    def wide(col, at):
        return jnp.concatenate([col[at : at + 8, :]] * Q_PARTS, axis=1)

    chunks = [(n, c) for n in range(len(exts)) for c in range(ITEMS // I_TILE)]

    def fast_tile(t, worst):
        q_rows, pos8 = tile_inputs(t)
        if before is None:
            raw = raw_scores(q_rows, 0, 0)
            tops = [jnp.full((8, Q_TILE), FLOOR, F32)] * 4
            for g in range(GROUPS):
                logit = raw[g * 8 : g * 8 + 8, :] * SCALE2 - wide(col_logq, g * 8)
                tops[g % 4] = jnp.maximum(tops[g % 4], logit)
            top = jnp.maximum(jnp.maximum(tops[0], tops[1]), jnp.maximum(tops[2], tops[3]))
            shift = jnp.broadcast_to(jnp.max(top, axis=0, keepdims=True), (8, Q_TILE))
            total = jnp.zeros((8, Q_TILE), F32)
            hit = jnp.full((8, Q_TILE), FLOOR, F32)
        else:
            shift, total, hit = [before[k, t] for k in range(3)]
        totals = [total, jnp.zeros((8, Q_TILE), F32)]
        hits = [hit, jnp.full((8, Q_TILE), FLOOR, F32)]
        for n, c in chunks:
            raw = raw_scores(q_rows, n, c)
            for g in range(GROUPS):
                at = n * ITEMS + c * I_TILE + g * 8
                logit = raw[g * 8 : g * 8 + 8, :] * SCALE2 - wide(col_logq, at) - shift
                totals[g % 2] = totals[g % 2] + jnp.exp2(logit)
                hits[g % 2] = jnp.where(wide(col_ids, at) == pos8, logit, hits[g % 2])
        total = totals[0] + totals[1]
        after[0, t] = shift
        after[1, t] = total
        after[2, t] = jnp.maximum(hits[0], hits[1])
        return jnp.maximum(worst, total)

    worst = lax.fori_loop(0, Q_STEPS, fast_tile, jnp.zeros((8, Q_TILE), F32))

    @pl.when(jnp.logical_not(jnp.max(worst) < 1e37))
    def _():
        def safe_tile(t, _):
            q_rows, pos8 = tile_inputs(t)
            if before is None:
                top = jnp.full((8, Q_TILE), FLOOR, F32)
                total = jnp.zeros((8, Q_TILE), F32)
                hit = jnp.full((8, Q_TILE), FLOOR, F32)
            else:
                top, total, hit = [before[k, t] for k in range(3)]
            found = hit > FLOOR / 2
            positive = jnp.where(found, hit + top, 0.0)
            for n, c in chunks:
                raw = raw_scores(q_rows, n, c)
                at = slice(n * ITEMS + c * I_TILE, n * ITEMS + (c + 1) * I_TILE)
                logit = raw * SCALE2 - jnp.concatenate([col_logq[at, :]] * Q_PARTS, axis=1)
                match = jnp.concatenate([col_ids[at, :]] * Q_PARTS, axis=1) == pos8[0:1]
                grouped = logit.reshape(GROUPS, 8, Q_TILE)
                new_top = jnp.maximum(top, jnp.max(grouped, axis=0))
                total = total * jnp.exp2(top - new_top) + jnp.sum(
                    jnp.exp2(grouped - new_top[None]), axis=0
                )
                positive = positive + jnp.sum(
                    jnp.where(match, logit, 0.0).reshape(GROUPS, 8, Q_TILE), axis=0
                )
                found = found | (
                    jnp.max(match.astype(F32).reshape(GROUPS, 8, Q_TILE), axis=0) > 0.0
                )
                top = new_top
            after[0, t] = top
            after[1, t] = total
            after[2, t] = jnp.where(found, positive - top, FLOOR)
            return 0

        lax.fori_loop(0, Q_STEPS, safe_tile, 0)


def own_positives(where_ref, pos_all):
    return pos_all.at[pl.ds(where_ref[0] * (QDEV // LANES), QDEV // LANES)]


def first_kernel(where_ref, q_ref, pos_all, ext0, ext1, state_ref, col_ids, col_logq):
    pos_ref = own_positives(where_ref, pos_all)
    score_blocks(q_ref, pos_ref, (ext0, ext1), col_ids, col_logq, None, state_ref)


def next_kernel(where_ref, q_ref, pos_all, ext, before_ref, state_ref, col_ids, col_logq):
    pos_ref = own_positives(where_ref, pos_all)
    score_blocks(q_ref, pos_ref, (ext,), col_ids, col_logq, before_ref, state_ref)


def last_kernel(
    where_ref, q_ref, pos_all, ext, before_ref, own, sibling, across,
    out_ref, state, parts, col_ids, col_logq,
):
    row = where_ref[0]
    col = where_ref[1]
    pos_ref = own_positives(where_ref, pos_all)
    score_blocks(q_ref, pos_ref, (ext,), col_ids, col_logq, before_ref, state)

    for t in range(Q_STEPS):
        top, total, hit = [state[k, t] for k in range(3)]
        highest = jnp.max(top, axis=0, keepdims=True)
        summed = jnp.sum(total * jnp.exp2(top - highest), axis=0, keepdims=True)
        positive = jnp.sum(jnp.where(hit > FLOOR / 2, hit + top, 0.0), axis=0, keepdims=True)
        both = (highest + jnp.log(summed) * LOG2E, positive)
        for k in range(2):
            for u in range(Q_PARTS):
                at = k * PART_POS + t * Q_PARTS + u
                parts[at : at + 1, :] = both[k][:, u * LANES : (u + 1) * LANES]
    out_ref[:, 0:PART_IDS, :] = jnp.broadcast_to(parts[...][None], (N_COLS, PART_IDS, LANES))

    lane = lax.broadcasted_iota(I32, (N_COLS, LANES), 1)
    place = lax.broadcasted_iota(I32, (N_COLS, 8, LANES), 1)
    slots = pl.ds(EXT_SLOTS + (row % 2) * N_COLS, N_COLS)
    found = jnp.zeros((N_COLS, 8, LANES), F32)
    for source, held in ((row, own), (row ^ 1, sibling), (row ^ 2, across), (row ^ 3, ext)):
        piece = jnp.where(row >= 2, held[slots, LANES:EMB].astype(F32), held[slots, 0:LANES].astype(F32))
        value = (
            piece * 4096.0
            + pltpu.roll(piece, LANES - CAP, 1) * 64.0
            + pltpu.roll(piece, LANES - 2 * CAP, 1)
            - 1.0
        )
        value = pltpu.roll(jnp.where(lane < CAP, value, 0.0), (col % 8) * CAP, 1)
        found = jnp.where(
            place == source, jnp.broadcast_to(value[:, None, :], (N_COLS, 8, LANES)), found
        )
    out_ref[:, PART_IDS:PART_ROWS, :] = found


STATE = ((3, Q_STEPS, 8, Q_TILE), F32)


def scored(kernel, n_blocks, out_shape, scratch, args, name):
    columns = [pltpu.VMEM((n_blocks * ITEMS, LANES), F32)] * 2
    return pl.pallas_call(
        kernel,
        in_specs=[SMEM_SPEC] + [VMEM_SPEC] * (len(args) - 1),
        out_specs=VMEM_SPEC,
        out_shape=pltpu.VMEM(*out_shape),
        scratch_shapes=scratch + columns,
        cost_estimate=pl.CostEstimate(
            flops=2 * QDEV * n_blocks * ITEMS * EMB,
            bytes_accessed=2 * (QDEV * EMB + n_blocks * ITEMS * EMB),
            transcendentals=QDEV * n_blocks * ITEMS,
        ),
        compiler_params=pltpu.CompilerParams(vmem_limit_bytes=20 << 20),
        name=name,
    )(args[0], *[near_core(a) for a in args[1:]])


def merge_kernel(parts_ref, pool_in, loss_ref, ids_ref, pool_out, sem):
    copy = pltpu.make_async_copy(pool_in, pool_out, sem)
    copy.start()
    part = parts_ref[:, 0:PART_POS, :]
    highest = jnp.max(part, axis=0)
    summed = jnp.sum(jnp.exp2(part - highest[None]), axis=0)
    hit = jnp.sum(parts_ref[:, PART_POS:PART_IDS, :], axis=0)
    loss_ref[...] = jnp.log(summed) + (highest - hit) * LN2
    for a in range(N_COLS // 8):
        found = jnp.sum(parts_ref[a * 8 : (a + 1) * 8, PART_IDS:PART_ROWS, :], axis=0).astype(I32)
        for r in range(N_ROWS):
            ids_ref[r * (N_COLS // 8) + a : r * (N_COLS // 8) + a + 1, :] = found[r : r + 1, :]
    copy.wait()


def merge(parts, pool):
    return pl.pallas_call(
        merge_kernel,
        in_specs=[VMEM_SPEC, VMEM_SPEC],
        out_specs=[VMEM_SPEC, VMEM_SPEC, ANY_SPEC],
        out_shape=[
            jax.ShapeDtypeStruct((QDEV // LANES, LANES), F32),
            jax.ShapeDtypeStruct((N_DEV * CAP // LANES, LANES), I32),
            pltpu.HBM(pool.shape, pool.dtype),
        ],
        scratch_shapes=[pltpu.SemaphoreType.DMA],
        compiler_params=pltpu.CompilerParams(vmem_limit_bytes=8 << 20),
        name="merge",
    )(near_core(parts), near_core(pool))


SWAP = [(0, 1), (1, 0)]


def local(features, w_in, w_out, item_ids, item_counts, owners, queries, positives):
    where = jnp.stack([lax.axis_index(ROWS), lax.axis_index(COLS)]).astype(I32)
    pos = positives.reshape(-1, LANES)
    own, send = tower(
        features,
        w_in,
        w_out,
        owners.reshape(BLOCKS, LANES),
        item_ids.reshape(BLOCKS, LANES),
        item_counts.reshape(BLOCKS, LANES),
    )
    across = lax.ppermute(own, "rows_0", SWAP)
    sibling = lax.ppermute(own, "rows_1", SWAP)
    pool_emb = lax.all_to_all(send, ROWS_COLS, split_axis=0, concat_axis=0, tiled=True)
    state = scored(first_kernel, 2, STATE, [], (where, queries, pos, own, sibling), "score_first")
    across, state = lax.optimization_barrier((across, state))
    far = lax.ppermute(across, "rows_1", SWAP)
    state = scored(next_kernel, 1, STATE, [], (where, queries, pos, across, state), "score_next")
    parts = scored(
        last_kernel,
        1,
        ((N_COLS, PART_ROWS, LANES), F32),
        [pltpu.VMEM(*STATE), pltpu.VMEM((PART_IDS, LANES), F32)],
        (where, queries, pos, far, state, own, sibling, across),
        "score_last",
    )
    parts = lax.all_to_all(parts, COLS, split_axis=0, concat_axis=0, tiled=True)
    loss, ids, pool_emb = merge(parts, pool_emb)
    return (pool_emb, ids.reshape(-1), loss.reshape(-1))


def solution(mesh):
    torus = Mesh(
        mesh.devices.reshape(2, 2, 2, 4, 4), ("rows_0", "rows_1", "cols_0", "cols_1", "cols_2")
    )
    placed = (
        P(ROWS_COLS, None),
        P(),
        P(),
        P(ROWS_COLS),
        P(ROWS_COLS),
        P(ROWS_COLS, None),
        P(ROWS, None),
        P(),
    )
    return jax.shard_map(
        local,
        mesh=torus,
        in_specs=placed,
        out_specs=(P(ROWS_COLS, None), P(ROWS_COLS), P(ROWS)),
        check_vma=False,
    )
```

time: 94.7 us -> 84.3 us (0.89)
  waiting for transfers between devices: 25.7 us -> 0.01 us
  blocking collectives: 0 us -> 20.9 us
  starting transfers between devices: 27.8 us -> 12.5 us
  Pallas kernels: 35.4 us -> 48.5 us
  local copies, waits for them, and re-layouts: 4.07 us -> 1.07 us
    all_to_all x0 -> x1, blocking collectives: none -> 20.9 us  [local(): parts = lax.all_to_all(parts, COLS, split_axis=0, concat_axis=0, tiled=True)]
    all_to_all x1 -> x0, waiting for transfers between devices: 13.4 us -> none  [local(): parts = lax.all_to_all(parts, COLS, split_axis=0, concat_axis=0, tiled=True)]
    pallas_call x4 -> x5, Pallas kernels: 35.4 us -> 48.5 us  [the longest x3 37.1 us: scored(): pl.pallas_call(kernel, in_specs=[SMEM_SPEC] + [VMEM_SPEC] * (len(args) -...]
    ppermute x6 -> x3, waiting for transfers between devices: 12.3 us -> 0.01 us  [the longest x1 0.01 us: local(): sibling = lax.ppermute(own, 'rows_1', SWAP)]
    all_to_all x1 -> x0, starting transfers between devices: 9.9 us -> none  [local(): parts = lax.all_to_all(parts, COLS, split_axis=0, concat_axis=0, tiled=True)]
    ppermute x6 -> x3, starting transfers between devices: 8.97 us -> 3.56 us  [the longest x1 3.39 us: local(): across = lax.ppermute(own, 'rows_0', SWAP)]
    unnamed x15 -> x8, local copies, waits for them, and re-layouts: 4.07 us -> 1.07 us
  transfers between devices with their start and end apart: 8 -> 4, of which waited for: 3 -> 0; matrix products, arithmetic and copies ran while one was open for 1% -> 0% of each run, Pallas kernels for 23% -> 44%
where the time goes in v2:
time: 84.3 us; the launch traced here: 83.8 us
  Pallas kernels  48.5 us (58%)
  blocking collectives  20.9 us (25%)
  starting transfers between devices  12.5 us (15%)
  local copies, waits for them, and re-layouts  1.07 us (1%)
    pallas_call x3, Pallas kernels, scored(): pl.pallas_call(kernel, in_specs=[SMEM_SPEC] + [VMEM_SPEC] * (len(args) -...  37.1 us
    all_to_all x1, blocking collectives, local(): parts = lax.all_to_all(parts, COLS, split_axis=0, concat_axis=0, tiled=True)  20.9 us
    pallas_call x1, Pallas kernels, tower(): pl.pallas_call(tower_kernel, in_specs=[ANY_SPEC] * 6, out_specs=[VMEM_SPE...  9.77 us
    all_to_all x1, starting transfers between devices, local(): lax.all_to_all(send, ROWS_COLS, split_axis=0, concat_axis=0, tiled=True)  8.92 us
    ppermute x1, starting transfers between devices, local(): across = lax.ppermute(own, 'rows_0', SWAP)  3.39 us
  transfers between devices with their start and end apart: 4, of which 0 were waited for; matrix products, arithmetic and copies ran while one was open for 0% of the time, Pallas kernels for 44%

profile of v2, /device:TPU:0, one launch (start us, length us, event | category | flops | bytes accessed | tf_op | source)
XLA Modules:
  0.0 83.8 jit_solution(16267338530359430280)
XLA Ops:
  0.6 0.0 copy-start
  0.6 0.0 copy-start.3
  0.7 9.8 %tower.1 = (bf16[1136,256]{1,0:T(8,128)(2,1)S(1)}, bf16[2048,256]{1,0:T(8,128)(2,1)}) custom-call(bf16[1024,2048]{1,0:T(8,128)(2,1)} %feat_hbm.1, bf16[2048,1024]{1,0:T(8,128)(2,1)} %w_in_hbm.1, bf16[1024,256]{1,0:T(8,128)(2,1)} %w_out_hbm.1, s32[8,128]{1,0:T(8,128)} %bitcast.16, s32[8,128]{1,0:T(8,128)} %bitcast.17, s32[8,128]{1,0:T(8,128)} %bitcast.18), custom_call_target="tpu_custom_call" | custom-call | flops 4831838208 | bytes 8388608 | tf_op jit(solution)/shard_map/tower/pallas_call | solution.py:171
  10.4 0.1 collective-permute-start.1
  10.5 3.4 %collective-permute-start = (bf16[1136,256]{1,0:T(8,128)(2,1)S(1)}, bf16[1136,256]{1,0:T(8,128)(2,1)}, u32[]{:S(2)}, u32[]{:S(2)}) collective-permute-start(bf16[1136,256]{1,0:T(8,128)(2,1)S(1)} %get-tuple-element.10.ext0.own), channel_id=1, source_target_pairs={{0,64},{64,0},{1,65},{65,1},{2,66},{66,2},{3,67},{67,3},{4,68},{68... | collective-permute-start | bytes 1744904 | tf_op jit(solution)/shard_map/ppermute | solution.py:432
  13.9 8.9 %all-to-all-start.1 = ((bf16[128,16,256]{2,1,0:T(8,128)(2,1)}), bf16[128,16,256]{2,1,0:T(8,128)(2,1)S(1)}, u32[]{:S(2)}, u32[]{:S(2)}) async-start(bf16[128,16,256]{2,1,0:T(8,128)(2,1)} %bitcast.6), calls=%async_computation.1 | async-start | bytes 2097152 | tf_op jit(solution)/shard_map/all_to_all | solution.py:434
  22.8 0.1 pad_add_fusion.where_ref
  22.9 0.0 collective-permute-done.1.ext1.sibling
  22.9 0.0 copy-start.1
  22.9 0.0 copy-done
  22.9 0.0 copy-done.3
  22.9 16.5 %score_first.1.before_ref = f32[3,8,8,256]{3,2,1,0:T(8,128)S(1)} custom-call(s32[2]{0:T(128)S(1)} %pad_add_fusion.where_ref, bf16[2048,256]{1,0:T(8,128)(2,1)S(1)} %copy-done, s32[64,128]{1,0:T(8,128)S(1)} %bitcast.11, bf16[1136,256]{1,0:T(8,128)(2,1)S(1)} %get-tuple-element.10.ext0.own, bf16[1136,256]{1,0:T(8,128)(2,1)S(1)} %collective-permute-done.1.ext1.sibling), custom_call_target="tpu_custom_call" | custom-call | flops 2147483648 | bytes 2097152 | tf_op jit(solution)/shard_map/score_first/pallas_call | solution.py:371
  39.4 0.0 collective-permute-done.ext.across
  39.4 0.1 collective-permute-start.2
  39.5 10.2 %score_next.1.before_ref = f32[3,8,8,256]{3,2,1,0:T(8,128)S(1)} custom-call(s32[2]{0:T(128)S(1)} %pad_add_fusion.where_ref, bf16[2048,256]{1,0:T(8,128)(2,1)S(1)} %copy-done, s32[64,128]{1,0:T(8,128)S(1)} %bitcast.12, bf16[1136,256]{1,0:T(8,128)(2,1)} %collective-permute-done.ext.across, f32[3,8,8,256]{3,2,1,0:T(8,128)S(1)} %score_first.1.before_ref), custom_call_target="tpu_custom_call" | custom-call | flops 1073741824 | bytes 1572864 | tf_op jit(solution)/shard_map/score_next/pallas_call | solution.py:371
  49.7 0.0 copy-done.1
  49.7 0.0 collective-permute-done.2.ext
  49.7 0.0 copy-start.2
  49.7 1.1 %copy-done.2 = bf16[1136,256]{1,0:T(8,128)(2,1)S(1)} copy-done((bf16[1136,256]{1,0:T(8,128)(2,1)S(1)}, bf16[1136,256]{1,0:T(8,128)(2,1)}, u32[]{:S(2)}) %copy-start.2) | copy-done | bytes 581656
  50.8 10.5 %score_last.1 = f32[32,40,128]{2,1,0:T(8,128)S(1)} custom-call(s32[2]{0:T(128)S(1)} %pad_add_fusion.where_ref, bf16[2048,256]{1,0:T(8,128)(2,1)S(1)} %copy-done, s32[64,128]{1,0:T(8,128)S(1)} %bitcast.13, bf16[1136,256]{1,0:T(8,128)(2,1)S(1)} %collective-permute-done.2.ext, f32[3,8,8,256]{3,2,1,0:T(8,128)S(1)} %score_next.1.before_ref, ...), custom_call_target="tpu_custom_call" | custom-call | flops 1073741824 | bytes 1572864 | tf_op jit(solution)/shard_map/score_last/pallas_call | solution.py:371
  61.3 0.0 all-to-all-done.1
  61.3 20.9 %all_to_all.16.parts_ref = f32[32,40,128]{2,1,0:T(8,128)S(1)} all-to-all(f32[32,40,128]{2,1,0:T(8,128)S(1)} %score_last.1), channel_id=1, replica_groups=mesh['rows_0'=2,'rows_1'=2,'cols_0'=2,'cols_1'=4,'cols_2'=4] {'cols_0','..., dimensions={0} | all-to-all | bytes 1310720 | tf_op jit(solution)/shard_map/all_to_all | solution.py:447
  82.2 1.6 %merge.1 = (f32[16,128]{1,0:T(8,128)}, s32[16,128]{1,0:T(8,128)}, bf16[2048,256]{1,0:T(8,128)(2,1)}) custom-call(f32[32,40,128]{2,1,0:T(8,128)S(1)} %all_to_all.16.parts_ref, bf16[2048,256]{1,0:T(8,128)(2,1)S(1)} %bitcast.10), custom_call_target="tpu_custom_call" | custom-call | tf_op jit(solution)/shard_map/merge/pallas_call | solution.py:403
Async XLA Ops:
  0.6 22.3 %copy-start = (bf16[2048,256]{1,0:T(8,128)(2,1)S(1)}, bf16[2048,256]{1,0:T(8,128)(2,1)}, u32[]{:S(2)}) copy-start(bf16[2048,256]{1,0:T(8,128)(2,1)} %q_ref.5) | copy-start | bytes 3145732
  0.6 22.3 %copy-start.3 = (s32[8192]{0:T(1024)S(1)}, s32[8192]{0:T(1024)}, u32[]{:S(2)}) copy-start(s32[8192]{0:T(1024)} %param.15) | copy-start | bytes 98308
  10.4 12.5 %collective-permute-start.1 = (bf16[1136,256]{1,0:T(8,128)(2,1)S(1)}, bf16[1136,256]{1,0:T(8,128)(2,1)S(1)}, u32[]{:S(2)}, u32[]{:S(2)}) collective-permute-start(bf16[1136,256]{1,0:T(8,128)(2,1)S(1)} %get-tuple-element.10.ext0.own), channel_id=1, source_target_pairs={{0,32},{32,0},{1,33},{33,1},{2,34},{34,2},{3,35},{35,3},{4,36},{36... | collective-permute-start | bytes 1744904 | tf_op jit(solution)/shard_map/ppermute | solution.py:433
  10.5 28.9 %collective-permute-start = (bf16[1136,256]{1,0:T(8,128)(2,1)S(1)}, bf16[1136,256]{1,0:T(8,128)(2,1)}, u32[]{:S(2)}, u32[]{:S(2)}) collective-permute-start(bf16[1136,256]{1,0:T(8,128)(2,1)S(1)} %get-tuple-element.10.ext0.own), channel_id=1, source_target_pairs={{0,64},{64,0},{1,65},{65,1},{2,66},{66,2},{3,67},{67,3},{4,68},{68... | collective-permute-start | bytes 1744904 | tf_op jit(solution)/shard_map/ppermute | solution.py:432
  13.9 47.4 %all-to-all-start.1 = ((bf16[128,16,256]{2,1,0:T(8,128)(2,1)}), bf16[128,16,256]{2,1,0:T(8,128)(2,1)S(1)}, u32[]{:S(2)}, u32[]{:S(2)}) async-start(bf16[128,16,256]{2,1,0:T(8,128)(2,1)} %bitcast.6), calls=%async_computation.1 | async-start | bytes 2097152 | tf_op jit(solution)/shard_map/all_to_all | solution.py:434
  22.9 26.8 %copy-start.1 = (bf16[1136,256]{1,0:T(8,128)(2,1)}, bf16[1136,256]{1,0:T(8,128)(2,1)S(1)}, u32[]{:S(2)}) copy-start(bf16[1136,256]{1,0:T(8,128)(2,1)S(1)} %collective-permute-done.1.ext1.sibling) | copy-start | bytes 1744900
  39.4 10.3 %collective-permute-start.2 = (bf16[1136,256]{1,0:T(8,128)(2,1)}, bf16[1136,256]{1,0:T(8,128)(2,1)S(1)}, u32[]{:S(2)}, u32[]{:S(2)}) collective-permute-start(bf16[1136,256]{1,0:T(8,128)(2,1)} %collective-permute-done.ext.across), channel_id=1, source_target_pairs={{0,32},{32,0},{1,33},{33,1},{2,34},{34,2},{3,35},{35,3},{4,36},{36... | collective-permute-start | bytes 1744904 | tf_op jit(solution)/shard_map/ppermute | solution.py:437
  49.7 1.1 %copy-start.2 = (bf16[1136,256]{1,0:T(8,128)(2,1)S(1)}, bf16[1136,256]{1,0:T(8,128)(2,1)}, u32[]{:S(2)}) copy-start(bf16[1136,256]{1,0:T(8,128)(2,1)} %copy-done.1) | copy-start | bytes 1744900

commit v3 on v2

--- a/solution.py
+++ b/solution.py
@@ -156,7 +156,6 @@
 
 VMEM_SPEC = pl.BlockSpec(memory_space=pltpu.VMEM)
 ANY_SPEC = pl.BlockSpec(memory_space=pl.ANY)
-SMEM_SPEC = pl.BlockSpec(memory_space=pltpu.SMEM)
 
 
 def near_core(value):
@@ -205,6 +204,11 @@
 Q_STEPS = QDEV // Q_TILE
 I_TILE = 512
 GROUPS = I_TILE // 8
+SAMPLE = 16
+
+
+def row_index():
+    return lax.axis_index("rows_0") * 2 + lax.axis_index("rows_1")
 
 
 def unpack_columns(exts, col_ids, col_logq):
@@ -221,13 +225,15 @@
                 col[at : at + LANES, :] = jnp.broadcast_to(turned[:, j : j + 1], (LANES, LANES))
 
 
-def score_blocks(q_ref, pos_ref, exts, col_ids, col_logq, before, after):
-    unpack_columns(exts, col_ids, col_logq)
+def score_tiles(q_ref, pos_all, row, tiles, exts, col_ids, col_logq, out_ref):
+    first, count = tiles
+    out_rows = count * Q_PARTS
 
     def tile_inputs(t):
         q_rows = q_ref[pl.ds(pl.multiple_of(t * Q_TILE, Q_TILE), Q_TILE), :]
+        at = row * (QDEV // LANES) + t * Q_PARTS
         pos_row = jnp.concatenate(
-            [pos_ref[pl.ds(t * Q_PARTS + u, 1), :].astype(F32) for u in range(Q_PARTS)], axis=1
+            [pos_all[pl.ds(at + u, 1), :].astype(F32) for u in range(Q_PARTS)], axis=1
         )
         return q_rows, jnp.broadcast_to(pos_row, (8, Q_TILE))
 
@@ -239,51 +245,50 @@
     def wide(col, at):
         return jnp.concatenate([col[at : at + 8, :]] * Q_PARTS, axis=1)
 
+    def finish(t, top, total, positive):
+        highest = jnp.max(top, axis=0, keepdims=True)
+        summed = jnp.sum(total * jnp.exp2(top - highest), axis=0, keepdims=True)
+        both = (highest + jnp.log(summed) * LOG2E, jnp.sum(positive, axis=0, keepdims=True))
+        for k in range(2):
+            for u in range(Q_PARTS):
+                at = k * out_rows + (t - first) * Q_PARTS + u
+                out_ref[pl.ds(at, 1), :] = both[k][:, u * LANES : (u + 1) * LANES]
+
     chunks = [(n, c) for n in range(len(exts)) for c in range(ITEMS // I_TILE)]
 
     def fast_tile(t, worst):
         q_rows, pos8 = tile_inputs(t)
-        if before is None:
-            raw = raw_scores(q_rows, 0, 0)
-            tops = [jnp.full((8, Q_TILE), FLOOR, F32)] * 4
-            for g in range(GROUPS):
-                logit = raw[g * 8 : g * 8 + 8, :] * SCALE2 - wide(col_logq, g * 8)
-                tops[g % 4] = jnp.maximum(tops[g % 4], logit)
-            top = jnp.maximum(jnp.maximum(tops[0], tops[1]), jnp.maximum(tops[2], tops[3]))
-            shift = jnp.broadcast_to(jnp.max(top, axis=0, keepdims=True), (8, Q_TILE))
-            total = jnp.zeros((8, Q_TILE), F32)
-            hit = jnp.full((8, Q_TILE), FLOOR, F32)
-        else:
-            shift, total, hit = [before[k, t] for k in range(3)]
-        totals = [total, jnp.zeros((8, Q_TILE), F32)]
-        hits = [hit, jnp.full((8, Q_TILE), FLOOR, F32)]
+        shift = None
+        totals = [jnp.zeros((8, Q_TILE), F32)] * 2
+        hits = [jnp.full((8, Q_TILE), FLOOR, F32)] * 2
         for n, c in chunks:
             raw = raw_scores(q_rows, n, c)
+            if shift is None:
+                tops = [jnp.full((8, Q_TILE), FLOOR, F32)] * 2
+                for g in range(SAMPLE):
+                    logit = raw[g * 8 : g * 8 + 8, :] * SCALE2 - wide(col_logq, g * 8)
+                    tops[g % 2] = jnp.maximum(tops[g % 2], logit)
+                top = jnp.maximum(tops[0], tops[1])
+                shift = jnp.broadcast_to(jnp.max(top, axis=0, keepdims=True), (8, Q_TILE))
             for g in range(GROUPS):
                 at = n * ITEMS + c * I_TILE + g * 8
                 logit = raw[g * 8 : g * 8 + 8, :] * SCALE2 - wide(col_logq, at) - shift
                 totals[g % 2] = totals[g % 2] + jnp.exp2(logit)
                 hits[g % 2] = jnp.where(wide(col_ids, at) == pos8, logit, hits[g % 2])
         total = totals[0] + totals[1]
-        after[0, t] = shift
-        after[1, t] = total
-        after[2, t] = jnp.maximum(hits[0], hits[1])
+        hit = jnp.maximum(hits[0], hits[1])
+        finish(t, shift, total, jnp.where(hit > FLOOR / 2, hit + shift, 0.0))
         return jnp.maximum(worst, total)
 
-    worst = lax.fori_loop(0, Q_STEPS, fast_tile, jnp.zeros((8, Q_TILE), F32))
+    worst = lax.fori_loop(first, first + count, fast_tile, jnp.zeros((8, Q_TILE), F32))
 
     @pl.when(jnp.logical_not(jnp.max(worst) < 1e37))
     def _():
         def safe_tile(t, _):
             q_rows, pos8 = tile_inputs(t)
-            if before is None:
-                top = jnp.full((8, Q_TILE), FLOOR, F32)
-                total = jnp.zeros((8, Q_TILE), F32)
-                hit = jnp.full((8, Q_TILE), FLOOR, F32)
-            else:
-                top, total, hit = [before[k, t] for k in range(3)]
-            found = hit > FLOOR / 2
-            positive = jnp.where(found, hit + top, 0.0)
+            top = jnp.full((8, Q_TILE), FLOOR, F32)
+            total = jnp.zeros((8, Q_TILE), F32)
+            positive = jnp.zeros((8, Q_TILE), F32)
             for n, c in chunks:
                 raw = raw_scores(q_rows, n, c)
                 at = slice(n * ITEMS + c * I_TILE, n * ITEMS + (c + 1) * I_TILE)
@@ -297,91 +302,82 @@
                 positive = positive + jnp.sum(
                     jnp.where(match, logit, 0.0).reshape(GROUPS, 8, Q_TILE), axis=0
                 )
-                found = found | (
-                    jnp.max(match.astype(F32).reshape(GROUPS, 8, Q_TILE), axis=0) > 0.0
-                )
                 top = new_top
-            after[0, t] = top
-            after[1, t] = total
-            after[2, t] = jnp.where(found, positive - top, FLOOR)
+            finish(t, top, total, positive)
             return 0
 
-        lax.fori_loop(0, Q_STEPS, safe_tile, 0)
-
-
-def own_positives(where_ref, pos_all):
-    return pos_all.at[pl.ds(where_ref[0] * (QDEV // LANES), QDEV // LANES)]
-
-
-def first_kernel(where_ref, q_ref, pos_all, ext0, ext1, state_ref, col_ids, col_logq):
-    pos_ref = own_positives(where_ref, pos_all)
-    score_blocks(q_ref, pos_ref, (ext0, ext1), col_ids, col_logq, None, state_ref)
-
-
-def next_kernel(where_ref, q_ref, pos_all, ext, before_ref, state_ref, col_ids, col_logq):
-    pos_ref = own_positives(where_ref, pos_all)
-    score_blocks(q_ref, pos_ref, (ext,), col_ids, col_logq, before_ref, state_ref)
-
-
-def last_kernel(
-    where_ref, q_ref, pos_all, ext, before_ref, own, sibling, across,
-    out_ref, state, parts, col_ids, col_logq,
-):
-    row = where_ref[0]
-    col = where_ref[1]
-    pos_ref = own_positives(where_ref, pos_all)
-    score_blocks(q_ref, pos_ref, (ext,), col_ids, col_logq, before_ref, state)
-
-    for t in range(Q_STEPS):
-        top, total, hit = [state[k, t] for k in range(3)]
-        highest = jnp.max(top, axis=0, keepdims=True)
-        summed = jnp.sum(total * jnp.exp2(top - highest), axis=0, keepdims=True)
-        positive = jnp.sum(jnp.where(hit > FLOOR / 2, hit + top, 0.0), axis=0, keepdims=True)
-        both = (highest + jnp.log(summed) * LOG2E, positive)
-        for k in range(2):
-            for u in range(Q_PARTS):
-                at = k * PART_POS + t * Q_PARTS + u
-                parts[at : at + 1, :] = both[k][:, u * LANES : (u + 1) * LANES]
-    out_ref[:, 0:PART_IDS, :] = jnp.broadcast_to(parts[...][None], (N_COLS, PART_IDS, LANES))
-
+        lax.fori_loop(first, first + count, safe_tile, 0)
+
+
+def slot_ids(held, row):
+    shift = (lax.axis_index("cols_1") * 4 + lax.axis_index("cols_2")) % 8 * CAP
     lane = lax.broadcasted_iota(I32, (N_COLS, LANES), 1)
+    slots = pl.ds(EXT_SLOTS + (row % 2) * N_COLS, N_COLS)
+    piece = jnp.where(
+        row >= 2, held[slots, LANES:EMB].astype(F32), held[slots, 0:LANES].astype(F32)
+    )
+    value = (
+        piece * 4096.0
+        + pltpu.roll(piece, LANES - CAP, 1) * 64.0
+        + pltpu.roll(piece, LANES - 2 * CAP, 1)
+        - 1.0
+    )
+    return pltpu.roll(jnp.where(lane < CAP, value, 0.0), shift, 1)
+
+
+def score_and_list(q_ref, pos_all, exts, out_ref, col_ids, col_logq):
+    row = row_index()
+    unpack_columns(exts, col_ids, col_logq)
+    for n, ext in enumerate(exts):
+        out_ref[PART_IDS + n * N_COLS : PART_IDS + (n + 1) * N_COLS, :] = slot_ids(ext, row)
+    score_tiles(q_ref, pos_all, row, (0, Q_STEPS), exts, col_ids, col_logq, out_ref)
+
+
+def first_kernel(q_ref, pos_all, own, out_ref, col_ids, col_logq):
+    score_and_list(q_ref, pos_all, (own,), out_ref, col_ids, col_logq)
+
+
+def next_kernel(q_ref, pos_all, sibling, across, out_ref, col_ids, col_logq):
+    score_and_list(q_ref, pos_all, (sibling, across), out_ref, col_ids, col_logq)
+
+
+def last_kernel(q_ref, pos_all, far, first, middle, out_ref, last, col_ids, col_logq):
+    score_and_list(q_ref, pos_all, (far,), last, col_ids, col_logq)
+    held = (first, middle, last)
+    sums = [ref[0:PART_POS, :] for ref in held]
+    highest = jnp.maximum(jnp.maximum(sums[0], sums[1]), sums[2])
+    total = sum(jnp.exp2(value - highest) for value in sums)
+    positive = sum(ref[PART_POS:PART_IDS, :] for ref in held)
+    parts = jnp.concatenate([highest + jnp.log(total) * LOG2E, positive], axis=0)
+    out_ref[:, 0:PART_IDS, :] = jnp.broadcast_to(parts[None], (N_COLS, PART_IDS, LANES))
+
+    row = row_index()
     place = lax.broadcasted_iota(I32, (N_COLS, 8, LANES), 1)
-    slots = pl.ds(EXT_SLOTS + (row % 2) * N_COLS, N_COLS)
     found = jnp.zeros((N_COLS, 8, LANES), F32)
-    for source, held in ((row, own), (row ^ 1, sibling), (row ^ 2, across), (row ^ 3, ext)):
-        piece = jnp.where(row >= 2, held[slots, LANES:EMB].astype(F32), held[slots, 0:LANES].astype(F32))
-        value = (
-            piece * 4096.0
-            + pltpu.roll(piece, LANES - CAP, 1) * 64.0
-            + pltpu.roll(piece, LANES - 2 * CAP, 1)
-            - 1.0
-        )
-        value = pltpu.roll(jnp.where(lane < CAP, value, 0.0), (col % 8) * CAP, 1)
+    for source, (ref, n) in enumerate(((first, 0), (middle, 0), (middle, 1), (last, 0))):
+        ids = ref[PART_IDS + n * N_COLS : PART_IDS + (n + 1) * N_COLS, :]
         found = jnp.where(
-            place == source, jnp.broadcast_to(value[:, None, :], (N_COLS, 8, LANES)), found
+            place == (row ^ source), jnp.broadcast_to(ids[:, None, :], (N_COLS, 8, LANES)), found
         )
     out_ref[:, PART_IDS:PART_ROWS, :] = found
-
-
-STATE = ((3, Q_STEPS, 8, Q_TILE), F32)
 
 
 def scored(kernel, n_blocks, out_shape, scratch, args, name):
     columns = [pltpu.VMEM((n_blocks * ITEMS, LANES), F32)] * 2
     return pl.pallas_call(
         kernel,
-        in_specs=[SMEM_SPEC] + [VMEM_SPEC] * (len(args) - 1),
+        in_specs=[VMEM_SPEC] * len(args),
         out_specs=VMEM_SPEC,
-        out_shape=pltpu.VMEM(*out_shape),
+        out_shape=pltpu.VMEM(out_shape, F32),
         scratch_shapes=scratch + columns,
         cost_estimate=pl.CostEstimate(
             flops=2 * QDEV * n_blocks * ITEMS * EMB,
-            bytes_accessed=2 * (QDEV * EMB + n_blocks * ITEMS * EMB),
+            bytes_accessed=2 * n_blocks * ITEMS * EMB,
             transcendentals=QDEV * n_blocks * ITEMS,
         ),
         compiler_params=pltpu.CompilerParams(vmem_limit_bytes=20 << 20),
         name=name,
-    )(args[0], *[near_core(a) for a in args[1:]])
+    )(*[near_core(a) for a in args])
 
 
 def merge_kernel(parts_ref, pool_in, loss_ref, ids_ref, pool_out, sem):
@@ -419,7 +415,6 @@
 
 
 def local(features, w_in, w_out, item_ids, item_counts, owners, queries, positives):
-    where = jnp.stack([lax.axis_index(ROWS), lax.axis_index(COLS)]).astype(I32)
     pos = positives.reshape(-1, LANES)
     own, send = tower(
         features,
@@ -431,17 +426,19 @@
     )
     across = lax.ppermute(own, "rows_0", SWAP)
     sibling = lax.ppermute(own, "rows_1", SWAP)
+    one = (PART_IDS + N_COLS, LANES)
+    two = (PART_IDS + 2 * N_COLS, LANES)
+    first = scored(first_kernel, 1, one, [], (queries, pos, own), "score_first")
+    send, _ = lax.optimization_barrier((send, first))
     pool_emb = lax.all_to_all(send, ROWS_COLS, split_axis=0, concat_axis=0, tiled=True)
-    state = scored(first_kernel, 2, STATE, [], (where, queries, pos, own, sibling), "score_first")
-    across, state = lax.optimization_barrier((across, state))
     far = lax.ppermute(across, "rows_1", SWAP)
-    state = scored(next_kernel, 1, STATE, [], (where, queries, pos, across, state), "score_next")
+    middle = scored(next_kernel, 2, two, [], (queries, pos, sibling, across), "score_next")
     parts = scored(
         last_kernel,
         1,
-        ((N_COLS, PART_ROWS, LANES), F32),
-        [pltpu.VMEM(*STATE), pltpu.VMEM((PART_IDS, LANES), F32)],
-        (where, queries, pos, far, state, own, sibling, across),
+        (N_COLS, PART_ROWS, LANES),
+        [pltpu.VMEM(one, F32)],
+        (queries, pos, far, first, middle),
         "score_last",
     )
     parts = lax.all_to_all(parts, COLS, split_axis=0, concat_axis=0, tiled=True)

time: 84.3 us -> 80.8 us (0.958)
  Pallas kernels: 48.5 us -> 44.8 us
  waiting for transfers between devices: 0.01 us -> 1.49 us
  local copies, waits for them, and re-layouts: 1.07 us -> 0.01 us
    pallas_call x3, Pallas kernels: 37.1 us -> 33.5 us  [scored(): pl.pallas_call(kernel, in_specs=[VMEM_SPEC] * len(args), out_specs=VMEM_S...]
    ppermute x1, waiting for transfers between devices: 0.01 us -> 1.48 us  [local(): sibling = lax.ppermute(own, 'rows_1', SWAP)]
    unnamed x8 -> x4, local copies, waits for them, and re-layouts: 1.07 us -> 0.01 us
  transfers between devices with their start and end apart: 4 -> 4, of which waited for: 0 -> 1; matrix products, arithmetic and copies ran while one was open for 0% -> 0% of each run, Pallas kernels for 44% -> 42%
where the time goes in v3:
time: 80.8 us; the launch traced here: 80.6 us
  Pallas kernels  44.8 us (55%)
  blocking collectives  20.7 us (26%)
  starting transfers between devices  12.9 us (16%)
  waiting for transfers between devices  1.49 us (2%)
    pallas_call x3, Pallas kernels, scored(): pl.pallas_call(kernel, in_specs=[VMEM_SPEC] * len(args), out_specs=VMEM_S...  33.5 us
    all_to_all x1, blocking collectives, local(): parts = lax.all_to_all(parts, COLS, split_axis=0, concat_axis=0, tiled=True)  20.7 us
    pallas_call x1, Pallas kernels, tower(): pl.pallas_call(tower_kernel, in_specs=[ANY_SPEC] * 6, out_specs=[VMEM_SPE...  9.77 us
    all_to_all x1, starting transfers between devices, local(): lax.all_to_all(send, ROWS_COLS, split_axis=0, concat_axis=0, tiled=True)  8.93 us
    ppermute x1, starting transfers between devices, local(): across = lax.ppermute(own, 'rows_0', SWAP)  3.39 us
  transfers between devices with their start and end apart: 4, of which 1 were waited for; matrix products, arithmetic and copies ran while one was open for 0% of the time, Pallas kernels for 42%

profile of v3, /device:TPU:0, one launch (start us, length us, event | category | flops | bytes accessed | tf_op | source)
XLA Modules:
  0.0 80.6 jit_solution(1321987054423515337)
XLA Ops:
  0.6 0.0 copy-start
  0.6 0.0 copy-start.1
  0.7 9.8 %tower.1 = (bf16[1136,256]{1,0:T(8,128)(2,1)S(1)}, bf16[2048,256]{1,0:T(8,128)(2,1)}) custom-call(bf16[1024,2048]{1,0:T(8,128)(2,1)} %feat_hbm.1, bf16[2048,1024]{1,0:T(8,128)(2,1)} %w_in_hbm.1, bf16[1024,256]{1,0:T(8,128)(2,1)} %w_out_hbm.1, s32[8,128]{1,0:T(8,128)} %bitcast.14, s32[8,128]{1,0:T(8,128)} %bitcast.15, s32[8,128]{1,0:T(8,128)} %bitcast.16), custom_call_target="tpu_custom_call" | custom-call | flops 4831838208 | bytes 8388608 | tf_op jit(solution)/shard_map/tower/pallas_call | solution.py:170
  10.4 3.4 %collective-permute-start = (bf16[1136,256]{1,0:T(8,128)(2,1)S(1)}, bf16[1136,256]{1,0:T(8,128)(2,1)S(1)}, u32[]{:S(2)}, u32[]{:S(2)}) collective-permute-start(bf16[1136,256]{1,0:T(8,128)(2,1)S(1)} %get-tuple-element.9.own), channel_id=1, source_target_pairs={{0,64},{64,0},{1,65},{65,1},{2,66},{66,2},{3,67},{67,3},{4,68},{68... | collective-permute-start | bytes 1744904 | tf_op jit(solution)/shard_map/ppermute | solution.py:427
  13.8 0.0 copy-done
  13.8 0.0 copy-done.1
  13.8 9.3 %score_first.1.first = f32[64,128]{1,0:T(8,128)S(1)} custom-call(bf16[2048,256]{1,0:T(8,128)(2,1)S(1)} %copy-done, s32[64,128]{1,0:T(8,128)S(1)} %bitcast.9, bf16[1136,256]{1,0:T(8,128)(2,1)S(1)} %get-tuple-element.9.own), custom_call_target="tpu_custom_call" | custom-call | flops 1073741824 | bytes 524288 | tf_op jit(solution)/shard_map/score_first/pallas_call | solution.py:367
  23.1 8.9 %all-to-all-start.1 = ((bf16[128,16,256]{2,1,0:T(8,128)(2,1)}), bf16[128,16,256]{2,1,0:T(8,128)(2,1)S(1)}, u32[]{:S(2)}, u32[]{:S(2)}) async-start(bf16[128,16,256]{2,1,0:T(8,128)(2,1)} %bitcast.4), calls=%async_computation.1 | async-start | bytes 2097152 | tf_op jit(solution)/shard_map/all_to_all | solution.py:433
  32.0 0.1 collective-permute-start.2
  32.1 0.0 collective-permute-done.across
  32.1 0.5 collective-permute-start.1
  32.6 1.5 %collective-permute-done.2.sibling = bf16[1136,256]{1,0:T(8,128)(2,1)S(1)} collective-permute-done((bf16[1136,256]{1,0:T(8,128)(2,1)S(1)}, bf16[1136,256]{1,0:T(8,128)(2,1)S(1)}, u32[]{:S(2)}, u32[]{:S(2)}) %collective-permute-start.2) | collective-permute-done | bytes 581664 | tf_op jit(solution)/shard_map/ppermute | solution.py:428
  34.1 14.8 %score_next.1.middle = f32[96,128]{1,0:T(8,128)S(1)} custom-call(bf16[2048,256]{1,0:T(8,128)(2,1)S(1)} %copy-done, s32[64,128]{1,0:T(8,128)S(1)} %bitcast.10, bf16[1136,256]{1,0:T(8,128)(2,1)S(1)} %collective-permute-done.2.sibling, bf16[1136,256]{1,0:T(8,128)(2,1)S(1)} %collective-permute-done.across), custom_call_target="tpu_custom_call" | custom-call | flops 2147483648 | bytes 1048576 | tf_op jit(solution)/shard_map/score_next/pallas_call | solution.py:367
  48.9 0.0 collective-permute-done.1.far
  48.9 9.4 %score_last.1 = f32[32,40,128]{2,1,0:T(8,128)S(1)} custom-call(bf16[2048,256]{1,0:T(8,128)(2,1)S(1)} %copy-done, s32[64,128]{1,0:T(8,128)S(1)} %bitcast.11, bf16[1136,256]{1,0:T(8,128)(2,1)S(1)} %collective-permute-done.1.far, f32[64,128]{1,0:T(8,128)S(1)} %score_first.1.first, f32[96,128]{1,0:T(8,128)S(1)} %score_next.1.middle), custom_call_target="tpu_custom_call" | custom-call | flops 1073741824 | bytes 524288 | tf_op jit(solution)/shard_map/score_last/pallas_call | solution.py:367
  58.3 0.0 all-to-all-done.1
  58.3 20.7 %all_to_all.16.parts_ref = f32[32,40,128]{2,1,0:T(8,128)S(1)} all-to-all(f32[32,40,128]{2,1,0:T(8,128)S(1)} %score_last.1), channel_id=1, replica_groups=mesh['rows_0'=2,'rows_1'=2,'cols_0'=2,'cols_1'=4,'cols_2'=4] {'cols_0','..., dimensions={0} | all-to-all | bytes 1310720 | tf_op jit(solution)/shard_map/all_to_all | solution.py:444
  79.1 1.6 %merge.1 = (f32[16,128]{1,0:T(8,128)}, s32[16,128]{1,0:T(8,128)}, bf16[2048,256]{1,0:T(8,128)(2,1)}) custom-call(f32[32,40,128]{2,1,0:T(8,128)S(1)} %all_to_all.16.parts_ref, bf16[2048,256]{1,0:T(8,128)(2,1)S(1)} %bitcast.8), custom_call_target="tpu_custom_call" | custom-call | tf_op jit(solution)/shard_map/merge/pallas_call | solution.py:399
Async XLA Ops:
  0.6 13.2 %copy-start = (bf16[2048,256]{1,0:T(8,128)(2,1)S(1)}, bf16[2048,256]{1,0:T(8,128)(2,1)}, u32[]{:S(2)}) copy-start(bf16[2048,256]{1,0:T(8,128)(2,1)} %q_ref.5) | copy-start | bytes 3145732
  0.6 13.2 %copy-start.1 = (s32[8192]{0:T(1024)S(1)}, s32[8192]{0:T(1024)}, u32[]{:S(2)}) copy-start(s32[8192]{0:T(1024)} %param.15) | copy-start | bytes 98308
  10.4 21.7 %collective-permute-start = (bf16[1136,256]{1,0:T(8,128)(2,1)S(1)}, bf16[1136,256]{1,0:T(8,128)(2,1)S(1)}, u32[]{:S(2)}, u32[]{:S(2)}) collective-permute-start(bf16[1136,256]{1,0:T(8,128)(2,1)S(1)} %get-tuple-element.9.own), channel_id=1, source_target_pairs={{0,64},{64,0},{1,65},{65,1},{2,66},{66,2},{3,67},{67,3},{4,68},{68... | collective-permute-start | bytes 1744904 | tf_op jit(solution)/shard_map/ppermute | solution.py:427
  23.1 35.2 %all-to-all-start.1 = ((bf16[128,16,256]{2,1,0:T(8,128)(2,1)}), bf16[128,16,256]{2,1,0:T(8,128)(2,1)S(1)}, u32[]{:S(2)}, u32[]{:S(2)}) async-start(bf16[128,16,256]{2,1,0:T(8,128)(2,1)} %bitcast.4), calls=%async_computation.1 | async-start | bytes 2097152 | tf_op jit(solution)/shard_map/all_to_all | solution.py:433
  32.0 2.1 %collective-permute-start.2 = (bf16[1136,256]{1,0:T(8,128)(2,1)S(1)}, bf16[1136,256]{1,0:T(8,128)(2,1)S(1)}, u32[]{:S(2)}, u32[]{:S(2)}) collective-permute-start(bf16[1136,256]{1,0:T(8,128)(2,1)S(1)} %get-tuple-element.9.own), channel_id=1, source_target_pairs={{0,32},{32,0},{1,33},{33,1},{2,34},{34,2},{3,35},{35,3},{4,36},{36... | collective-permute-start | bytes 1744904 | tf_op jit(solution)/shard_map/ppermute | solution.py:428
  32.1 16.8 %collective-permute-start.1 = (bf16[1136,256]{1,0:T(8,128)(2,1)S(1)}, bf16[1136,256]{1,0:T(8,128)(2,1)S(1)}, u32[]{:S(2)}, u32[]{:S(2)}) collective-permute-start(bf16[1136,256]{1,0:T(8,128)(2,1)S(1)} %collective-permute-done.across), channel_id=1, source_target_pairs={{0,32},{32,0},{1,33},{33,1},{2,34},{34,2},{3,35},{35,3},{4,36},{36... | collective-permute-start | bytes 1744904 | tf_op jit(solution)/shard_map/ppermute | solution.py:434

commit v4 on v3

--- a/solution.py
+++ b/solution.py
@@ -42,11 +42,14 @@
 PART_POS = QDEV // LANES
 PART_IDS = 2 * PART_POS
 PART_ROWS = PART_IDS + 8
+N_X = 4
+N_PEERS = N_COLS // N_X
+X_ROWS = PART_IDS + N_ROWS * N_PEERS
 
 NT = (((1,), (1,)), ((), ()))
 
-K_CHUNK = 512
-K_STEPS = F_IN // K_CHUNK
+K_AT = (0, 256, 1024, F_IN)
+K_STEPS = len(K_AT) - 1
 ROW_BLOCK = 256
 
 
@@ -66,7 +69,7 @@
         copy.start()
     copies = []
     for k in range(K_STEPS):
-        at = pl.ds(k * K_CHUNK, K_CHUNK)
+        at = pl.ds(K_AT[k], K_AT[k + 1] - K_AT[k])
         copies.append(
             (
                 pltpu.make_async_copy(w_in_hbm.at[at], w_in.at[at], w_in_sem.at[k]),
@@ -130,7 +133,7 @@
         last = k == K_STEPS - 1
         if last:
             w_out_copy.wait()
-        at = slice(k * K_CHUNK, (k + 1) * K_CHUNK)
+        at = slice(K_AT[k], K_AT[k + 1])
         for b in range(ITEMS // ROW_BLOCK):
             rows = slice(b * ROW_BLOCK, (b + 1) * ROW_BLOCK)
             part = jnp.dot(feat[rows, at], w_in[at, :], preferred_element_type=F32)
@@ -199,7 +202,7 @@
     )(*[in_hbm(a) for a in (features, w_in, w_out, owners, ids, counts)])
 
 
-Q_TILE = 256
+Q_TILE = 512
 Q_PARTS = Q_TILE // LANES
 Q_STEPS = QDEV // Q_TILE
 I_TILE = 512
@@ -280,7 +283,7 @@
         finish(t, shift, total, jnp.where(hit > FLOOR / 2, hit + shift, 0.0))
         return jnp.maximum(worst, total)
 
-    worst = lax.fori_loop(first, first + count, fast_tile, jnp.zeros((8, Q_TILE), F32))
+    worst = lax.fori_loop(first, first + count, fast_tile, jnp.zeros((8, Q_TILE), F32), unroll=True)
 
     @pl.when(jnp.logical_not(jnp.max(worst) < 1e37))
     def _():
@@ -333,15 +336,18 @@
     score_tiles(q_ref, pos_all, row, (0, Q_STEPS), exts, col_ids, col_logq, out_ref)
 
 
-def first_kernel(q_ref, pos_all, own, out_ref, col_ids, col_logq):
-    score_and_list(q_ref, pos_all, (own,), out_ref, col_ids, col_logq)
-
-
-def next_kernel(q_ref, pos_all, sibling, across, out_ref, col_ids, col_logq):
-    score_and_list(q_ref, pos_all, (sibling, across), out_ref, col_ids, col_logq)
-
-
-def last_kernel(q_ref, pos_all, far, first, middle, out_ref, last, col_ids, col_logq):
+def first_kernel(q_ref, pos_all, own, sibling, out_ref, col_ids, col_logq):
+    score_and_list(q_ref, pos_all, (own, sibling), out_ref, col_ids, col_logq)
+
+
+def next_kernel(q_ref, pos_all, across, first, out_ref, col_ids, col_logq):
+    del first
+    score_and_list(q_ref, pos_all, (across,), out_ref, col_ids, col_logq)
+
+
+def last_kernel(q_ref, pos_all, far, first, middle, mine, *rest):
+    to_x = rest[0 : N_X - 1]
+    last, col_ids, col_logq = rest[N_X - 1 :]
     score_and_list(q_ref, pos_all, (far,), last, col_ids, col_logq)
     held = (first, middle, last)
     sums = [ref[0:PART_POS, :] for ref in held]
@@ -349,26 +355,62 @@
     total = sum(jnp.exp2(value - highest) for value in sums)
     positive = sum(ref[PART_POS:PART_IDS, :] for ref in held)
     parts = jnp.concatenate([highest + jnp.log(total) * LOG2E, positive], axis=0)
-    out_ref[:, 0:PART_IDS, :] = jnp.broadcast_to(parts[None], (N_COLS, PART_IDS, LANES))
-
     row = row_index()
-    place = lax.broadcasted_iota(I32, (N_COLS, 8, LANES), 1)
-    found = jnp.zeros((N_COLS, 8, LANES), F32)
-    for source, (ref, n) in enumerate(((first, 0), (middle, 0), (middle, 1), (last, 0))):
-        ids = ref[PART_IDS + n * N_COLS : PART_IDS + (n + 1) * N_COLS, :]
-        found = jnp.where(
-            place == (row ^ source), jnp.broadcast_to(ids[:, None, :], (N_COLS, 8, LANES)), found
-        )
+    x = lax.axis_index("cols_1")
+    group = N_COLS // 2
+    for step, out_ref in enumerate((mine, *to_x)):
+        out_ref[0:PART_IDS, :] = parts
+        goal = (x + step) % N_X * N_X
+        for source, (ref, n) in enumerate(((first, 0), (first, 1), (middle, 0), (last, 0))):
+            at = PART_IDS + n * N_COLS
+            ids = jnp.concatenate(
+                [ref[pl.ds(at + goal, N_X), :], ref[pl.ds(at + group + goal, N_X), :]], axis=0
+            )
+            out_ref[pl.ds(PART_IDS + (row ^ source) * N_PEERS, N_PEERS), :] = ids
+
+
+def collect_kernel(mine, *rest):
+    out_ref = rest[-1]
+    held = (mine, *rest[:-2])
+    sums = [ref[0:PART_POS, :] for ref in held]
+    highest = sums[0]
+    for value in sums[1:]:
+        highest = jnp.maximum(highest, value)
+    total = sum(jnp.exp2(value - highest) for value in sums)
+    positive = sum(ref[PART_POS:PART_IDS, :] for ref in held)
+    parts = jnp.concatenate([highest + jnp.log(total) * LOG2E, positive], axis=0)
+    out_ref[:, 0:PART_IDS, :] = jnp.broadcast_to(parts[None], (N_PEERS, PART_IDS, LANES))
+
+    x = lax.axis_index("cols_1")
+    place = lax.broadcasted_iota(I32, (N_PEERS, 8, LANES), 1)
+    found = jnp.zeros((N_PEERS, 8, LANES), F32)
+    for step, ref in enumerate(held):
+        source = (x + N_X - step) % N_X // 2 * N_ROWS
+        for r in range(N_ROWS):
+            ids = ref[PART_IDS + r * N_PEERS : PART_IDS + (r + 1) * N_PEERS, :]
+            wide = jnp.broadcast_to(ids[:, None, :], (N_PEERS, 8, LANES))
+            found = found + jnp.where(place == source + r, wide, 0.0)
     out_ref[:, PART_IDS:PART_ROWS, :] = found
 
 
-def scored(kernel, n_blocks, out_shape, scratch, args, name):
+def collect(held):
+    return pl.pallas_call(
+        collect_kernel,
+        in_specs=[VMEM_SPEC] * len(held),
+        out_specs=VMEM_SPEC,
+        out_shape=pltpu.VMEM((N_PEERS, PART_ROWS, LANES), F32),
+        compiler_params=pltpu.CompilerParams(vmem_limit_bytes=8 << 20),
+        name="collect",
+    )(*[near_core(a) for a in held])
+
+
+def scored(kernel, n_blocks, out_shapes, scratch, args, name):
     columns = [pltpu.VMEM((n_blocks * ITEMS, LANES), F32)] * 2
     return pl.pallas_call(
         kernel,
         in_specs=[VMEM_SPEC] * len(args),
-        out_specs=VMEM_SPEC,
-        out_shape=pltpu.VMEM(out_shape, F32),
+        out_specs=[VMEM_SPEC] * len(out_shapes),
+        out_shape=[pltpu.VMEM(shape, F32) for shape in out_shapes],
         scratch_shapes=scratch + columns,
         cost_estimate=pl.CostEstimate(
             flops=2 * QDEV * n_blocks * ITEMS * EMB,
@@ -388,10 +430,13 @@
     summed = jnp.sum(jnp.exp2(part - highest[None]), axis=0)
     hit = jnp.sum(parts_ref[:, PART_POS:PART_IDS, :], axis=0)
     loss_ref[...] = jnp.log(summed) + (highest - hit) * LN2
-    for a in range(N_COLS // 8):
-        found = jnp.sum(parts_ref[a * 8 : (a + 1) * 8, PART_IDS:PART_ROWS, :], axis=0).astype(I32)
-        for r in range(N_ROWS):
-            ids_ref[r * (N_COLS // 8) + a : r * (N_COLS // 8) + a + 1, :] = found[r : r + 1, :]
+    half = N_PEERS // 2
+    for y in range(2):
+        found = jnp.sum(parts_ref[y * half : (y + 1) * half, PART_IDS:PART_ROWS, :], axis=0)
+        for h in range(2):
+            for r in range(N_ROWS):
+                at = r * (N_COLS // 8) + y * 2 + h
+                ids_ref[at : at + 1, :] = found[h * N_ROWS + r : h * N_ROWS + r + 1, :].astype(I32)
     copy.wait()
 
 
@@ -428,20 +473,26 @@
     sibling = lax.ppermute(own, "rows_1", SWAP)
     one = (PART_IDS + N_COLS, LANES)
     two = (PART_IDS + 2 * N_COLS, LANES)
-    first = scored(first_kernel, 1, one, [], (queries, pos, own), "score_first")
+    (first,) = scored(first_kernel, 2, [two], [], (queries, pos, own, sibling), "score_first")
     send, _ = lax.optimization_barrier((send, first))
     pool_emb = lax.all_to_all(send, ROWS_COLS, split_axis=0, concat_axis=0, tiled=True)
     far = lax.ppermute(across, "rows_1", SWAP)
-    middle = scored(next_kernel, 2, two, [], (queries, pos, sibling, across), "score_next")
-    parts = scored(
+    (middle,) = scored(next_kernel, 1, [one], [], (queries, pos, across, first), "score_next")
+    mine, *to_x = scored(
         last_kernel,
         1,
-        (N_COLS, PART_ROWS, LANES),
+        [(X_ROWS, LANES)] * N_X,
         [pltpu.VMEM(one, F32)],
         (queries, pos, far, first, middle),
         "score_last",
     )
-    parts = lax.all_to_all(parts, COLS, split_axis=0, concat_axis=0, tiled=True)
+    held = [mine] + [
+        lax.ppermute(part, "cols_1", [(x, (x + step) % N_X) for x in range(N_X)])
+        for step, part in enumerate(to_x, 1)
+    ]
+    parts = lax.all_to_all(
+        collect(held + [pool_emb]), ("cols_0", "cols_2"), split_axis=0, concat_axis=0, tiled=True
+    )
     loss, ids, pool_emb = merge(parts, pool_emb)
     return (pool_emb, ids.reshape(-1), loss.reshape(-1))
 

time: 80.8 us -> 70.6 us (0.87)
  Pallas kernels: 44.8 us -> 36.2 us
  blocking collectives: 20.7 us -> 12.2 us
  starting transfers between devices: 12.9 us -> 18.6 us
  waiting for transfers between devices: 1.49 us -> 2.46 us
    all_to_all x1, blocking collectives: 20.7 us -> 12.2 us  [local(): lax.all_to_all(collect(held + [pool_emb]), ('cols_0', 'cols_2'), split_ax...]
    pallas_call x3 -> x4, Pallas kernels: 33.5 us -> 25.2 us  [the longest x3 25.1 us: scored(): pl.pallas_call(kernel, in_specs=[VMEM_SPEC] * len(args), out_specs=[VMEM_...]
    ppermute x0 -> x3, starting transfers between devices: none -> 5.26 us  [local(): lax.ppermute(part, 'cols_1', [(x, (x + step) % N_X) for x in range(N_X)])]
    ppermute x0 -> x3, waiting for transfers between devices: none -> 2.45 us  [local(): lax.ppermute(part, 'cols_1', [(x, (x + step) % N_X) for x in range(N_X)])]
    ppermute x1, waiting for transfers between devices: 1.48 us -> 0.01 us  [local(): sibling = lax.ppermute(own, 'rows_1', SWAP)]
    all_to_all x1, starting transfers between devices: 8.93 us -> 9.76 us  [local(): lax.all_to_all(send, ROWS_COLS, split_axis=0, concat_axis=0, tiled=True)]
  transfers between devices with their start and end apart: 4 -> 7, of which waited for: 1 -> 2; matrix products, arithmetic and copies ran while one was open for 0% -> 0% of each run, Pallas kernels for 42% -> 36%
where the time goes in v4:
time: 70.6 us; the launch traced here: 70.4 us
  Pallas kernels  36.2 us (51%)
  starting transfers between devices  18.6 us (26%)
  blocking collectives  12.2 us (17%)
  waiting for transfers between devices  2.46 us (3%)
  between operations  0.88 us (1%)
    pallas_call x3, Pallas kernels, scored(): pl.pallas_call(kernel, in_specs=[VMEM_SPEC] * len(args), out_specs=[VMEM_...  25.1 us
    all_to_all x1, blocking collectives, local(): lax.all_to_all(collect(held + [pool_emb]), ('cols_0', 'cols_2'), split_ax...  12.2 us
    all_to_all x1, starting transfers between devices, local(): lax.all_to_all(send, ROWS_COLS, split_axis=0, concat_axis=0, tiled=True)  9.76 us
    pallas_call x1, Pallas kernels, tower(): pl.pallas_call(tower_kernel, in_specs=[ANY_SPEC] * 6, out_specs=[VMEM_SPE...  9.44 us
    ppermute x3, starting transfers between devices, local(): lax.ppermute(part, 'cols_1', [(x, (x + step) % N_X) for x in range(N_X)])  5.26 us
    ppermute x1, starting transfers between devices, local(): across = lax.ppermute(own, 'rows_0', SWAP)  3.39 us
    ppermute x3, waiting for transfers between devices, local(): lax.ppermute(part, 'cols_1', [(x, (x + step) % N_X) for x in range(N_X)])  2.45 us
    pallas_call x1, Pallas kernels, merge(): pl.pallas_call(merge_kernel, in_specs=[VMEM_SPEC, VMEM_SPEC], out_specs=[...  1.58 us
  transfers between devices with their start and end apart: 7, of which 2 were waited for; matrix products, arithmetic and copies ran while one was open for 0% of the time, Pallas kernels for 36%

profile of v4, /device:TPU:0, one launch (start us, length us, event | category | flops | bytes accessed | tf_op | source)
XLA Modules:
  0.0 70.4 jit_solution(4071165359680989994)
XLA Ops:
  0.6 0.0 copy-start
  0.6 0.0 copy-start.1
  0.7 9.4 %tower.1 = (bf16[1136,256]{1,0:T(8,128)(2,1)S(1)}, bf16[2048,256]{1,0:T(8,128)(2,1)}) custom-call(bf16[1024,2048]{1,0:T(8,128)(2,1)} %feat_hbm.1, bf16[2048,1024]{1,0:T(8,128)(2,1)} %w_in_hbm.1, bf16[1024,256]{1,0:T(8,128)(2,1)} %w_out_hbm.1, s32[8,128]{1,0:T(8,128)} %bitcast.15, s32[8,128]{1,0:T(8,128)} %bitcast.16, s32[8,128]{1,0:T(8,128)} %bitcast.17), custom_call_target="tpu_custom_call" | custom-call | flops 4831838208 | bytes 8388608 | tf_op jit(solution)/shard_map/tower/pallas_call | solution.py:173
  10.1 0.1 collective-permute-start.2
  10.2 3.4 %collective-permute-start = (bf16[1136,256]{1,0:T(8,128)(2,1)S(1)}, bf16[1136,256]{1,0:T(8,128)(2,1)S(1)}, u32[]{:S(2)}, u32[]{:S(2)}) collective-permute-start(bf16[1136,256]{1,0:T(8,128)(2,1)S(1)} %get-tuple-element.13.own), channel_id=1, source_target_pairs={{0,64},{64,0},{1,65},{65,1},{2,66},{66,2},{3,67},{67,3},{4,68},{68... | collective-permute-start | bytes 1744904 | tf_op jit(solution)/shard_map/ppermute | solution.py:472
  13.6 0.0 collective-permute-done.2.sibling
  13.6 0.0 copy-done
  13.6 0.0 copy-done.1
  13.6 12.0 %score_first.1.first = f32[96,128]{1,0:T(8,128)S(1)} custom-call(bf16[2048,256]{1,0:T(8,128)(2,1)S(1)} %copy-done, s32[64,128]{1,0:T(8,128)S(1)} %bitcast.10, bf16[1136,256]{1,0:T(8,128)(2,1)S(1)} %get-tuple-element.13.own, bf16[1136,256]{1,0:T(8,128)(2,1)S(1)} %collective-permute-done.2.sibling), custom_call_target="tpu_custom_call" | custom-call | flops 2147483648 | bytes 1048576 | tf_op jit(solution)/shard_map/score_first/pallas_call | solution.py:409
  25.6 9.8 %all-to-all-start = ((bf16[128,16,256]{2,1,0:T(8,128)(2,1)}), bf16[128,16,256]{2,1,0:T(8,128)(2,1)S(1)}, u32[]{:S(2)}, u32[]{:S(2)}) async-start(bf16[128,16,256]{2,1,0:T(8,128)(2,1)} %bitcast.4), calls=%async_computation | async-start | bytes 2097152 | tf_op jit(solution)/shard_map/all_to_all | solution.py:478
  35.4 0.0 collective-permute-done.across
  35.4 0.1 collective-permute-start.1
  35.5 6.6 %score_next.1.middle = f32[64,128]{1,0:T(8,128)S(1)} custom-call(bf16[2048,256]{1,0:T(8,128)(2,1)S(1)} %copy-done, s32[64,128]{1,0:T(8,128)S(1)} %bitcast.11, bf16[1136,256]{1,0:T(8,128)(2,1)S(1)} %collective-permute-done.across, f32[96,128]{1,0:T(8,128)S(1)} %score_first.1.first), custom_call_target="tpu_custom_call" | custom-call | flops 1073741824 | bytes 524288 | tf_op jit(solution)/shard_map/score_next/pallas_call | solution.py:409
  42.1 0.0 collective-permute-done.1.far
  42.1 6.5 %score_last.1 = (f32[64,128]{1,0:T(8,128)S(1)}, f32[64,128]{1,0:T(8,128)S(1)}, f32[64,128]{1,0:T(8,128)S(1)}, f32[64,128]{1,0:T(8,128)S(1)}) custom-call(bf16[2048,256]{1,0:T(8,128)(2,1)S(1)} %copy-done, s32[64,128]{1,0:T(8,128)S(1)} %bitcast.12, bf16[1136,256]{1,0:T(8,128)(2,1)S(1)} %collective-permute-done.1.far, f32[96,128]{1,0:T(8,128)S(1)} %score_first.1.first, ...), custom_call_target="tpu_custom_call" | custom-call | flops 1073741824 | bytes 524288 | tf_op jit(solution)/shard_map/score_last/pallas_call | solution.py:409
  48.6 1.1 %collective-permute-start.3 = (f32[64,128]{1,0:T(8,128)S(1)}, f32[64,128]{1,0:T(8,128)S(1)}, u32[]{:S(2)}, u32[]{:S(2)}) collective-permute-start(f32[64,128]{1,0:T(8,128)S(1)} %get-tuple-element.15), channel_id=1, source_target_pairs={{0,4},{4,8},{8,12},{12,0},{1,5},{5,9},{9,13},{13,1},{2,6},{6,10},{... | collective-permute-start | bytes 98312 | tf_op jit(solution)/shard_map/ppermute | solution.py:490
  49.7 2.7 %collective-permute-start.4 = (f32[64,128]{1,0:T(8,128)S(1)}, f32[64,128]{1,0:T(8,128)S(1)}, u32[]{:S(2)}, u32[]{:S(2)}) collective-permute-start(f32[64,128]{1,0:T(8,128)S(1)} %get-tuple-element.16), channel_id=1, source_target_pairs={{0,8},{4,12},{8,0},{12,4},{1,9},{5,13},{9,1},{13,5},{2,10},{6,14},... | collective-permute-start | bytes 98312 | tf_op jit(solution)/shard_map/ppermute | solution.py:490
  52.4 1.5 %collective-permute-start.5 = (f32[64,128]{1,0:T(8,128)S(1)}, f32[64,128]{1,0:T(8,128)S(1)}, u32[]{:S(2)}, u32[]{:S(2)}) collective-permute-start(f32[64,128]{1,0:T(8,128)S(1)} %get-tuple-element.17), channel_id=1, source_target_pairs={{0,12},{4,0},{8,4},{12,8},{1,13},{5,1},{9,5},{13,9},{2,14},{6,2},{... | collective-permute-start | bytes 98312 | tf_op jit(solution)/shard_map/ppermute | solution.py:490
  53.9 0.0 collective-permute-done.3.rest_0_
  53.9 1.3 %collective-permute-done.4.rest_1_ = f32[64,128]{1,0:T(8,128)S(1)} collective-permute-done((f32[64,128]{1,0:T(8,128)S(1)}, f32[64,128]{1,0:T(8,128)S(1)}, u32[]{:S(2)}, u32[]{:S(2)}) %collective-permute-start.4) | collective-permute-done | bytes 32800 | tf_op jit(solution)/shard_map/ppermute | solution.py:490
  55.1 1.2 %collective-permute-done.5.rest_2_ = f32[64,128]{1,0:T(8,128)S(1)} collective-permute-done((f32[64,128]{1,0:T(8,128)S(1)}, f32[64,128]{1,0:T(8,128)S(1)}, u32[]{:S(2)}, u32[]{:S(2)}) %collective-permute-start.5) | collective-permute-done | bytes 32800 | tf_op jit(solution)/shard_map/ppermute | solution.py:490
  56.3 0.0 all-to-all-done
  56.3 0.1 collect.1
  56.4 12.2 %all_to_all.16.parts_ref = f32[8,40,128]{2,1,0:T(8,128)S(1)} all-to-all(f32[8,40,128]{2,1,0:T(8,128)S(1)} %collect.1), channel_id=1, replica_groups=mesh['rows_0'=2,'rows_1'=2,'cols_0'=2,'cols_1'=4,'cols_2'=4] {'cols_0','..., dimensions={0} | all-to-all | bytes 327680 | tf_op jit(solution)/shard_map/all_to_all | solution.py:493
  68.6 1.6 %merge.1 = (f32[16,128]{1,0:T(8,128)}, s32[16,128]{1,0:T(8,128)}, bf16[2048,256]{1,0:T(8,128)(2,1)}) custom-call(f32[8,40,128]{2,1,0:T(8,128)S(1)} %all_to_all.16.parts_ref, bf16[2048,256]{1,0:T(8,128)(2,1)S(1)} %bitcast.9), custom_call_target="tpu_custom_call" | custom-call | tf_op jit(solution)/shard_map/merge/pallas_call | solution.py:444
Async XLA Ops:
  0.6 12.9 %copy-start = (bf16[2048,256]{1,0:T(8,128)(2,1)S(1)}, bf16[2048,256]{1,0:T(8,128)(2,1)}, u32[]{:S(2)}) copy-start(bf16[2048,256]{1,0:T(8,128)(2,1)} %q_ref.5) | copy-start | bytes 3145732
  0.6 12.9 %copy-start.1 = (s32[8192]{0:T(1024)S(1)}, s32[8192]{0:T(1024)}, u32[]{:S(2)}) copy-start(s32[8192]{0:T(1024)} %param.15) | copy-start | bytes 98308
  10.1 3.5 %collective-permute-start.2 = (bf16[1136,256]{1,0:T(8,128)(2,1)S(1)}, bf16[1136,256]{1,0:T(8,128)(2,1)S(1)}, u32[]{:S(2)}, u32[]{:S(2)}) collective-permute-start(bf16[1136,256]{1,0:T(8,128)(2,1)S(1)} %get-tuple-element.13.own), channel_id=1, source_target_pairs={{0,32},{32,0},{1,33},{33,1},{2,34},{34,2},{3,35},{35,3},{4,36},{36... | collective-permute-start | bytes 1744904 | tf_op jit(solution)/shard_map/ppermute | solution.py:473
  10.2 25.2 %collective-permute-start = (bf16[1136,256]{1,0:T(8,128)(2,1)S(1)}, bf16[1136,256]{1,0:T(8,128)(2,1)S(1)}, u32[]{:S(2)}, u32[]{:S(2)}) collective-permute-start(bf16[1136,256]{1,0:T(8,128)(2,1)S(1)} %get-tuple-element.13.own), channel_id=1, source_target_pairs={{0,64},{64,0},{1,65},{65,1},{2,66},{66,2},{3,67},{67,3},{4,68},{68... | collective-permute-start | bytes 1744904 | tf_op jit(solution)/shard_map/ppermute | solution.py:472
  25.6 30.7 %all-to-all-start = ((bf16[128,16,256]{2,1,0:T(8,128)(2,1)}), bf16[128,16,256]{2,1,0:T(8,128)(2,1)S(1)}, u32[]{:S(2)}, u32[]{:S(2)}) async-start(bf16[128,16,256]{2,1,0:T(8,128)(2,1)} %bitcast.4), calls=%async_computation | async-start | bytes 2097152 | tf_op jit(solution)/shard_map/all_to_all | solution.py:478
  35.4 6.7 %collective-permute-start.1 = (bf16[1136,256]{1,0:T(8,128)(2,1)S(1)}, bf16[1136,256]{1,0:T(8,128)(2,1)S(1)}, u32[]{:S(2)}, u32[]{:S(2)}) collective-permute-start(bf16[1136,256]{1,0:T(8,128)(2,1)S(1)} %collective-permute-done.across), channel_id=1, source_target_pairs={{0,32},{32,0},{1,33},{33,1},{2,34},{34,2},{3,35},{35,3},{4,36},{36... | collective-permute-start | bytes 1744904 | tf_op jit(solution)/shard_map/ppermute | solution.py:479
  48.6 5.3 %collective-permute-start.3 = (f32[64,128]{1,0:T(8,128)S(1)}, f32[64,128]{1,0:T(8,128)S(1)}, u32[]{:S(2)}, u32[]{:S(2)}) collective-permute-start(f32[64,128]{1,0:T(8,128)S(1)} %get-tuple-element.15), channel_id=1, source_target_pairs={{0,4},{4,8},{8,12},{12,0},{1,5},{5,9},{9,13},{13,1},{2,6},{6,10},{... | collective-permute-start | bytes 98312 | tf_op jit(solution)/shard_map/ppermute | solution.py:490
  49.7 5.4 %collective-permute-start.4 = (f32[64,128]{1,0:T(8,128)S(1)}, f32[64,128]{1,0:T(8,128)S(1)}, u32[]{:S(2)}, u32[]{:S(2)}) collective-permute-start(f32[64,128]{1,0:T(8,128)S(1)} %get-tuple-element.16), channel_id=1, source_target_pairs={{0,8},{4,12},{8,0},{12,4},{1,9},{5,13},{9,1},{13,5},{2,10},{6,14},... | collective-permute-start | bytes 98312 | tf_op jit(solution)/shard_map/ppermute | solution.py:490
  52.4 3.9 %collective-permute-start.5 = (f32[64,128]{1,0:T(8,128)S(1)}, f32[64,128]{1,0:T(8,128)S(1)}, u32[]{:S(2)}, u32[]{:S(2)}) collective-permute-start(f32[64,128]{1,0:T(8,128)S(1)} %get-tuple-element.17), channel_id=1, source_target_pairs={{0,12},{4,0},{8,4},{12,8},{1,13},{5,1},{9,5},{13,9},{2,14},{6,2},{... | collective-permute-start | bytes 98312 | tf_op jit(solution)/shard_map/ppermute | solution.py:490

commit v5 on v4

--- a/solution.py
+++ b/solution.py
@@ -55,8 +55,8 @@
 
 def tower_kernel(
     feat_hbm, w_in_hbm, w_out_hbm, owners_hbm, ids_hbm, counts_hbm,
-    ext_ref, send_ref,
-    feat, w_in, w_out, acc, owners_ref, ids_ref, counts_ref, slots,
+    ext_ref, slots,
+    feat, w_in, w_out, acc, owners_ref, ids_ref, counts_ref,
     feat_sem, w_in_sem, w_out_sem, small_sem,
 ):
     small = [
@@ -147,15 +147,6 @@
                     hidden, w_out[...], preferred_element_type=F32
                 ).astype(BF16)
 
-    chunk = 512
-    slot_row = jnp.concatenate([slots[j : j + 1, :] for j in range(BLOCKS)], axis=1)
-    for c in range(N_DEV * CAP // chunk):
-        place = lax.broadcasted_iota(I32, (chunk, ITEMS), 0) + c * chunk
-        chosen = (place == slot_row).astype(F32).astype(BF16)
-        send_ref[c * chunk : (c + 1) * chunk, :] = jnp.dot(
-            chosen, ext_ref[0:ITEMS, :], preferred_element_type=F32
-        ).astype(BF16)
-
 
 VMEM_SPEC = pl.BlockSpec(memory_space=pltpu.VMEM)
 ANY_SPEC = pl.BlockSpec(memory_space=pl.ANY)
@@ -176,14 +167,13 @@
         out_specs=[VMEM_SPEC, VMEM_SPEC],
         out_shape=[
             pltpu.VMEM((EXT_ROWS, EMB), BF16),
-            pltpu.VMEM((N_DEV * CAP, EMB), BF16),
+            pltpu.VMEM((BLOCKS, LANES), I32),
         ],
         scratch_shapes=[
             pltpu.VMEM((ITEMS, F_IN), BF16),
             pltpu.VMEM((F_IN, HID), BF16),
             pltpu.VMEM((HID, EMB), BF16),
             pltpu.VMEM((ITEMS, HID), F32),
-            pltpu.VMEM((BLOCKS, LANES), I32),
             pltpu.VMEM((BLOCKS, LANES), I32),
             pltpu.VMEM((BLOCKS, LANES), I32),
             pltpu.VMEM((BLOCKS, LANES), I32),
@@ -336,8 +326,27 @@
     score_tiles(q_ref, pos_all, row, (0, Q_STEPS), exts, col_ids, col_logq, out_ref)
 
 
-def first_kernel(q_ref, pos_all, own, sibling, out_ref, col_ids, col_logq):
+SEND_CHUNK = 512
+SEND_STEPS = N_DEV * CAP // SEND_CHUNK
+
+
+def first_kernel(
+    q_ref, pos_all, own, sibling, slots, out_ref, send_hbm, send, sems, col_ids, col_logq
+):
+    slot_row = jnp.concatenate([slots[j : j + 1, :] for j in range(BLOCKS)], axis=1)
+    copies = []
+    for c in range(SEND_STEPS):
+        place = lax.broadcasted_iota(I32, (SEND_CHUNK, ITEMS), 0) + c * SEND_CHUNK
+        chosen = (place == slot_row).astype(F32).astype(BF16)
+        at = pl.ds(c * SEND_CHUNK, SEND_CHUNK)
+        send[at, :] = jnp.dot(
+            chosen, own[0:ITEMS, :], preferred_element_type=F32
+        ).astype(BF16)
+        copies.append(pltpu.make_async_copy(send.at[at], send_hbm.at[at], sems.at[c]))
+        copies[c].start()
     score_and_list(q_ref, pos_all, (own, sibling), out_ref, col_ids, col_logq)
+    for copy in copies:
+        copy.wait()
 
 
 def next_kernel(q_ref, pos_all, across, first, out_ref, col_ids, col_logq):
@@ -393,24 +402,24 @@
     out_ref[:, PART_IDS:PART_ROWS, :] = found
 
 
-def collect(held):
+def collect(held, pool):
     return pl.pallas_call(
         collect_kernel,
-        in_specs=[VMEM_SPEC] * len(held),
+        in_specs=[VMEM_SPEC] * (len(held) + 1),
         out_specs=VMEM_SPEC,
         out_shape=pltpu.VMEM((N_PEERS, PART_ROWS, LANES), F32),
         compiler_params=pltpu.CompilerParams(vmem_limit_bytes=8 << 20),
         name="collect",
-    )(*[near_core(a) for a in held])
-
-
-def scored(kernel, n_blocks, out_shapes, scratch, args, name):
+    )(*[near_core(a) for a in held], near_core(pool))
+
+
+def scored(kernel, n_blocks, out_shapes, scratch, args, name, in_hbm_too=()):
     columns = [pltpu.VMEM((n_blocks * ITEMS, LANES), F32)] * 2
     return pl.pallas_call(
         kernel,
         in_specs=[VMEM_SPEC] * len(args),
-        out_specs=[VMEM_SPEC] * len(out_shapes),
-        out_shape=[pltpu.VMEM(shape, F32) for shape in out_shapes],
+        out_specs=[VMEM_SPEC] * len(out_shapes) + [ANY_SPEC] * len(in_hbm_too),
+        out_shape=[pltpu.VMEM(shape, F32) for shape in out_shapes] + list(in_hbm_too),
         scratch_shapes=scratch + columns,
         cost_estimate=pl.CostEstimate(
             flops=2 * QDEV * n_blocks * ITEMS * EMB,
@@ -422,9 +431,16 @@
     )(*[near_core(a) for a in args])
 
 
-def merge_kernel(parts_ref, pool_in, loss_ref, ids_ref, pool_out, sem):
-    copy = pltpu.make_async_copy(pool_in, pool_out, sem)
-    copy.start()
+POOL_STEPS = 8
+
+
+def merge_kernel(parts_ref, pool_in, loss_ref, ids_ref, pool_out, sems):
+    rows = N_DEV * CAP // POOL_STEPS
+    copies = []
+    for k in range(POOL_STEPS):
+        at = pl.ds(k * rows, rows)
+        copies.append(pltpu.make_async_copy(pool_in.at[at], pool_out.at[at], sems.at[k]))
+        copies[k].start()
     part = parts_ref[:, 0:PART_POS, :]
     highest = jnp.max(part, axis=0)
     summed = jnp.sum(jnp.exp2(part - highest[None]), axis=0)
@@ -437,7 +453,8 @@
             for r in range(N_ROWS):
                 at = r * (N_COLS // 8) + y * 2 + h
                 ids_ref[at : at + 1, :] = found[h * N_ROWS + r : h * N_ROWS + r + 1, :].astype(I32)
-    copy.wait()
+    for copy in copies:
+        copy.wait()
 
 
 def merge(parts, pool):
@@ -450,7 +467,7 @@
             jax.ShapeDtypeStruct((N_DEV * CAP // LANES, LANES), I32),
             pltpu.HBM(pool.shape, pool.dtype),
         ],
-        scratch_shapes=[pltpu.SemaphoreType.DMA],
+        scratch_shapes=[pltpu.SemaphoreType.DMA((POOL_STEPS,))],
         compiler_params=pltpu.CompilerParams(vmem_limit_bytes=8 << 20),
         name="merge",
     )(near_core(parts), near_core(pool))
@@ -461,7 +478,7 @@
 
 def local(features, w_in, w_out, item_ids, item_counts, owners, queries, positives):
     pos = positives.reshape(-1, LANES)
-    own, send = tower(
+    own, slots = tower(
         features,
         w_in,
         w_out,
@@ -473,8 +490,16 @@
     sibling = lax.ppermute(own, "rows_1", SWAP)
     one = (PART_IDS + N_COLS, LANES)
     two = (PART_IDS + 2 * N_COLS, LANES)
-    (first,) = scored(first_kernel, 2, [two], [], (queries, pos, own, sibling), "score_first")
-    send, _ = lax.optimization_barrier((send, first))
+    sent = pltpu.HBM((N_DEV * CAP, EMB), BF16)
+    first, send = scored(
+        first_kernel,
+        2,
+        [two],
+        [pltpu.VMEM((N_DEV * CAP, EMB), BF16), pltpu.SemaphoreType.DMA((SEND_STEPS,))],
+        (queries, pos, own, sibling, slots),
+        "score_first",
+        [sent],
+    )
     pool_emb = lax.all_to_all(send, ROWS_COLS, split_axis=0, concat_axis=0, tiled=True)
     far = lax.ppermute(across, "rows_1", SWAP)
     (middle,) = scored(next_kernel, 1, [one], [], (queries, pos, across, first), "score_next")
@@ -491,7 +516,7 @@
         for step, part in enumerate(to_x, 1)
     ]
     parts = lax.all_to_all(
-        collect(held + [pool_emb]), ("cols_0", "cols_2"), split_axis=0, concat_axis=0, tiled=True
+        collect(held, pool_emb), ("cols_0", "cols_2"), split_axis=0, concat_axis=0, tiled=True
     )
     loss, ids, pool_emb = merge(parts, pool_emb)
     return (pool_emb, ids.reshape(-1), loss.reshape(-1))

time: 70.6 us -> 69.6 us (0.986)
  Pallas kernels: 36.2 us -> 35.2 us
    pallas_call x1, Pallas kernels: 9.44 us -> 7.38 us  [tower(): pl.pallas_call(tower_kernel, in_specs=[ANY_SPEC] * 6, out_specs=[VMEM_SPE...]
    pallas_call x3, Pallas kernels: 25.1 us -> 26.1 us  [scored(): pl.pallas_call(kernel, in_specs=[VMEM_SPEC] * len(args), out_specs=[VMEM_...]
  transfers between devices with their start and end apart: 7 -> 7, of which waited for: 2 -> 2; matrix products, arithmetic and copies ran while one was open for 0% -> 0% of each run, Pallas kernels for 36% -> 38%
where the time goes in v5:
time: 69.6 us; the launch traced here: 69.4 us
  Pallas kernels  35.2 us (51%)
  starting transfers between devices  18.6 us (27%)
  blocking collectives  12.2 us (18%)
  waiting for transfers between devices  2.46 us (4%)
  between operations  0.88 us (1%)
    pallas_call x3, Pallas kernels, scored(): pl.pallas_call(kernel, in_specs=[VMEM_SPEC] * len(args), out_specs=[VMEM_...  26.1 us
    all_to_all x1, blocking collectives, local(): lax.all_to_all(collect(held, pool_emb), ('cols_0', 'cols_2'), split_axis=...  12.2 us
    all_to_all x1, starting transfers between devices, local(): lax.all_to_all(send, ROWS_COLS, split_axis=0, concat_axis=0, tiled=True)  9.77 us
    pallas_call x1, Pallas kernels, tower(): pl.pallas_call(tower_kernel, in_specs=[ANY_SPEC] * 6, out_specs=[VMEM_SPE...  7.38 us
    ppermute x3, starting transfers between devices, local(): lax.ppermute(part, 'cols_1', [(x, (x + step) % N_X) for x in range(N_X)])  5.26 us
    ppermute x1, starting transfers between devices, local(): across = lax.ppermute(own, 'rows_0', SWAP)  3.39 us
    ppermute x3, waiting for transfers between devices, local(): lax.ppermute(part, 'cols_1', [(x, (x + step) % N_X) for x in range(N_X)])  2.45 us
    pallas_call x1, Pallas kernels, merge(): pl.pallas_call(merge_kernel, in_specs=[VMEM_SPEC, VMEM_SPEC], out_specs=[...  1.63 us
  transfers between devices with their start and end apart: 7, of which 2 were waited for; matrix products, arithmetic and copies ran while one was open for 0% of the time, Pallas kernels for 38%

profile of v5, /device:TPU:0, one launch (start us, length us, event | category | flops | bytes accessed | tf_op | source)
XLA Modules:
  0.0 69.4 jit_solution(5934659186185642385)
XLA Ops:
  0.6 0.0 copy-start
  0.6 0.0 copy-start.1
  0.7 7.4 %tower.1 = (bf16[1136,256]{1,0:T(8,128)(2,1)S(1)}, s32[8,128]{1,0:T(8,128)S(1)}) custom-call(bf16[1024,2048]{1,0:T(8,128)(2,1)} %feat_hbm.1, bf16[2048,1024]{1,0:T(8,128)(2,1)} %w_in_hbm.1, bf16[1024,256]{1,0:T(8,128)(2,1)} %w_out_hbm.1, s32[8,128]{1,0:T(8,128)} %bitcast.16, s32[8,128]{1,0:T(8,128)} %bitcast.17, s32[8,128]{1,0:T(8,128)} %bitcast.18), custom_call_target="tpu_custom_call" | custom-call | flops 4831838208 | bytes 8388608 | tf_op jit(solution)/shard_map/tower/pallas_call | solution.py:164
  8.0 0.1 collective-permute-start.2
  8.1 3.4 %collective-permute-start = (bf16[1136,256]{1,0:T(8,128)(2,1)S(1)}, bf16[1136,256]{1,0:T(8,128)(2,1)S(1)}, u32[]{:S(2)}, u32[]{:S(2)}) collective-permute-start(bf16[1136,256]{1,0:T(8,128)(2,1)S(1)} %get-tuple-element.14.own), channel_id=1, source_target_pairs={{0,64},{64,0},{1,65},{65,1},{2,66},{66,2},{3,67},{67,3},{4,68},{68... | collective-permute-start | bytes 1744904 | tf_op jit(solution)/shard_map/ppermute | solution.py:489
  11.5 0.0 collective-permute-done.2.sibling
  11.5 0.0 copy-done
  11.5 0.0 copy-done.1
  11.5 13.0 %score_first.1 = (f32[96,128]{1,0:T(8,128)S(1)}, bf16[2048,256]{1,0:T(8,128)(2,1)}) custom-call(bf16[2048,256]{1,0:T(8,128)(2,1)S(1)} %copy-done, s32[64,128]{1,0:T(8,128)S(1)} %bitcast.10, bf16[1136,256]{1,0:T(8,128)(2,1)S(1)} %get-tuple-element.14.own, bf16[1136,256]{1,0:T(8,128)(2,1)S(1)} %collective-permute-done.2.sibling, ...), custom_call_target="tpu_custom_call" | custom-call | flops 2147483648 | bytes 1048576 | tf_op jit(solution)/shard_map/score_first/pallas_call | solution.py:418
  24.5 9.8 %all-to-all-start = ((bf16[128,16,256]{2,1,0:T(8,128)(2,1)}), bf16[128,16,256]{2,1,0:T(8,128)(2,1)S(1)}, u32[]{:S(2)}, u32[]{:S(2)}) async-start(bf16[128,16,256]{2,1,0:T(8,128)(2,1)} %bitcast.13), calls=%async_computation | async-start | bytes 2097152 | tf_op jit(solution)/shard_map/all_to_all | solution.py:503
  34.3 0.0 collective-permute-done.across
  34.3 0.1 collective-permute-start.1
  34.4 6.5 %score_next.1.middle = f32[64,128]{1,0:T(8,128)S(1)} custom-call(bf16[2048,256]{1,0:T(8,128)(2,1)S(1)} %copy-done, s32[64,128]{1,0:T(8,128)S(1)} %bitcast.11, bf16[1136,256]{1,0:T(8,128)(2,1)S(1)} %collective-permute-done.across, f32[96,128]{1,0:T(8,128)S(1)} %get-tuple-element.16.first), custom_call_target="tpu_custom_call" | custom-call | flops 1073741824 | bytes 524288 | tf_op jit(solution)/shard_map/score_next/pallas_call | solution.py:418
  40.9 0.0 collective-permute-done.1.far
  40.9 6.6 %score_last.1 = (f32[64,128]{1,0:T(8,128)S(1)}, f32[64,128]{1,0:T(8,128)S(1)}, f32[64,128]{1,0:T(8,128)S(1)}, f32[64,128]{1,0:T(8,128)S(1)}) custom-call(bf16[2048,256]{1,0:T(8,128)(2,1)S(1)} %copy-done, s32[64,128]{1,0:T(8,128)S(1)} %bitcast.12, bf16[1136,256]{1,0:T(8,128)(2,1)S(1)} %collective-permute-done.1.far, f32[96,128]{1,0:T(8,128)S(1)} %get-tuple-element.16.first, ...), custom_call_target="tpu_custom_call" | custom-call | flops 1073741824 | bytes 524288 | tf_op jit(solution)/shard_map/score_last/pallas_call | solution.py:418
  47.5 1.1 %collective-permute-start.3 = (f32[64,128]{1,0:T(8,128)S(1)}, f32[64,128]{1,0:T(8,128)S(1)}, u32[]{:S(2)}, u32[]{:S(2)}) collective-permute-start(f32[64,128]{1,0:T(8,128)S(1)} %get-tuple-element.18), channel_id=1, source_target_pairs={{0,4},{4,8},{8,12},{12,0},{1,5},{5,9},{9,13},{13,1},{2,6},{6,10},{... | collective-permute-start | bytes 98312 | tf_op jit(solution)/shard_map/ppermute | solution.py:515
  48.7 2.7 %collective-permute-start.4 = (f32[64,128]{1,0:T(8,128)S(1)}, f32[64,128]{1,0:T(8,128)S(1)}, u32[]{:S(2)}, u32[]{:S(2)}) collective-permute-start(f32[64,128]{1,0:T(8,128)S(1)} %get-tuple-element.19), channel_id=1, source_target_pairs={{0,8},{4,12},{8,0},{12,4},{1,9},{5,13},{9,1},{13,5},{2,10},{6,14},... | collective-permute-start | bytes 98312 | tf_op jit(solution)/shard_map/ppermute | solution.py:515
  51.3 1.5 %collective-permute-start.5 = (f32[64,128]{1,0:T(8,128)S(1)}, f32[64,128]{1,0:T(8,128)S(1)}, u32[]{:S(2)}, u32[]{:S(2)}) collective-permute-start(f32[64,128]{1,0:T(8,128)S(1)} %get-tuple-element.20), channel_id=1, source_target_pairs={{0,12},{4,0},{8,4},{12,8},{1,13},{5,1},{9,5},{13,9},{2,14},{6,2},{... | collective-permute-start | bytes 98312 | tf_op jit(solution)/shard_map/ppermute | solution.py:515
  52.8 0.0 collective-permute-done.3.rest_0_
  52.8 1.3 %collective-permute-done.4.rest_1_ = f32[64,128]{1,0:T(8,128)S(1)} collective-permute-done((f32[64,128]{1,0:T(8,128)S(1)}, f32[64,128]{1,0:T(8,128)S(1)}, u32[]{:S(2)}, u32[]{:S(2)}) %collective-permute-start.4) | collective-permute-done | bytes 32800 | tf_op jit(solution)/shard_map/ppermute | solution.py:515
  54.1 1.2 %collective-permute-done.5.rest_2_ = f32[64,128]{1,0:T(8,128)S(1)} collective-permute-done((f32[64,128]{1,0:T(8,128)S(1)}, f32[64,128]{1,0:T(8,128)S(1)}, u32[]{:S(2)}, u32[]{:S(2)}) %collective-permute-start.5) | collective-permute-done | bytes 32800 | tf_op jit(solution)/shard_map/ppermute | solution.py:515
  55.3 0.0 all-to-all-done
  55.3 0.1 collect.1
  55.4 12.2 %all_to_all.16.parts_ref = f32[8,40,128]{2,1,0:T(8,128)S(1)} all-to-all(f32[8,40,128]{2,1,0:T(8,128)S(1)} %collect.1), channel_id=1, replica_groups=mesh['rows_0'=2,'rows_1'=2,'cols_0'=2,'cols_1'=4,'cols_2'=4] {'cols_0','..., dimensions={0} | all-to-all | bytes 327680 | tf_op jit(solution)/shard_map/all_to_all | solution.py:518
  67.6 1.6 %merge.1 = (f32[16,128]{1,0:T(8,128)}, s32[16,128]{1,0:T(8,128)}, bf16[2048,256]{1,0:T(8,128)(2,1)}) custom-call(f32[8,40,128]{2,1,0:T(8,128)S(1)} %all_to_all.16.parts_ref, bf16[2048,256]{1,0:T(8,128)(2,1)S(1)} %bitcast.9), custom_call_target="tpu_custom_call" | custom-call | tf_op jit(solution)/shard_map/merge/pallas_call | solution.py:461
Async XLA Ops:
  0.6 10.9 %copy-start = (bf16[2048,256]{1,0:T(8,128)(2,1)S(1)}, bf16[2048,256]{1,0:T(8,128)(2,1)}, u32[]{:S(2)}) copy-start(bf16[2048,256]{1,0:T(8,128)(2,1)} %q_ref.5) | copy-start | bytes 3145732
  0.6 10.9 %copy-start.1 = (s32[8192]{0:T(1024)S(1)}, s32[8192]{0:T(1024)}, u32[]{:S(2)}) copy-start(s32[8192]{0:T(1024)} %param.15) | copy-start | bytes 98308
  8.0 3.5 %collective-permute-start.2 = (bf16[1136,256]{1,0:T(8,128)(2,1)S(1)}, bf16[1136,256]{1,0:T(8,128)(2,1)S(1)}, u32[]{:S(2)}, u32[]{:S(2)}) collective-permute-start(bf16[1136,256]{1,0:T(8,128)(2,1)S(1)} %get-tuple-element.14.own), channel_id=1, source_target_pairs={{0,32},{32,0},{1,33},{33,1},{2,34},{34,2},{3,35},{35,3},{4,36},{36... | collective-permute-start | bytes 1744904 | tf_op jit(solution)/shard_map/ppermute | solution.py:490
  8.1 26.2 %collective-permute-start = (bf16[1136,256]{1,0:T(8,128)(2,1)S(1)}, bf16[1136,256]{1,0:T(8,128)(2,1)S(1)}, u32[]{:S(2)}, u32[]{:S(2)}) collective-permute-start(bf16[1136,256]{1,0:T(8,128)(2,1)S(1)} %get-tuple-element.14.own), channel_id=1, source_target_pairs={{0,64},{64,0},{1,65},{65,1},{2,66},{66,2},{3,67},{67,3},{4,68},{68... | collective-permute-start | bytes 1744904 | tf_op jit(solution)/shard_map/ppermute | solution.py:489
  24.5 30.7 %all-to-all-start = ((bf16[128,16,256]{2,1,0:T(8,128)(2,1)}), bf16[128,16,256]{2,1,0:T(8,128)(2,1)S(1)}, u32[]{:S(2)}, u32[]{:S(2)}) async-start(bf16[128,16,256]{2,1,0:T(8,128)(2,1)} %bitcast.13), calls=%async_computation | async-start | bytes 2097152 | tf_op jit(solution)/shard_map/all_to_all | solution.py:503
  34.3 6.6 %collective-permute-start.1 = (bf16[1136,256]{1,0:T(8,128)(2,1)S(1)}, bf16[1136,256]{1,0:T(8,128)(2,1)S(1)}, u32[]{:S(2)}, u32[]{:S(2)}) collective-permute-start(bf16[1136,256]{1,0:T(8,128)(2,1)S(1)} %collective-permute-done.across), channel_id=1, source_target_pairs={{0,32},{32,0},{1,33},{33,1},{2,34},{34,2},{3,35},{35,3},{4,36},{36... | collective-permute-start | bytes 1744904 | tf_op jit(solution)/shard_map/ppermute | solution.py:504
  47.5 5.3 %collective-permute-start.3 = (f32[64,128]{1,0:T(8,128)S(1)}, f32[64,128]{1,0:T(8,128)S(1)}, u32[]{:S(2)}, u32[]{:S(2)}) collective-permute-start(f32[64,128]{1,0:T(8,128)S(1)} %get-tuple-element.18), channel_id=1, source_target_pairs={{0,4},{4,8},{8,12},{12,0},{1,5},{5,9},{9,13},{13,1},{2,6},{6,10},{... | collective-permute-start | bytes 98312 | tf_op jit(solution)/shard_map/ppermute | solution.py:515
  48.7 5.4 %collective-permute-start.4 = (f32[64,128]{1,0:T(8,128)S(1)}, f32[64,128]{1,0:T(8,128)S(1)}, u32[]{:S(2)}, u32[]{:S(2)}) collective-permute-start(f32[64,128]{1,0:T(8,128)S(1)} %get-tuple-element.19), channel_id=1, source_target_pairs={{0,8},{4,12},{8,0},{12,4},{1,9},{5,13},{9,1},{13,5},{2,10},{6,14},... | collective-permute-start | bytes 98312 | tf_op jit(solution)/shard_map/ppermute | solution.py:515
  51.3 3.9 %collective-permute-start.5 = (f32[64,128]{1,0:T(8,128)S(1)}, f32[64,128]{1,0:T(8,128)S(1)}, u32[]{:S(2)}, u32[]{:S(2)}) collective-permute-start(f32[64,128]{1,0:T(8,128)S(1)} %get-tuple-element.20), channel_id=1, source_target_pairs={{0,12},{4,0},{8,4},{12,8},{1,13},{5,1},{9,5},{13,9},{2,14},{6,2},{... | collective-permute-start | bytes 98312 | tf_op jit(solution)/shard_map/ppermute | solution.py:515

commit v6 on v5

--- a/solution.py
+++ b/solution.py
@@ -187,7 +187,7 @@
             bytes_accessed=2 * (ITEMS * F_IN + F_IN * HID),
             transcendentals=0,
         ),
-        compiler_params=pltpu.CompilerParams(vmem_limit_bytes=28 << 20),
+        compiler_params=pltpu.CompilerParams(vmem_limit_bytes=20 << 20),
         name="tower",
     )(*[in_hbm(a) for a in (features, w_in, w_out, owners, ids, counts)])
 
@@ -206,8 +206,10 @@
 
 def unpack_columns(exts, col_ids, col_logq):
     fill = jnp.zeros((LANES - BLOCKS, LANES), F32)
-    for n, ext in enumerate(exts):
-        a, b, c = [ext[at : at + 16, :].astype(F32) for at in (EXT_A, EXT_B, EXT_C)]
+    for n, (ext, skip) in enumerate(exts):
+        a, b, c = [
+            ext[at - skip : at - skip + 16, :].astype(F32) for at in (EXT_A, EXT_B, EXT_C)
+        ]
         a, b, c = a[0:BLOCKS], b[0:BLOCKS], c[0:BLOCKS]
         ids = a[:, 0:LANES] * 4096.0 + a[:, LANES:EMB] * 64.0 + b[:, 0:LANES]
         logq = jnp.log(b[:, LANES:EMB] * 256.0 + c[:, 0:LANES] + 1.0) * LOG2E
@@ -218,10 +220,7 @@
                 col[at : at + LANES, :] = jnp.broadcast_to(turned[:, j : j + 1], (LANES, LANES))
 
 
-def score_tiles(q_ref, pos_all, row, tiles, exts, col_ids, col_logq, out_ref):
-    first, count = tiles
-    out_rows = count * Q_PARTS
-
+def score_tiles(q_ref, pos_all, row, exts, chunks, col_ids, col_logq, out_ref):
     def tile_inputs(t):
         q_rows = q_ref[pl.ds(pl.multiple_of(t * Q_TILE, Q_TILE), Q_TILE), :]
         at = row * (QDEV // LANES) + t * Q_PARTS
@@ -231,8 +230,10 @@
         return q_rows, jnp.broadcast_to(pos_row, (8, Q_TILE))
 
     def raw_scores(q_rows, n, c):
+        ext, skip = exts[n]
+        first = c * I_TILE - min(skip, I_TILE)
         return lax.dot_general(
-            exts[n][c * I_TILE : (c + 1) * I_TILE, :], q_rows, NT, preferred_element_type=F32
+            ext[first : first + I_TILE, :], q_rows, NT, preferred_element_type=F32
         )
 
     def wide(col, at):
@@ -244,10 +245,8 @@
         both = (highest + jnp.log(summed) * LOG2E, jnp.sum(positive, axis=0, keepdims=True))
         for k in range(2):
             for u in range(Q_PARTS):
-                at = k * out_rows + (t - first) * Q_PARTS + u
+                at = k * PART_POS + t * Q_PARTS + u
                 out_ref[pl.ds(at, 1), :] = both[k][:, u * LANES : (u + 1) * LANES]
-
-    chunks = [(n, c) for n in range(len(exts)) for c in range(ITEMS // I_TILE)]
 
     def fast_tile(t, worst):
         q_rows, pos8 = tile_inputs(t)
@@ -259,7 +258,8 @@
             if shift is None:
                 tops = [jnp.full((8, Q_TILE), FLOOR, F32)] * 2
                 for g in range(SAMPLE):
-                    logit = raw[g * 8 : g * 8 + 8, :] * SCALE2 - wide(col_logq, g * 8)
+                    at = n * ITEMS + c * I_TILE + g * 8
+                    logit = raw[g * 8 : g * 8 + 8, :] * SCALE2 - wide(col_logq, at)
                     tops[g % 2] = jnp.maximum(tops[g % 2], logit)
                 top = jnp.maximum(tops[0], tops[1])
                 shift = jnp.broadcast_to(jnp.max(top, axis=0, keepdims=True), (8, Q_TILE))
@@ -273,7 +273,7 @@
         finish(t, shift, total, jnp.where(hit > FLOOR / 2, hit + shift, 0.0))
         return jnp.maximum(worst, total)
 
-    worst = lax.fori_loop(first, first + count, fast_tile, jnp.zeros((8, Q_TILE), F32), unroll=True)
+    worst = lax.fori_loop(0, Q_STEPS, fast_tile, jnp.zeros((8, Q_TILE), F32), unroll=True)
 
     @pl.when(jnp.logical_not(jnp.max(worst) < 1e37))
     def _():
@@ -299,7 +299,7 @@
             finish(t, top, total, positive)
             return 0
 
-        lax.fori_loop(first, first + count, safe_tile, 0)
+        lax.fori_loop(0, Q_STEPS, safe_tile, 0)
 
 
 def slot_ids(held, row):
@@ -318,12 +318,17 @@
     return pltpu.roll(jnp.where(lane < CAP, value, 0.0), shift, 1)
 
 
-def score_and_list(q_ref, pos_all, exts, out_ref, col_ids, col_logq):
+WHOLE = tuple(range(ITEMS // I_TILE))
+REST_SKIP = EXT_A - (ITEMS - I_TILE)
+REST_ROWS = EXT_ROWS - REST_SKIP
+
+
+def score_and_list(q_ref, pos_all, exts, chunks, listed, out_ref, col_ids, col_logq):
     row = row_index()
     unpack_columns(exts, col_ids, col_logq)
-    for n, ext in enumerate(exts):
+    for n, ext in enumerate(listed):
         out_ref[PART_IDS + n * N_COLS : PART_IDS + (n + 1) * N_COLS, :] = slot_ids(ext, row)
-    score_tiles(q_ref, pos_all, row, (0, Q_STEPS), exts, col_ids, col_logq, out_ref)
+    score_tiles(q_ref, pos_all, row, exts, chunks, col_ids, col_logq, out_ref)
 
 
 SEND_CHUNK = 512
@@ -331,7 +336,7 @@
 
 
 def first_kernel(
-    q_ref, pos_all, own, sibling, slots, out_ref, send_hbm, send, sems, col_ids, col_logq
+    q_ref, pos_all, own, sibling, slots, out_ref, send_hbm, rest, send, sems, col_ids, col_logq
 ):
     slot_row = jnp.concatenate([slots[j : j + 1, :] for j in range(BLOCKS)], axis=1)
     copies = []
@@ -344,20 +349,36 @@
         ).astype(BF16)
         copies.append(pltpu.make_async_copy(send.at[at], send_hbm.at[at], sems.at[c]))
         copies[c].start()
-    score_and_list(q_ref, pos_all, (own, sibling), out_ref, col_ids, col_logq)
+    for k, (at, to, rows) in enumerate(
+        ((ITEMS - I_TILE, 0, I_TILE), (EXT_A, I_TILE, EXT_ROWS - EXT_A))
+    ):
+        copies.append(
+            pltpu.make_async_copy(
+                sibling.at[pl.ds(at, rows)], rest.at[pl.ds(to, rows)], sems.at[SEND_STEPS + k]
+            )
+        )
+        copies[-1].start()
+    both = ((own, 0), (sibling, 0))
+    chunks = [(0, c) for c in WHOLE] + [(1, c) for c in WHOLE[:1]]
+    score_and_list(q_ref, pos_all, both, chunks, (own, sibling), out_ref, col_ids, col_logq)
     for copy in copies:
         copy.wait()
 
 
-def next_kernel(q_ref, pos_all, across, first, out_ref, col_ids, col_logq):
+def next_kernel(q_ref, pos_all, rest, across, first, out_ref, col_ids, col_logq):
     del first
-    score_and_list(q_ref, pos_all, (across,), out_ref, col_ids, col_logq)
+    chunks = [(0, c) for c in WHOLE[1:]] + [(1, c) for c in WHOLE]
+    score_and_list(
+        q_ref, pos_all, ((rest, REST_SKIP), (across, 0)), chunks, (across,), out_ref, col_ids,
+        col_logq,
+    )
 
 
 def last_kernel(q_ref, pos_all, far, first, middle, mine, *rest):
     to_x = rest[0 : N_X - 1]
     last, col_ids, col_logq = rest[N_X - 1 :]
-    score_and_list(q_ref, pos_all, (far,), last, col_ids, col_logq)
+    chunks = [(0, c) for c in WHOLE]
+    score_and_list(q_ref, pos_all, ((far, 0),), chunks, (far,), last, col_ids, col_logq)
     held = (first, middle, last)
     sums = [ref[0:PART_POS, :] for ref in held]
     highest = jnp.maximum(jnp.maximum(sums[0], sums[1]), sums[2])
@@ -419,16 +440,16 @@
         kernel,
         in_specs=[VMEM_SPEC] * len(args),
         out_specs=[VMEM_SPEC] * len(out_shapes) + [ANY_SPEC] * len(in_hbm_too),
-        out_shape=[pltpu.VMEM(shape, F32) for shape in out_shapes] + list(in_hbm_too),
+        out_shape=[pltpu.VMEM(*shape) for shape in out_shapes] + list(in_hbm_too),
         scratch_shapes=scratch + columns,
         cost_estimate=pl.CostEstimate(
             flops=2 * QDEV * n_blocks * ITEMS * EMB,
             bytes_accessed=2 * n_blocks * ITEMS * EMB,
             transcendentals=QDEV * n_blocks * ITEMS,
         ),
-        compiler_params=pltpu.CompilerParams(vmem_limit_bytes=20 << 20),
+        compiler_params=pltpu.CompilerParams(vmem_limit_bytes=12 << 20),
         name=name,
-    )(*[near_core(a) for a in args])
+    )(*[near_core(a) if a.shape[0] != REST_ROWS else in_hbm(a) for a in args])
 
 
 POOL_STEPS = 8
@@ -488,26 +509,28 @@
     )
     across = lax.ppermute(own, "rows_0", SWAP)
     sibling = lax.ppermute(own, "rows_1", SWAP)
-    one = (PART_IDS + N_COLS, LANES)
-    two = (PART_IDS + 2 * N_COLS, LANES)
+    one = ((PART_IDS + N_COLS, LANES), F32)
+    two = ((PART_IDS + 2 * N_COLS, LANES), F32)
     sent = pltpu.HBM((N_DEV * CAP, EMB), BF16)
-    first, send = scored(
+    first, send, rest = scored(
         first_kernel,
         2,
         [two],
-        [pltpu.VMEM((N_DEV * CAP, EMB), BF16), pltpu.SemaphoreType.DMA((SEND_STEPS,))],
+        [pltpu.VMEM((N_DEV * CAP, EMB), BF16), pltpu.SemaphoreType.DMA((SEND_STEPS + 2,))],
         (queries, pos, own, sibling, slots),
         "score_first",
-        [sent],
+        [sent, pltpu.HBM((REST_ROWS, EMB), BF16)],
     )
     pool_emb = lax.all_to_all(send, ROWS_COLS, split_axis=0, concat_axis=0, tiled=True)
     far = lax.ppermute(across, "rows_1", SWAP)
-    (middle,) = scored(next_kernel, 1, [one], [], (queries, pos, across, first), "score_next")
+    (middle,) = scored(
+        next_kernel, 2, [one], [], (queries, pos, rest, across, first), "score_next"
+    )
     mine, *to_x = scored(
         last_kernel,
         1,
-        [(X_ROWS, LANES)] * N_X,
-        [pltpu.VMEM(one, F32)],
+        [((X_ROWS, LANES), F32)] * N_X,
+        [pltpu.VMEM(*one)],
         (queries, pos, far, first, middle),
         "score_last",
     )

time: 69.6 us -> 70.7 us (1.016)
  Pallas kernels: 35.2 us -> 36.1 us
    pallas_call x3, Pallas kernels: 26.1 us -> 27 us  [scored(): pl.pallas_call(kernel, in_specs=[VMEM_SPEC] * len(args), out_specs=[VMEM_...]
where the time goes in v6:
time: 70.7 us; the launch traced here: 70.4 us
  Pallas kernels  36.1 us (51%)
  starting transfers between devices  18.8 us (27%)
  blocking collectives  12.2 us (17%)
  waiting for transfers between devices  2.46 us (3%)
  between operations  0.88 us (1%)
    pallas_call x3, Pallas kernels, scored(): pl.pallas_call(kernel, in_specs=[VMEM_SPEC] * len(args), out_specs=[VMEM_...  27 us
    all_to_all x1, blocking collectives, local(): lax.all_to_all(collect(held, pool_emb), ('cols_0', 'cols_2'), split_axis=...  12.2 us
    all_to_all x1, starting transfers between devices, local(): lax.all_to_all(send, ROWS_COLS, split_axis=0, concat_axis=0, tiled=True)  9.76 us
    pallas_call x1, Pallas kernels, tower(): pl.pallas_call(tower_kernel, in_specs=[ANY_SPEC] * 6, out_specs=[VMEM_SPE...  7.38 us
    ppermute x3, starting transfers between devices, local(): lax.ppermute(part, 'cols_1', [(x, (x + step) % N_X) for x in range(N_X)])  5.26 us
    ppermute x1, starting transfers between devices, local(): across = lax.ppermute(own, 'rows_0', SWAP)  3.39 us
    ppermute x3, waiting for transfers between devices, local(): lax.ppermute(part, 'cols_1', [(x, (x + step) % N_X) for x in range(N_X)])  2.45 us
    pallas_call x1, Pallas kernels, merge(): pl.pallas_call(merge_kernel, in_specs=[VMEM_SPEC, VMEM_SPEC], out_specs=[...  1.63 us
  transfers between devices with their start and end apart: 7, of which 2 were waited for; matrix products, arithmetic and copies ran while one was open for 0% of the time, Pallas kernels for 38%

profile of v6, /device:TPU:0, one launch (start us, length us, event | category | flops | bytes accessed | tf_op | source)
XLA Modules:
  0.0 70.4 jit_solution(106125644746365111)
XLA Ops:
  0.6 0.0 copy-start
  0.6 0.0 copy-start.1
  0.7 7.4 %tower.1 = (bf16[1136,256]{1,0:T(8,128)(2,1)S(1)}, s32[8,128]{1,0:T(8,128)S(1)}) custom-call(bf16[1024,2048]{1,0:T(8,128)(2,1)} %feat_hbm.1, bf16[2048,1024]{1,0:T(8,128)(2,1)} %w_in_hbm.1, bf16[1024,256]{1,0:T(8,128)(2,1)} %w_out_hbm.1, s32[8,128]{1,0:T(8,128)} %bitcast.16, s32[8,128]{1,0:T(8,128)} %bitcast.17, s32[8,128]{1,0:T(8,128)} %bitcast.18), custom_call_target="tpu_custom_call" | custom-call | flops 4831838208 | bytes 8388608 | tf_op jit(solution)/shard_map/tower/pallas_call | solution.py:164
  8.0 0.1 collective-permute-start.2
  8.1 3.4 %collective-permute-start = (bf16[1136,256]{1,0:T(8,128)(2,1)S(1)}, bf16[1136,256]{1,0:T(8,128)(2,1)S(1)}, u32[]{:S(2)}, u32[]{:S(2)}) collective-permute-start(bf16[1136,256]{1,0:T(8,128)(2,1)S(1)} %get-tuple-element.15.own), channel_id=1, source_target_pairs={{0,64},{64,0},{1,65},{65,1},{2,66},{66,2},{3,67},{67,3},{4,68},{68... | collective-permute-start | bytes 1744904 | tf_op jit(solution)/shard_map/ppermute | solution.py:510
  11.5 0.0 collective-permute-done.2.sibling
  11.5 0.0 copy-done
  11.5 0.0 copy-done.1
  11.5 10.1 %score_first.1 = (f32[96,128]{1,0:T(8,128)S(1)}, bf16[2048,256]{1,0:T(8,128)(2,1)}, bf16[560,256]{1,0:T(8,128)(2,1)}) custom-call(bf16[2048,256]{1,0:T(8,128)(2,1)S(1)} %copy-done, s32[64,128]{1,0:T(8,128)S(1)} %bitcast.10, bf16[1136,256]{1,0:T(8,128)(2,1)S(1)} %get-tuple-element.15.own, bf16[1136,256]{1,0:T(8,128)(2,1)S(1)} %collective-permute-done.2.sibling, ...), custom_call_target="tpu_custom_call" | custom-call | flops 2147483648 | bytes 1048576 | tf_op jit(solution)/shard_map/score_first/pallas_call | solution.py:439
  21.7 9.8 %all-to-all-start = ((bf16[128,16,256]{2,1,0:T(8,128)(2,1)}), bf16[128,16,256]{2,1,0:T(8,128)(2,1)S(1)}, u32[]{:S(2)}, u32[]{:S(2)}) async-start(bf16[128,16,256]{2,1,0:T(8,128)(2,1)} %bitcast.13), calls=%async_computation | async-start | bytes 2097152 | tf_op jit(solution)/shard_map/all_to_all | solution.py:524
  31.4 0.0 collective-permute-done.across
  31.4 0.3 collective-permute-start.1
  31.7 10.2 %score_next.1.middle = f32[64,128]{1,0:T(8,128)S(1)} custom-call(bf16[2048,256]{1,0:T(8,128)(2,1)S(1)} %copy-done, s32[64,128]{1,0:T(8,128)S(1)} %bitcast.11, bf16[560,256]{1,0:T(8,128)(2,1)} %get-tuple-element.18.rest, bf16[1136,256]{1,0:T(8,128)(2,1)S(1)} %collective-permute-done.across, f32[96,128]{1,0:T(8,128)S(1)} %get-tuple-element.17.first), custom_call_target="tpu_custom_call" | custom-call | flops 2147483648 | bytes 1048576 | tf_op jit(solution)/shard_map/score_next/pallas_call | solution.py:439
  42.0 0.0 collective-permute-done.1.far
  42.0 6.6 %score_last.1 = (f32[64,128]{1,0:T(8,128)S(1)}, f32[64,128]{1,0:T(8,128)S(1)}, f32[64,128]{1,0:T(8,128)S(1)}, f32[64,128]{1,0:T(8,128)S(1)}) custom-call(bf16[2048,256]{1,0:T(8,128)(2,1)S(1)} %copy-done, s32[64,128]{1,0:T(8,128)S(1)} %bitcast.12, bf16[1136,256]{1,0:T(8,128)(2,1)S(1)} %collective-permute-done.1.far, f32[96,128]{1,0:T(8,128)S(1)} %get-tuple-element.17.first, ...), custom_call_target="tpu_custom_call" | custom-call | flops 1073741824 | bytes 524288 | tf_op jit(solution)/shard_map/score_last/pallas_call | solution.py:439
  48.6 1.1 %collective-permute-start.3 = (f32[64,128]{1,0:T(8,128)S(1)}, f32[64,128]{1,0:T(8,128)S(1)}, u32[]{:S(2)}, u32[]{:S(2)}) collective-permute-start(f32[64,128]{1,0:T(8,128)S(1)} %get-tuple-element.20), channel_id=1, source_target_pairs={{0,4},{4,8},{8,12},{12,0},{1,5},{5,9},{9,13},{13,1},{2,6},{6,10},{... | collective-permute-start | bytes 98312 | tf_op jit(solution)/shard_map/ppermute | solution.py:538
  49.7 2.7 %collective-permute-start.4 = (f32[64,128]{1,0:T(8,128)S(1)}, f32[64,128]{1,0:T(8,128)S(1)}, u32[]{:S(2)}, u32[]{:S(2)}) collective-permute-start(f32[64,128]{1,0:T(8,128)S(1)} %get-tuple-element.21), channel_id=1, source_target_pairs={{0,8},{4,12},{8,0},{12,4},{1,9},{5,13},{9,1},{13,5},{2,10},{6,14},... | collective-permute-start | bytes 98312 | tf_op jit(solution)/shard_map/ppermute | solution.py:538
  52.4 1.5 %collective-permute-start.5 = (f32[64,128]{1,0:T(8,128)S(1)}, f32[64,128]{1,0:T(8,128)S(1)}, u32[]{:S(2)}, u32[]{:S(2)}) collective-permute-start(f32[64,128]{1,0:T(8,128)S(1)} %get-tuple-element.22), channel_id=1, source_target_pairs={{0,12},{4,0},{8,4},{12,8},{1,13},{5,1},{9,5},{13,9},{2,14},{6,2},{... | collective-permute-start | bytes 98312 | tf_op jit(solution)/shard_map/ppermute | solution.py:538
  53.9 0.0 collective-permute-done.3.rest_0_
  53.9 1.3 %collective-permute-done.4.rest_1_ = f32[64,128]{1,0:T(8,128)S(1)} collective-permute-done((f32[64,128]{1,0:T(8,128)S(1)}, f32[64,128]{1,0:T(8,128)S(1)}, u32[]{:S(2)}, u32[]{:S(2)}) %collective-permute-start.4) | collective-permute-done | bytes 32800 | tf_op jit(solution)/shard_map/ppermute | solution.py:538
  55.2 1.2 %collective-permute-done.5.rest_2_ = f32[64,128]{1,0:T(8,128)S(1)} collective-permute-done((f32[64,128]{1,0:T(8,128)S(1)}, f32[64,128]{1,0:T(8,128)S(1)}, u32[]{:S(2)}, u32[]{:S(2)}) %collective-permute-start.5) | collective-permute-done | bytes 32800 | tf_op jit(solution)/shard_map/ppermute | solution.py:538
  56.3 0.0 all-to-all-done
  56.3 0.1 collect.1
  56.4 12.2 %all_to_all.16.parts_ref = f32[8,40,128]{2,1,0:T(8,128)S(1)} all-to-all(f32[8,40,128]{2,1,0:T(8,128)S(1)} %collect.1), channel_id=1, replica_groups=mesh['rows_0'=2,'rows_1'=2,'cols_0'=2,'cols_1'=4,'cols_2'=4] {'cols_0','..., dimensions={0} | all-to-all | bytes 327680 | tf_op jit(solution)/shard_map/all_to_all | solution.py:541
  68.7 1.6 %merge.1 = (f32[16,128]{1,0:T(8,128)}, s32[16,128]{1,0:T(8,128)}, bf16[2048,256]{1,0:T(8,128)(2,1)}) custom-call(f32[8,40,128]{2,1,0:T(8,128)S(1)} %all_to_all.16.parts_ref, bf16[2048,256]{1,0:T(8,128)(2,1)S(1)} %bitcast.9), custom_call_target="tpu_custom_call" | custom-call | tf_op jit(solution)/shard_map/merge/pallas_call | solution.py:482
Async XLA Ops:
  0.6 10.9 %copy-start = (bf16[2048,256]{1,0:T(8,128)(2,1)S(1)}, bf16[2048,256]{1,0:T(8,128)(2,1)}, u32[]{:S(2)}) copy-start(bf16[2048,256]{1,0:T(8,128)(2,1)} %q_ref.5) | copy-start | bytes 3145732
  0.6 10.9 %copy-start.1 = (s32[8192]{0:T(1024)S(1)}, s32[8192]{0:T(1024)}, u32[]{:S(2)}) copy-start(s32[8192]{0:T(1024)} %param.15) | copy-start | bytes 98308
  8.0 3.5 %collective-permute-start.2 = (bf16[1136,256]{1,0:T(8,128)(2,1)S(1)}, bf16[1136,256]{1,0:T(8,128)(2,1)S(1)}, u32[]{:S(2)}, u32[]{:S(2)}) collective-permute-start(bf16[1136,256]{1,0:T(8,128)(2,1)S(1)} %get-tuple-element.15.own), channel_id=1, source_target_pairs={{0,32},{32,0},{1,33},{33,1},{2,34},{34,2},{3,35},{35,3},{4,36},{36... | collective-permute-start | bytes 1744904 | tf_op jit(solution)/shard_map/ppermute | solution.py:511
  8.1 23.3 %collective-permute-start = (bf16[1136,256]{1,0:T(8,128)(2,1)S(1)}, bf16[1136,256]{1,0:T(8,128)(2,1)S(1)}, u32[]{:S(2)}, u32[]{:S(2)}) collective-permute-start(bf16[1136,256]{1,0:T(8,128)(2,1)S(1)} %get-tuple-element.15.own), channel_id=1, source_target_pairs={{0,64},{64,0},{1,65},{65,1},{2,66},{66,2},{3,67},{67,3},{4,68},{68... | collective-permute-start | bytes 1744904 | tf_op jit(solution)/shard_map/ppermute | solution.py:510
  21.7 34.7 %all-to-all-start = ((bf16[128,16,256]{2,1,0:T(8,128)(2,1)}), bf16[128,16,256]{2,1,0:T(8,128)(2,1)S(1)}, u32[]{:S(2)}, u32[]{:S(2)}) async-start(bf16[128,16,256]{2,1,0:T(8,128)(2,1)} %bitcast.13), calls=%async_computation | async-start | bytes 2097152 | tf_op jit(solution)/shard_map/all_to_all | solution.py:524
  31.4 10.5 %collective-permute-start.1 = (bf16[1136,256]{1,0:T(8,128)(2,1)S(1)}, bf16[1136,256]{1,0:T(8,128)(2,1)S(1)}, u32[]{:S(2)}, u32[]{:S(2)}) collective-permute-start(bf16[1136,256]{1,0:T(8,128)(2,1)S(1)} %collective-permute-done.across), channel_id=1, source_target_pairs={{0,32},{32,0},{1,33},{33,1},{2,34},{34,2},{3,35},{35,3},{4,36},{36... | collective-permute-start | bytes 1744904 | tf_op jit(solution)/shard_map/ppermute | solution.py:525
  48.6 5.3 %collective-permute-start.3 = (f32[64,128]{1,0:T(8,128)S(1)}, f32[64,128]{1,0:T(8,128)S(1)}, u32[]{:S(2)}, u32[]{:S(2)}) collective-permute-start(f32[64,128]{1,0:T(8,128)S(1)} %get-tuple-element.20), channel_id=1, source_target_pairs={{0,4},{4,8},{8,12},{12,0},{1,5},{5,9},{9,13},{13,1},{2,6},{6,10},{... | collective-permute-start | bytes 98312 | tf_op jit(solution)/shard_map/ppermute | solution.py:538
  49.7 5.4 %collective-permute-start.4 = (f32[64,128]{1,0:T(8,128)S(1)}, f32[64,128]{1,0:T(8,128)S(1)}, u32[]{:S(2)}, u32[]{:S(2)}) collective-permute-start(f32[64,128]{1,0:T(8,128)S(1)} %get-tuple-element.21), channel_id=1, source_target_pairs={{0,8},{4,12},{8,0},{12,4},{1,9},{5,13},{9,1},{13,5},{2,10},{6,14},... | collective-permute-start | bytes 98312 | tf_op jit(solution)/shard_map/ppermute | solution.py:538
  52.4 3.9 %collective-permute-start.5 = (f32[64,128]{1,0:T(8,128)S(1)}, f32[64,128]{1,0:T(8,128)S(1)}, u32[]{:S(2)}, u32[]{:S(2)}) collective-permute-start(f32[64,128]{1,0:T(8,128)S(1)} %get-tuple-element.22), channel_id=1, source_target_pairs={{0,12},{4,0},{8,4},{12,8},{1,13},{5,1},{9,5},{13,9},{2,14},{6,2},{... | collective-permute-start | bytes 98312 | tf_op jit(solution)/shard_map/ppermute | solution.py:538

commit v7 on v6

--- a/solution.py
+++ b/solution.py
@@ -197,14 +197,14 @@
 Q_STEPS = QDEV // Q_TILE
 I_TILE = 512
 GROUPS = I_TILE // 8
-SAMPLE = 16
+SAMPLE = 4
 
 
 def row_index():
     return lax.axis_index("rows_0") * 2 + lax.axis_index("rows_1")
 
 
-def unpack_columns(exts, col_ids, col_logq):
+def unpack_columns(exts, chunks, col_ids, col_logq):
     fill = jnp.zeros((LANES - BLOCKS, LANES), F32)
     for n, (ext, skip) in enumerate(exts):
         a, b, c = [
@@ -216,6 +216,8 @@
         for value, col in ((ids, col_ids), (logq, col_logq)):
             turned = jnp.concatenate([value, fill], axis=0).T
             for j in range(BLOCKS):
+                if (n, j * LANES // I_TILE) not in chunks:
+                    continue
                 at = n * ITEMS + j * LANES
                 col[at : at + LANES, :] = jnp.broadcast_to(turned[:, j : j + 1], (LANES, LANES))
 
@@ -325,7 +327,7 @@
 
 def score_and_list(q_ref, pos_all, exts, chunks, listed, out_ref, col_ids, col_logq):
     row = row_index()
-    unpack_columns(exts, col_ids, col_logq)
+    unpack_columns(exts, chunks, col_ids, col_logq)
     for n, ext in enumerate(listed):
         out_ref[PART_IDS + n * N_COLS : PART_IDS + (n + 1) * N_COLS, :] = slot_ids(ext, row)
     score_tiles(q_ref, pos_all, row, exts, chunks, col_ids, col_logq, out_ref)

time: 70.7 us -> 70.3 us (level)
  no operation moved by 1% of the time
where the time goes in v7:
time: 70.3 us; the launch traced here: 70.1 us
  Pallas kernels  35.8 us (51%)
  starting transfers between devices  18.8 us (27%)
  blocking collectives  12.2 us (17%)
  waiting for transfers between devices  2.46 us (3%)
  between operations  0.88 us (1%)
    pallas_call x3, Pallas kernels, scored(): pl.pallas_call(kernel, in_specs=[VMEM_SPEC] * len(args), out_specs=[VMEM_...  26.6 us
    all_to_all x1, blocking collectives, local(): lax.all_to_all(collect(held, pool_emb), ('cols_0', 'cols_2'), split_axis=...  12.2 us
    all_to_all x1, starting transfers between devices, local(): lax.all_to_all(send, ROWS_COLS, split_axis=0, concat_axis=0, tiled=True)  9.76 us
    pallas_call x1, Pallas kernels, tower(): pl.pallas_call(tower_kernel, in_specs=[ANY_SPEC] * 6, out_specs=[VMEM_SPE...  7.38 us
    ppermute x3, starting transfers between devices, local(): lax.ppermute(part, 'cols_1', [(x, (x + step) % N_X) for x in range(N_X)])  5.26 us
    ppermute x1, starting transfers between devices, local(): across = lax.ppermute(own, 'rows_0', SWAP)  3.39 us
    ppermute x3, waiting for transfers between devices, local(): lax.ppermute(part, 'cols_1', [(x, (x + step) % N_X) for x in range(N_X)])  2.45 us
    pallas_call x1, Pallas kernels, merge(): pl.pallas_call(merge_kernel, in_specs=[VMEM_SPEC, VMEM_SPEC], out_specs=[...  1.63 us
  transfers between devices with their start and end apart: 7, of which 2 were waited for; matrix products, arithmetic and copies ran while one was open for 0% of the time, Pallas kernels for 38%

profile of v7, /device:TPU:0, one launch (start us, length us, event | category | flops | bytes accessed | tf_op | source)
XLA Modules:
  0.0 70.1 jit_solution(3400242338270636916)
XLA Ops:
  0.6 0.0 copy-start
  0.6 0.0 copy-start.1
  0.7 7.4 %tower.1 = (bf16[1136,256]{1,0:T(8,128)(2,1)S(1)}, s32[8,128]{1,0:T(8,128)S(1)}) custom-call(bf16[1024,2048]{1,0:T(8,128)(2,1)} %feat_hbm.1, bf16[2048,1024]{1,0:T(8,128)(2,1)} %w_in_hbm.1, bf16[1024,256]{1,0:T(8,128)(2,1)} %w_out_hbm.1, s32[8,128]{1,0:T(8,128)} %bitcast.16, s32[8,128]{1,0:T(8,128)} %bitcast.17, s32[8,128]{1,0:T(8,128)} %bitcast.18), custom_call_target="tpu_custom_call" | custom-call | flops 4831838208 | bytes 8388608 | tf_op jit(solution)/shard_map/tower/pallas_call | solution.py:164
  8.0 0.1 collective-permute-start.2
  8.1 3.4 %collective-permute-start = (bf16[1136,256]{1,0:T(8,128)(2,1)S(1)}, bf16[1136,256]{1,0:T(8,128)(2,1)S(1)}, u32[]{:S(2)}, u32[]{:S(2)}) collective-permute-start(bf16[1136,256]{1,0:T(8,128)(2,1)S(1)} %get-tuple-element.15.own), channel_id=1, source_target_pairs={{0,64},{64,0},{1,65},{65,1},{2,66},{66,2},{3,67},{67,3},{4,68},{68... | collective-permute-start | bytes 1744904 | tf_op jit(solution)/shard_map/ppermute | solution.py:512
  11.5 0.0 collective-permute-done.2.sibling
  11.5 0.0 copy-done
  11.5 0.0 copy-done.1
  11.5 10.0 %score_first.1 = (f32[96,128]{1,0:T(8,128)S(1)}, bf16[2048,256]{1,0:T(8,128)(2,1)}, bf16[560,256]{1,0:T(8,128)(2,1)}) custom-call(bf16[2048,256]{1,0:T(8,128)(2,1)S(1)} %copy-done, s32[64,128]{1,0:T(8,128)S(1)} %bitcast.10, bf16[1136,256]{1,0:T(8,128)(2,1)S(1)} %get-tuple-element.15.own, bf16[1136,256]{1,0:T(8,128)(2,1)S(1)} %collective-permute-done.2.sibling, ...), custom_call_target="tpu_custom_call" | custom-call | flops 2147483648 | bytes 1048576 | tf_op jit(solution)/shard_map/score_first/pallas_call | solution.py:441
  21.5 9.8 %all-to-all-start = ((bf16[128,16,256]{2,1,0:T(8,128)(2,1)}), bf16[128,16,256]{2,1,0:T(8,128)(2,1)S(1)}, u32[]{:S(2)}, u32[]{:S(2)}) async-start(bf16[128,16,256]{2,1,0:T(8,128)(2,1)} %bitcast.13), calls=%async_computation | async-start | bytes 2097152 | tf_op jit(solution)/shard_map/all_to_all | solution.py:526
  31.3 0.0 collective-permute-done.across
  31.3 0.3 collective-permute-start.1
  31.6 10.2 %score_next.1.middle = f32[64,128]{1,0:T(8,128)S(1)} custom-call(bf16[2048,256]{1,0:T(8,128)(2,1)S(1)} %copy-done, s32[64,128]{1,0:T(8,128)S(1)} %bitcast.11, bf16[560,256]{1,0:T(8,128)(2,1)} %get-tuple-element.18.rest, bf16[1136,256]{1,0:T(8,128)(2,1)S(1)} %collective-permute-done.across, f32[96,128]{1,0:T(8,128)S(1)} %get-tuple-element.17.first), custom_call_target="tpu_custom_call" | custom-call | flops 2147483648 | bytes 1048576 | tf_op jit(solution)/shard_map/score_next/pallas_call | solution.py:441
  41.7 0.0 collective-permute-done.1.far
  41.8 6.5 %score_last.1 = (f32[64,128]{1,0:T(8,128)S(1)}, f32[64,128]{1,0:T(8,128)S(1)}, f32[64,128]{1,0:T(8,128)S(1)}, f32[64,128]{1,0:T(8,128)S(1)}) custom-call(bf16[2048,256]{1,0:T(8,128)(2,1)S(1)} %copy-done, s32[64,128]{1,0:T(8,128)S(1)} %bitcast.12, bf16[1136,256]{1,0:T(8,128)(2,1)S(1)} %collective-permute-done.1.far, f32[96,128]{1,0:T(8,128)S(1)} %get-tuple-element.17.first, ...), custom_call_target="tpu_custom_call" | custom-call | flops 1073741824 | bytes 524288 | tf_op jit(solution)/shard_map/score_last/pallas_call | solution.py:441
  48.3 1.1 %collective-permute-start.3 = (f32[64,128]{1,0:T(8,128)S(1)}, f32[64,128]{1,0:T(8,128)S(1)}, u32[]{:S(2)}, u32[]{:S(2)}) collective-permute-start(f32[64,128]{1,0:T(8,128)S(1)} %get-tuple-element.20), channel_id=1, source_target_pairs={{0,4},{4,8},{8,12},{12,0},{1,5},{5,9},{9,13},{13,1},{2,6},{6,10},{... | collective-permute-start | bytes 98312 | tf_op jit(solution)/shard_map/ppermute | solution.py:540
  49.4 2.7 %collective-permute-start.4 = (f32[64,128]{1,0:T(8,128)S(1)}, f32[64,128]{1,0:T(8,128)S(1)}, u32[]{:S(2)}, u32[]{:S(2)}) collective-permute-start(f32[64,128]{1,0:T(8,128)S(1)} %get-tuple-element.21), channel_id=1, source_target_pairs={{0,8},{4,12},{8,0},{12,4},{1,9},{5,13},{9,1},{13,5},{2,10},{6,14},... | collective-permute-start | bytes 98312 | tf_op jit(solution)/shard_map/ppermute | solution.py:540
  52.1 1.5 %collective-permute-start.5 = (f32[64,128]{1,0:T(8,128)S(1)}, f32[64,128]{1,0:T(8,128)S(1)}, u32[]{:S(2)}, u32[]{:S(2)}) collective-permute-start(f32[64,128]{1,0:T(8,128)S(1)} %get-tuple-element.22), channel_id=1, source_target_pairs={{0,12},{4,0},{8,4},{12,8},{1,13},{5,1},{9,5},{13,9},{2,14},{6,2},{... | collective-permute-start | bytes 98312 | tf_op jit(solution)/shard_map/ppermute | solution.py:540
  53.5 0.0 collective-permute-done.3.rest_0_
  53.5 1.3 %collective-permute-done.4.rest_1_ = f32[64,128]{1,0:T(8,128)S(1)} collective-permute-done((f32[64,128]{1,0:T(8,128)S(1)}, f32[64,128]{1,0:T(8,128)S(1)}, u32[]{:S(2)}, u32[]{:S(2)}) %collective-permute-start.4) | collective-permute-done | bytes 32800 | tf_op jit(solution)/shard_map/ppermute | solution.py:540
  54.8 1.2 %collective-permute-done.5.rest_2_ = f32[64,128]{1,0:T(8,128)S(1)} collective-permute-done((f32[64,128]{1,0:T(8,128)S(1)}, f32[64,128]{1,0:T(8,128)S(1)}, u32[]{:S(2)}, u32[]{:S(2)}) %collective-permute-start.5) | collective-permute-done | bytes 32800 | tf_op jit(solution)/shard_map/ppermute | solution.py:540
  56.0 0.0 all-to-all-done
  56.0 0.1 collect.1
  56.1 12.2 %all_to_all.16.parts_ref = f32[8,40,128]{2,1,0:T(8,128)S(1)} all-to-all(f32[8,40,128]{2,1,0:T(8,128)S(1)} %collect.1), channel_id=1, replica_groups=mesh['rows_0'=2,'rows_1'=2,'cols_0'=2,'cols_1'=4,'cols_2'=4] {'cols_0','..., dimensions={0} | all-to-all | bytes 327680 | tf_op jit(solution)/shard_map/all_to_all | solution.py:543
  68.3 1.6 %merge.1 = (f32[16,128]{1,0:T(8,128)}, s32[16,128]{1,0:T(8,128)}, bf16[2048,256]{1,0:T(8,128)(2,1)}) custom-call(f32[8,40,128]{2,1,0:T(8,128)S(1)} %all_to_all.16.parts_ref, bf16[2048,256]{1,0:T(8,128)(2,1)S(1)} %bitcast.9), custom_call_target="tpu_custom_call" | custom-call | tf_op jit(solution)/shard_map/merge/pallas_call | solution.py:484
Async XLA Ops:
  0.6 10.9 %copy-start = (bf16[2048,256]{1,0:T(8,128)(2,1)S(1)}, bf16[2048,256]{1,0:T(8,128)(2,1)}, u32[]{:S(2)}) copy-start(bf16[2048,256]{1,0:T(8,128)(2,1)} %q_ref.5) | copy-start | bytes 3145732
  0.6 10.9 %copy-start.1 = (s32[8192]{0:T(1024)S(1)}, s32[8192]{0:T(1024)}, u32[]{:S(2)}) copy-start(s32[8192]{0:T(1024)} %param.15) | copy-start | bytes 98308
  8.0 3.5 %collective-permute-start.2 = (bf16[1136,256]{1,0:T(8,128)(2,1)S(1)}, bf16[1136,256]{1,0:T(8,128)(2,1)S(1)}, u32[]{:S(2)}, u32[]{:S(2)}) collective-permute-start(bf16[1136,256]{1,0:T(8,128)(2,1)S(1)} %get-tuple-element.15.own), channel_id=1, source_target_pairs={{0,32},{32,0},{1,33},{33,1},{2,34},{34,2},{3,35},{35,3},{4,36},{36... | collective-permute-start | bytes 1744904 | tf_op jit(solution)/shard_map/ppermute | solution.py:513
  8.1 23.2 %collective-permute-start = (bf16[1136,256]{1,0:T(8,128)(2,1)S(1)}, bf16[1136,256]{1,0:T(8,128)(2,1)S(1)}, u32[]{:S(2)}, u32[]{:S(2)}) collective-permute-start(bf16[1136,256]{1,0:T(8,128)(2,1)S(1)} %get-tuple-element.15.own), channel_id=1, source_target_pairs={{0,64},{64,0},{1,65},{65,1},{2,66},{66,2},{3,67},{67,3},{4,68},{68... | collective-permute-start | bytes 1744904 | tf_op jit(solution)/shard_map/ppermute | solution.py:512
  21.5 34.4 %all-to-all-start = ((bf16[128,16,256]{2,1,0:T(8,128)(2,1)}), bf16[128,16,256]{2,1,0:T(8,128)(2,1)S(1)}, u32[]{:S(2)}, u32[]{:S(2)}) async-start(bf16[128,16,256]{2,1,0:T(8,128)(2,1)} %bitcast.13), calls=%async_computation | async-start | bytes 2097152 | tf_op jit(solution)/shard_map/all_to_all | solution.py:526
  31.3 10.4 %collective-permute-start.1 = (bf16[1136,256]{1,0:T(8,128)(2,1)S(1)}, bf16[1136,256]{1,0:T(8,128)(2,1)S(1)}, u32[]{:S(2)}, u32[]{:S(2)}) collective-permute-start(bf16[1136,256]{1,0:T(8,128)(2,1)S(1)} %collective-permute-done.across), channel_id=1, source_target_pairs={{0,32},{32,0},{1,33},{33,1},{2,34},{34,2},{3,35},{35,3},{4,36},{36... | collective-permute-start | bytes 1744904 | tf_op jit(solution)/shard_map/ppermute | solution.py:527
  48.3 5.3 %collective-permute-start.3 = (f32[64,128]{1,0:T(8,128)S(1)}, f32[64,128]{1,0:T(8,128)S(1)}, u32[]{:S(2)}, u32[]{:S(2)}) collective-permute-start(f32[64,128]{1,0:T(8,128)S(1)} %get-tuple-element.20), channel_id=1, source_target_pairs={{0,4},{4,8},{8,12},{12,0},{1,5},{5,9},{9,13},{13,1},{2,6},{6,10},{... | collective-permute-start | bytes 98312 | tf_op jit(solution)/shard_map/ppermute | solution.py:540
  49.4 5.4 %collective-permute-start.4 = (f32[64,128]{1,0:T(8,128)S(1)}, f32[64,128]{1,0:T(8,128)S(1)}, u32[]{:S(2)}, u32[]{:S(2)}) collective-permute-start(f32[64,128]{1,0:T(8,128)S(1)} %get-tuple-element.21), channel_id=1, source_target_pairs={{0,8},{4,12},{8,0},{12,4},{1,9},{5,13},{9,1},{13,5},{2,10},{6,14},... | collective-permute-start | bytes 98312 | tf_op jit(solution)/shard_map/ppermute | solution.py:540
  52.1 3.9 %collective-permute-start.5 = (f32[64,128]{1,0:T(8,128)S(1)}, f32[64,128]{1,0:T(8,128)S(1)}, u32[]{:S(2)}, u32[]{:S(2)}) collective-permute-start(f32[64,128]{1,0:T(8,128)S(1)} %get-tuple-element.22), channel_id=1, source_target_pairs={{0,12},{4,0},{8,4},{12,8},{1,13},{5,1},{9,5},{13,9},{2,14},{6,2},{... | collective-permute-start | bytes 98312 | tf_op jit(solution)/shard_map/ppermute | solution.py:540
